TPU v7x, 256 devices: a whole 4x4x8 slice. The times are simulated.
256 devices in a mesh: expert: 8 (over z), tp: 32 (over x, y, core).
Axes of the slice: x: 4, y: 4, z: 8, core: 2. Of those that a mesh axis runs over, the one named last changes fastest.
Arguments:
- tokens: bfloat16 [1024, 4096], P('expert', 'tp'), may hold values from -6 to 6
- norm_gain: bfloat16 [4096], replicated, may hold values from 0.5 to 1.5
- route_logits: float32 [1024, 2], P('expert'), may hold values from -6 to 6
- expert_ids: int32 [1024, 2], P('expert'), may hold values from 0 to 7, all different within a row; in each aligned block of 128 rows (0 to 127, 128 to 255, ...) at most 64 rows name the same one
- active: int32 [1024], P('expert'), may hold values 0 or 1
- gate_weight: bfloat16 [8, 14336, 4096], P('expert', 'tp'), may hold values from -0.09375 to 0.09375
- up_weight: bfloat16 [8, 14336, 4096], P('expert', 'tp'), may hold values from -0.09375 to 0.09375
- down_weight: bfloat16 [8, 14336, 4096], P('expert', 'tp'), may hold values from -0.046875 to 0.046875
Outputs:
- mixed: bfloat16 [1024, 4096], P('expert', 'tp')
Inputs may be any that keep to these rules, and one draw needn't show every extreme that they name: `expert_ids`: each token names 2 different experts. In each block of 128 consecutive token slots (the slots of one index of expert) no expert is named by more than 64 tokens, a bound that some block reaches. `active`: each entry is 0 or 1.
All inputs are finite; a program needn't handle non-finite values.
Results may differ from a plain program's by a relative error of at most 0.0025.
Values may be sent and summed in bfloat16 or wider, within the bound.
No kernel may reach another device: no remote copies, remote signals or barrier semaphores. Data moves between devices by JAX's collectives and lax.ppermute only.
A program may use at most 64 MiB of HBM per device.

v0:
```python
import functools

import jax
import jax.numpy as jnp
from jax import lax
from jax.experimental import pallas as pl
from jax.experimental.pallas import tpu as pltpu
from jax.sharding import Mesh
from jax.sharding import PartitionSpec as P


TP = ("tp_0", "tp_1", "tp_2")
epsilon = 1e-05
F32, BF16 = jnp.float32, jnp.bfloat16
MIB = 1024 * 1024
CHUNKS = 2
LOAD_MIB = 41


def moved(array, target):
    nx, ny, cores = (lax.axis_size(a) for a in TP)
    flat = lambda x, y, core: ((x % nx) * ny + y % ny) * cores + core
    pairs = [
        (flat(x, y, core), flat(*target(x, y, core)))
        for x in range(nx)
        for y in range(ny)
        for core in range(cores)
    ]
    return lax.ppermute(array, TP, pairs)


def along(array, stage, step):
    def target(x, y, core):
        return (x + step, y, core) if core == stage else (x, y + step, core)

    return moved(array, target)


def swapped(array):
    return moved(array, lambda x, y, core: (x, y, 1 - core))


def column(row):
    count = row.shape[1]
    eye = lax.broadcasted_iota(jnp.int32, (count, count), 0) == lax.broadcasted_iota(jnp.int32, (count, count), 1)
    return jnp.sum(jnp.where(eye, row, jnp.zeros_like(row)), axis=1, keepdims=True)


def seats(ids_ref, active_ref, seat_limit, experts):
    count = ids_ref.shape[1]
    live = column(active_ref[...])
    first, second = column(ids_ref[0:1, :]), column(ids_ref[1:2, :])
    number = lax.broadcasted_iota(jnp.int32, (count, 128), 1)
    named = ((first == number) | (second == number)) & (live > 0)
    earlier = lax.broadcasted_iota(jnp.int32, (count, count), 1) < lax.broadcasted_iota(jnp.int32, (count, count), 0)
    place = jnp.dot(earlier.astype(BF16), named.astype(BF16), preferred_element_type=F32).astype(jnp.int32)
    place = jnp.where(named, place, -1)
    spot = lax.broadcasted_iota(jnp.int32, (count, seat_limit), 1)
    return live, first, second, [place[:, e : e + 1] == spot for e in range(experts)]


def dispatch_kernel(seat_limit, experts, ids_ref, active_ref, tokens_ref, out_ref):
    _, _, _, columns = seats(ids_ref, active_ref, seat_limit, experts)
    rows = tokens_ref[...]
    for e, hot in enumerate(columns):
        picked = lax.dot_general(
            hot.astype(BF16), rows, (((0,), (0,)), ((), ())), preferred_element_type=F32
        )
        out_ref[e] = picked.astype(BF16)


def combine_kernel(seat_limit, experts, ids_ref, active_ref, logits_ref, arrived_ref, out_ref):
    live, first, second, columns = seats(ids_ref, active_ref, seat_limit, experts)
    logits = logits_ref[...]
    raised = jnp.exp(logits - jnp.max(logits, axis=0, keepdims=True))
    probs = raised / jnp.sum(raised, axis=0, keepdims=True)
    total = jnp.zeros(out_ref.shape, F32)
    for k, ids in enumerate((first, second)):
        picked = jnp.zeros(out_ref.shape, F32)
        for e, hot in enumerate(columns):
            mine = (hot & (ids == e)).astype(BF16)
            picked = picked + jnp.dot(mine, arrived_ref[e], preferred_element_type=F32)
        total = total + column(probs[k : k + 1, :]) * live.astype(F32) * picked
    out_ref[...] = total.astype(BF16)


def expert_kernel(n, where_ref, *refs):
    own, partner = refs[:n], refs[n : 2 * n]
    gain_ref, gate_ref, up_ref, down_ref, keep_ref, send_ref, normed_ref = refs[2 * n :]
    x, y, core = where_ref[0], where_ref[1], where_ref[2]
    rows = normed_ref.shape[0]
    width = own[0].shape[-1]
    squares = jnp.zeros((rows, width), F32)
    for pieces in (own, partner):
        for k2 in range(n):
            for k1 in range(n):
                value = pieces[k2][k1].astype(F32)
                squares = squares + value * value
    mean_square = jnp.sum(squares, axis=1, keepdims=True) / (2 * n * n * width)
    scale = lax.rsqrt(mean_square + epsilon)
    for pieces, parity in ((own, core), (partner, 1 - core)):
        for k2 in range(n):
            for k1 in range(n):
                at_x = lax.rem(x - jnp.where(parity == 0, k1, k2) + n, n)
                at_y = lax.rem(y - jnp.where(parity == 0, k2, k1) + n, n)
                t = (at_x * n + at_y) * 2 + parity
                value = pieces[k2][k1].astype(F32) * scale * gain_ref[:, pl.ds(pl.multiple_of(t * width, width), width)].astype(F32)
                normed_ref[:, pl.ds(pl.multiple_of(t * width, width), width)] = value.astype(BF16)
    normed = normed_ref[...]
    dims = (((1,), (1,)), ((), ()))
    gate = lax.dot_general(normed, gate_ref[...], dims, preferred_element_type=F32)
    up = lax.dot_general(normed, up_ref[...], dims, preferred_element_type=F32)
    hidden = (gate / (1.0 + jnp.exp(-gate)) * up).astype(BF16)
    for dx in range(n):
        for dy in range(n):
            q = lax.rem(x + dx, n) * n + lax.rem(y + dy, n)
            part = down_ref[:, pl.ds(pl.multiple_of(q * 2 * width, 2 * width), 2 * width)]
            both = jnp.dot(hidden, part, preferred_element_type=F32)
            low, high = both[:, :width], both[:, width:]
            one, two = jnp.where(core == 0, dx, dy), jnp.where(core == 0, dy, dx)
            keep_ref[one, two] = jnp.where(core == 0, low, high)
            send_ref[two, one] = jnp.where(core == 0, high, low)


def load_kernel(skipped, *refs):
    refs = refs[skipped:]
    sources, targets, sems = refs[:3], refs[3:6], refs[6]
    copies = [pltpu.make_async_copy(a, b, sems.at[i]) for i, (a, b) in enumerate(zip(sources, targets))]
    for copy in copies:
        copy.start()
    for copy in copies:
        copy.wait()


def loaded(after, weights):
    hbm = pl.BlockSpec(memory_space=pltpu.HBM)
    return pl.pallas_call(
        functools.partial(load_kernel, len(after)),
        out_shape=[jax.ShapeDtypeStruct(w.shape, w.dtype) for w in weights],
        in_specs=[hbm] * (len(after) + len(weights)),
        out_specs=[pl.BlockSpec(memory_space=pltpu.VMEM)] * len(weights),
        scratch_shapes=[pltpu.SemaphoreType.DMA((len(weights),))],
        compiler_params=pltpu.CompilerParams(vmem_limit_bytes=LOAD_MIB * MIB),
        cost_estimate=pl.CostEstimate(flops=1500000000, transcendentals=0, bytes_accessed=0),
    )(*after, *weights)


def stack_kernel(*refs):
    half = len(refs) - CHUNKS
    for chunk, out_ref in enumerate(refs[half:]):
        for k, ref in enumerate(refs[:half]):
            out_ref[k] = ref[chunk]


def stacked(pieces):
    out = jax.ShapeDtypeStruct((len(pieces),) + pieces[0].shape[1:], BF16)
    return pl.pallas_call(
        stack_kernel,
        out_shape=[out] * CHUNKS,
        compiler_params=pltpu.CompilerParams(vmem_limit_bytes=4 * MIB),
    )(*pieces)


def experts_of(where, own, partner, gains, gate, up, down):
    n = len(own)
    _, rows, width = own[0].shape
    model = gate.shape[1]
    vmem = pl.BlockSpec(memory_space=pltpu.VMEM)
    out = jax.ShapeDtypeStruct((n, n, rows, width), F32)
    return pl.pallas_call(
        functools.partial(expert_kernel, n),
        out_shape=(out, out),
        in_specs=[pl.BlockSpec(memory_space=pltpu.SMEM)] + [vmem] * (2 * n + 4),
        out_specs=(vmem, vmem),
        scratch_shapes=[pltpu.VMEM((rows, model), BF16)],
        compiler_params=pltpu.CompilerParams(vmem_limit_bytes=10 * MIB),
        cost_estimate=pl.CostEstimate(flops=3000000000, transcendentals=0, bytes_accessed=0),
    )(where, *own, *partner, gains, gate, up, down)


STEPS = 8
TOP = 32000.0
SPARE = 16


def scaled(blocks, refs):
    largest = functools.reduce(jnp.maximum, [jnp.abs(b) for group in blocks for b in group])
    largest = jnp.maximum(jnp.max(largest, axis=1, keepdims=True), 1e-32)
    code = jnp.ceil(STEPS * jnp.log2(largest)) + 1.0
    factor = TOP * jnp.exp2(code * (-1.0 / STEPS))
    rows, width = blocks[0][0].shape
    eye = lax.broadcasted_iota(jnp.int32, (width, width), 0) == lax.broadcasted_iota(jnp.int32, (width, width), 1)
    line = lax.broadcasted_iota(jnp.int32, (SPARE, width), 0)
    tile = jnp.zeros((SPARE, width), F32)
    for g in range(rows // width):
        part = jnp.sum(jnp.where(eye, code[g * width : (g + 1) * width], 0.0), axis=0, keepdims=True)
        tile = jnp.where(line == g, part, tile)
    for group, ref in zip(blocks, refs):
        for i, b in enumerate(group):
            ref[pl.ds(i * rows, rows), :] = jnp.round(b * factor).astype(jnp.int32).astype(jnp.int16)
        ref[pl.ds(len(group) * rows, SPARE), :] = tile.astype(jnp.int32).astype(jnp.int16)


def factors(ref, count, rows):
    tile = ref[pl.ds(count * rows, SPARE), :].astype(jnp.int32).astype(F32)
    width = tile.shape[1]
    code = jnp.concatenate([column(tile[g : g + 1, :]) for g in range(rows // width)], axis=0)
    return jnp.exp2(code * (1.0 / STEPS)) * (1.0 / TOP)


def widened(ref, i, rows):
    return ref[pl.ds(i * rows, rows), :].astype(jnp.int32).astype(F32)


def first_kernel(keep_ref, got_ref, own_ref, *out_refs):
    n = keep_ref.shape[0]
    for k2 in range(n):
        own_ref[k2] = keep_ref[0, k2] + got_ref[0, k2]
    blocks = [[keep_ref[k1, k2] + got_ref[k1, k2] for k2 in range(n)] for k1 in range(1, n)]
    scaled(blocks, out_refs)


def second_kernel(chunks, *refs):
    ins, sum_ref, out_refs = refs[: 4 * chunks], refs[4 * chunks], refs[4 * chunks + 1 :]
    n, rows, _ = ins[0].shape
    totals = []
    for chunk in range(chunks):
        own_ref, *got_refs = ins[4 * chunk : 4 * chunk + 4]
        by = [factors(got, n, rows) for got in got_refs]
        totals.append([])
        for k2 in range(n):
            total = own_ref[k2]
            for got, factor in zip(got_refs, by):
                total = total + widened(got, k2, rows) * factor
            totals[-1].append(total)
    totals = [jnp.concatenate(parts, axis=0) for parts in zip(*totals)]
    sum_ref[...] = totals[0]
    scaled([[total] for total in totals[1:]], out_refs)


def third_kernel(own_ref, *refs):
    got_refs, out_ref = refs[:-1], refs[-1]
    rows, _ = own_ref.shape
    total = own_ref[...]
    for got in got_refs:
        total = total + widened(got, 0, rows) * factors(got, 1, rows)
    out_ref[...] = total.astype(BF16)


def coded(blocks, rows, width):
    return jax.ShapeDtypeStruct((blocks * rows + SPARE, width), jnp.int16)


def started(keep, send):
    n, _, rows, width = keep.shape
    own, *parts = pl.pallas_call(
        first_kernel,
        out_shape=[jax.ShapeDtypeStruct((n, rows, width), F32)] + [coded(n, rows, width)] * (n - 1),
        compiler_params=pltpu.CompilerParams(vmem_limit_bytes=8 * MIB),
    )(keep, swapped(send))
    return [own] + [along(part, 0, k + 1) for k, part in enumerate(parts)]


def finished(chunks):
    n, rows, width = chunks[0][0].shape
    rows = rows * len(chunks)
    own, *parts = pl.pallas_call(
        functools.partial(second_kernel, len(chunks)),
        out_shape=[jax.ShapeDtypeStruct((rows, width), F32)] + [coded(1, rows, width)] * (n - 1),
        compiler_params=pltpu.CompilerParams(vmem_limit_bytes=4 * MIB),
    )(*[a for chunk in chunks for a in chunk])
    parts = [along(part, 1, k + 1) for k, part in enumerate(parts)]
    return pl.pallas_call(
        third_kernel,
        out_shape=jax.ShapeDtypeStruct((rows, width), BF16),
        compiler_params=pltpu.CompilerParams(vmem_limit_bytes=2 * MIB),
    )(own, *parts)


def local(tokens, norm_gain, route_logits, expert_ids, active, gate_weight, up_weight, down_weight):
    groups = lax.axis_size("expert")
    count, width = tokens.shape
    seat_limit = count // 2
    model = norm_gain.shape[0]
    where = jnp.stack([lax.axis_index(a) for a in TP]).astype(jnp.int32)
    gains = norm_gain.reshape(1, model)
    active_row, ids = active.reshape(1, count), expert_ids.T
    sent = pl.pallas_call(
        functools.partial(dispatch_kernel, seat_limit, groups),
        out_shape=jax.ShapeDtypeStruct((groups, seat_limit, width), BF16),
        compiler_params=pltpu.CompilerParams(vmem_limit_bytes=60 * MIB),
    )(ids, active_row, tokens)
    arriving = lax.all_to_all(sent, "expert", split_axis=0, concat_axis=0, tiled=True)
    n = lax.axis_size(TP[0])
    rows = arriving.reshape(CHUNKS, -1, width)
    first = [rows] + [along(rows, 0, k) for k in range(1, n)]
    weights = loaded((rows, gains, where), (gate_weight[0], up_weight[0], down_weight[0]))
    owns = []
    for stack in stacked(first):
        owns.append([stack] + [along(stack, 1, k) for k in range(1, n)])
    chunks = []
    for own in owns:
        partner = [swapped(a) for a in own]
        keep, send = experts_of(where, own, partner, gains, *weights)
        chunks.append(started(keep, send))
    returning = finished(chunks).reshape(groups, seat_limit, width)
    arrived = lax.all_to_all(returning, "expert", split_axis=0, concat_axis=0, tiled=True)
    return pl.pallas_call(
        functools.partial(combine_kernel, seat_limit, groups),
        out_shape=jax.ShapeDtypeStruct((count, width), BF16),
        compiler_params=pltpu.CompilerParams(vmem_limit_bytes=2 * MIB),
    )(ids, active_row, route_logits.T, arrived)


def solution(mesh):
    split = Mesh(
        mesh.devices.reshape(mesh.shape["expert"], 4, 4, 2), ("expert", "tp_0", "tp_1", "tp_2")
    )
    in_specs = (
        P("expert", TP),
        P(),
        P("expert", None),
        P("expert", None),
        P("expert"),
        P("expert", TP, None),
        P("expert", TP, None),
        P("expert", TP, None),
    )
    out_specs = P("expert", TP)
    return jax.shard_map(local, mesh=split, in_specs=in_specs, out_specs=out_specs, check_vma=False)
```

profile of v0, /device:TPU:2, one launch (start us, length us, event | category | flops | bytes accessed | tf_op | source)
XLA Modules:
  0.0 102.0 jit_solution(4787098656519747698)
XLA Ops:
  0.0 2.2 %shard_map.82 = bf16[8,64,128]{2,1,0:T(8,128)(2,1)} custom-call(s32[2,128]{1,0:T(2,128)} %bitcast.17, s32[1,128]{1,0:T(1,128)} %bitcast.19, bf16[128,128]{1,0:T(8,128)(2,1)} %tokens_ref.1), custom_call_target="tpu_custom_call" | custom-call | tf_op jit(solution)/shard_map/pallas_call | solution.py:288
  2.2 17.6 %all_to_all.10 = bf16[8,64,128]{2,1,0:T(8,128)(2,1)S(1)} all-to-all(bf16[8,64,128]{2,1,0:T(8,128)(2,1)} %shard_map.82), channel_id=1, replica_groups=mesh['expert'=8,'tp_0'=4,'tp_1'=4,'tp_2'=2] {'expert'}, dimensions={0} | all-to-all | bytes 262144 | tf_op jit(solution)/shard_map/all_to_all | solution.py:293
  19.8 1.5 %collective-permute-start = (bf16[2,256,128]{2,1,0:T(8,128)(2,1)S(1)}, bf16[2,256,128]{2,1,0:T(8,128)(2,1)S(1)}, u32[]{:S(2)}, u32[]{:S(2)}) collective-permute-start(bf16[2,256,128]{2,1,0:T(8,128)(2,1)S(1)} %bitcast.11), channel_id=1, source_target_pairs={{0,8},{1,3},{2,10},{3,5},{4,12},{5,7},{6,14},{7,1},{8,16},{9,11},{... | collective-permute-start | bytes 393224 | tf_op jit(solution)/shard_map/ppermute | solution.py:29
  21.3 1.1 %collective-permute-start.1 = (bf16[2,256,128]{2,1,0:T(8,128)(2,1)S(1)}, bf16[2,256,128]{2,1,0:T(8,128)(2,1)S(1)}, u32[]{:S(2)}, u32[]{:S(2)}) collective-permute-start(bf16[2,256,128]{2,1,0:T(8,128)(2,1)S(1)} %bitcast.12), channel_id=1, source_target_pairs={{0,16},{1,5},{2,18},{3,7},{4,20},{5,1},{6,22},{7,3},{8,24},{9,13},... | collective-permute-start | bytes 393224 | tf_op jit(solution)/shard_map/ppermute | solution.py:29
  22.4 2.2 %collective-permute-start.2 = (bf16[2,256,128]{2,1,0:T(8,128)(2,1)S(1)}, bf16[2,256,128]{2,1,0:T(8,128)(2,1)S(1)}, u32[]{:S(2)}, u32[]{:S(2)}) collective-permute-start(bf16[2,256,128]{2,1,0:T(8,128)(2,1)S(1)} %bitcast.13), channel_id=1, source_target_pairs={{0,24},{1,7},{2,26},{3,1},{4,28},{5,3},{6,30},{7,5},{8,0},{9,15},{... | collective-permute-start | bytes 393224 | tf_op jit(solution)/shard_map/ppermute | solution.py:29
  24.7 3.1 %collective-permute-done.1.refs_2_ = bf16[2,256,128]{2,1,0:T(8,128)(2,1)S(1)} collective-permute-done((bf16[2,256,128]{2,1,0:T(8,128)(2,1)S(1)}, bf16[2,256,128]{2,1,0:T(8,128)(2,1)S(1)}, u32[]{:S(2)}, u32[]{:S(2)}) %collective-permute-start.1) | collective-permute-done | bytes 131104 | tf_op jit(solution)/shard_map/ppermute | solution.py:29
  27.8 0.9 collective-permute-done.2.refs_3_
  28.8 1.7 %collective-permute-start.14 = (bf16[4,256,128]{2,1,0:T(8,128)(2,1)S(1)}, bf16[4,256,128]{2,1,0:T(8,128)(2,1)S(1)}, u32[]{:S(2)}, u32[]{:S(2)}) collective-permute-start(bf16[4,256,128]{2,1,0:T(8,128)(2,1)S(1)} %get-tuple-element.36.refs_0_), channel_id=1, source_target_pairs={{0,2},{1,9},{2,4},{3,11},{4,6},{5,13},{6,0},{7,15},{8,10},{9,17},{... | collective-permute-start | bytes 786440 | tf_op jit(solution)/shard_map/ppermute | solution.py:29
  30.4 2.9 %collective-permute-start.15 = (bf16[4,256,128]{2,1,0:T(8,128)(2,1)S(1)}, bf16[4,256,128]{2,1,0:T(8,128)(2,1)S(1)}, u32[]{:S(2)}, u32[]{:S(2)}) collective-permute-start(bf16[4,256,128]{2,1,0:T(8,128)(2,1)S(1)} %get-tuple-element.36.refs_0_), channel_id=1, source_target_pairs={{0,4},{1,17},{2,6},{3,19},{4,0},{5,21},{6,2},{7,23},{8,12},{9,25},... | collective-permute-start | bytes 786440 | tf_op jit(solution)/shard_map/ppermute | solution.py:29
  33.3 1.3 %collective-permute-start.16 = (bf16[4,256,128]{2,1,0:T(8,128)(2,1)S(1)}, bf16[4,256,128]{2,1,0:T(8,128)(2,1)S(1)}, u32[]{:S(2)}, u32[]{:S(2)}) collective-permute-start(bf16[4,256,128]{2,1,0:T(8,128)(2,1)S(1)} %get-tuple-element.36.refs_0_), channel_id=1, source_target_pairs={{0,6},{1,25},{2,0},{3,27},{4,2},{5,29},{6,4},{7,31},{8,14},{9,1},{... | collective-permute-start | bytes 786440 | tf_op jit(solution)/shard_map/ppermute | solution.py:29
  35.4 1.1 %collective-permute-done.14.refs_1_ = bf16[4,256,128]{2,1,0:T(8,128)(2,1)S(1)} collective-permute-done((bf16[4,256,128]{2,1,0:T(8,128)(2,1)S(1)}, bf16[4,256,128]{2,1,0:T(8,128)(2,1)S(1)}, u32[]{:S(2)}, u32[]{:S(2)}) %collective-permute-start.14) | collective-permute-done | bytes 262176 | tf_op jit(solution)/shard_map/ppermute | solution.py:29
  36.4 2.0 %collective-permute-start.4 = (bf16[4,256,128]{2,1,0:T(8,128)(2,1)S(1)}, bf16[4,256,128]{2,1,0:T(8,128)(2,1)S(1)}, u32[]{:S(2)}, u32[]{:S(2)}) collective-permute-start(bf16[4,256,128]{2,1,0:T(8,128)(2,1)S(1)} %get-tuple-element.26.refs_0_), channel_id=1, source_target_pairs={{0,4},{1,17},{2,6},{3,19},{4,0},{5,21},{6,2},{7,23},{8,12},{9,25},... | collective-permute-start | bytes 786440 | tf_op jit(solution)/shard_map/ppermute | solution.py:29
  38.4 2.2 %collective-permute-done.15.refs_2_ = bf16[4,256,128]{2,1,0:T(8,128)(2,1)S(1)} collective-permute-done((bf16[4,256,128]{2,1,0:T(8,128)(2,1)S(1)}, bf16[4,256,128]{2,1,0:T(8,128)(2,1)S(1)}, u32[]{:S(2)}, u32[]{:S(2)}) %collective-permute-start.15) | collective-permute-done | bytes 262176 | tf_op jit(solution)/shard_map/ppermute | solution.py:29
  41.1 2.2 %collective-permute-done.3.refs_1_ = bf16[4,256,128]{2,1,0:T(8,128)(2,1)S(1)} collective-permute-done((bf16[4,256,128]{2,1,0:T(8,128)(2,1)S(1)}, bf16[4,256,128]{2,1,0:T(8,128)(2,1)S(1)}, u32[]{:S(2)}, u32[]{:S(2)}) %collective-permute-start.3) | collective-permute-done | bytes 262176 | tf_op jit(solution)/shard_map/ppermute | solution.py:29
  43.3 0.7 reshape.14.refs_1_.refs_8_
  44.1 4.2 %shard_map.84 = (bf16[448,4096]{1,0:T(8,128)(2,1)S(1)}, bf16[448,4096]{1,0:T(8,128)(2,1)S(1)}, bf16[448,4096]{1,0:T(8,128)(2,1)S(1)}) custom-call(bf16[2,256,128]{2,1,0:T(8,128)(2,1)S(1)} %bitcast.15, bf16[1,4096]{1,0:T(2,128)(2,1)S(1)} %reshape.14.refs_1_.refs_8_, s32[3]{0:T(128)S(1)} %pad_add_fusion.refs_2_.where_ref, bf16[448,4096]{1,0:T(8,128)(2,1)} %bitcast.22, ...), custom_call_target="tpu_custom_call" | custom-call | flops 1500000000 | tf_op jit(solution)/shard_map/pallas_call | solution.py:137
  49.7 5.2 %shard_map.87 = (f32[4,4,256,128]{3,2,1,0:T(8,128)S(1)}, f32[4,4,256,128]{3,2,1,0:T(8,128)S(1)}) custom-call(s32[3]{0:T(128)S(1)} %pad_add_fusion.refs_2_.where_ref, bf16[4,256,128]{2,1,0:T(8,128)(2,1)S(1)} %get-tuple-element.36.refs_0_, bf16[4,256,128]{2,1,0:T(8,128)(2,1)S(1)} %collective-permute-done.14.refs_1_, ...), custom_call_target="tpu_custom_call" | custom-call | flops 3000000000 | tf_op jit(solution)/shard_map/pallas_call | solution.py:170
  55.3 5.3 %shard_map.85 = (f32[4,4,256,128]{3,2,1,0:T(8,128)S(1)}, f32[4,4,256,128]{3,2,1,0:T(8,128)S(1)}) custom-call(s32[3]{0:T(128)S(1)} %pad_add_fusion.refs_2_.where_ref, bf16[4,256,128]{2,1,0:T(8,128)(2,1)S(1)} %get-tuple-element.26.refs_0_, bf16[4,256,128]{2,1,0:T(8,128)(2,1)S(1)} %collective-permute-done.3.refs_1_, ...), custom_call_target="tpu_custom_call" | custom-call | flops 3000000000 | tf_op jit(solution)/shard_map/pallas_call | solution.py:170
  61.5 1.1 %collective-permute-start.22 = (s16[1040,128]{1,0:T(8,128)(2,1)S(1)}, s16[1040,128]{1,0:T(8,128)(2,1)S(1)}, u32[]{:S(2)}, u32[]{:S(2)}) collective-permute-start(s16[1040,128]{1,0:T(8,128)(2,1)S(1)} %get-tuple-element.40), channel_id=1, source_target_pairs={{0,8},{1,3},{2,10},{3,5},{4,12},{5,7},{6,14},{7,1},{8,16},{9,11},{... | collective-permute-start | bytes 798728 | tf_op jit(solution)/shard_map/ppermute | solution.py:29
  62.6 1.8 %collective-permute-start.23 = (s16[1040,128]{1,0:T(8,128)(2,1)S(1)}, s16[1040,128]{1,0:T(8,128)(2,1)S(1)}, u32[]{:S(2)}, u32[]{:S(2)}) collective-permute-start(s16[1040,128]{1,0:T(8,128)(2,1)S(1)} %get-tuple-element.41), channel_id=1, source_target_pairs={{0,16},{1,5},{2,18},{3,7},{4,20},{5,1},{6,22},{7,3},{8,24},{9,13},... | collective-permute-start | bytes 798728 | tf_op jit(solution)/shard_map/ppermute | solution.py:29
  64.4 2.0 %collective-permute-start.24 = (s16[1040,128]{1,0:T(8,128)(2,1)S(1)}, s16[1040,128]{1,0:T(8,128)(2,1)S(1)}, u32[]{:S(2)}, u32[]{:S(2)}) collective-permute-start(s16[1040,128]{1,0:T(8,128)(2,1)S(1)} %get-tuple-element.42), channel_id=1, source_target_pairs={{0,24},{1,7},{2,26},{3,1},{4,28},{5,3},{6,30},{7,5},{8,0},{9,15},{... | collective-permute-start | bytes 798728 | tf_op jit(solution)/shard_map/ppermute | solution.py:29
  67.1 2.9 %collective-permute-start.12 = (s16[1040,128]{1,0:T(8,128)(2,1)S(1)}, s16[1040,128]{1,0:T(8,128)(2,1)S(1)}, u32[]{:S(2)}, u32[]{:S(2)}) collective-permute-start(s16[1040,128]{1,0:T(8,128)(2,1)S(1)} %get-tuple-element.34), channel_id=1, source_target_pairs={{0,16},{1,5},{2,18},{3,7},{4,20},{5,1},{6,22},{7,3},{8,24},{9,13},... | collective-permute-start | bytes 798728 | tf_op jit(solution)/shard_map/ppermute | solution.py:29
  70.6 2.8 %collective-permute-done.24.refs_7_ = s16[1040,128]{1,0:T(8,128)(2,1)S(1)} collective-permute-done((s16[1040,128]{1,0:T(8,128)(2,1)S(1)}, s16[1040,128]{1,0:T(8,128)(2,1)S(1)}, u32[]{:S(2)}, u32[]{:S(2)}) %collective-permute-start.24) | collective-permute-done | bytes 266272 | tf_op jit(solution)/shard_map/ppermute | solution.py:29
  73.7 2.6 %collective-permute-done.12.refs_2_ = s16[1040,128]{1,0:T(8,128)(2,1)S(1)} collective-permute-done((s16[1040,128]{1,0:T(8,128)(2,1)S(1)}, s16[1040,128]{1,0:T(8,128)(2,1)S(1)}, u32[]{:S(2)}, u32[]{:S(2)}) %collective-permute-start.12) | collective-permute-done | bytes 266272 | tf_op jit(solution)/shard_map/ppermute | solution.py:29
  76.3 2.8 %collective-permute-done.13.refs_3_ = s16[1040,128]{1,0:T(8,128)(2,1)S(1)} collective-permute-done((s16[1040,128]{1,0:T(8,128)(2,1)S(1)}, s16[1040,128]{1,0:T(8,128)(2,1)S(1)}, u32[]{:S(2)}, u32[]{:S(2)}) %collective-permute-start.13) | collective-permute-done | bytes 266272 | tf_op jit(solution)/shard_map/ppermute | solution.py:29
  79.1 1.0 shard_map.89
  80.1 2.0 %collective-permute-start.26 = (s16[528,128]{1,0:T(8,128)(2,1)S(1)}, s16[528,128]{1,0:T(8,128)(2,1)S(1)}, u32[]{:S(2)}, u32[]{:S(2)}) collective-permute-start(s16[528,128]{1,0:T(8,128)(2,1)S(1)} %get-tuple-element.45), channel_id=1, source_target_pairs={{0,4},{1,17},{2,6},{3,19},{4,0},{5,21},{6,2},{7,23},{8,12},{9,25},... | collective-permute-start | bytes 405512 | tf_op jit(solution)/shard_map/ppermute | solution.py:29
  82.2 1.4 %collective-permute-start.27 = (s16[528,128]{1,0:T(8,128)(2,1)S(1)}, s16[528,128]{1,0:T(8,128)(2,1)S(1)}, u32[]{:S(2)}, u32[]{:S(2)}) collective-permute-start(s16[528,128]{1,0:T(8,128)(2,1)S(1)} %get-tuple-element.46), channel_id=1, source_target_pairs={{0,6},{1,25},{2,0},{3,27},{4,2},{5,29},{6,4},{7,31},{8,14},{9,1},{... | collective-permute-start | bytes 405512 | tf_op jit(solution)/shard_map/ppermute | solution.py:29
  83.5 4.3 %collective-permute-done.25.refs_0_ = s16[528,128]{1,0:T(8,128)(2,1)S(1)} collective-permute-done((s16[528,128]{1,0:T(8,128)(2,1)S(1)}, s16[528,128]{1,0:T(8,128)(2,1)S(1)}, u32[]{:S(2)}, u32[]{:S(2)}) %collective-permute-start.25) | collective-permute-done | bytes 135200 | tf_op jit(solution)/shard_map/ppermute | solution.py:29
  87.8 0.9 collective-permute-done.27.refs_2_
  89.2 11.5 %all_to_all.11.arrived_ref = bf16[8,64,128]{2,1,0:T(8,128)(2,1)S(1)} all-to-all(bf16[8,64,128]{2,1,0:T(8,128)(2,1)S(1)} %bitcast.16), channel_id=1, replica_groups=mesh['expert'=8,'tp_0'=4,'tp_1'=4,'tp_2'=2] {'expert'}, dimensions={0} | all-to-all | bytes 262144 | tf_op jit(solution)/shard_map/all_to_all | solution.py:307
  100.7 1.3 %shard_map.91 = bf16[128,128]{1,0:T(8,128)(2,1)} custom-call(s32[2,128]{1,0:T(2,128)S(1)} %bitcast.18, s32[1,128]{1,0:T(1,128)S(1)} %bitcast.20, f32[2,128]{1,0:T(2,128)S(1)} %bitcast.21, bf16[8,64,128]{2,1,0:T(8,128)(2,1)S(1)} %all_to_all.11.arrived_ref), custom_call_target="tpu_custom_call" | custom-call | tf_op jit(solution)/shard_map/pallas_call | solution.py:308
  (44 shorter events, 6.3 us)
Async XLA Ops:
  19.8 5.0 %collective-permute-start = (bf16[2,256,128]{2,1,0:T(8,128)(2,1)S(1)}, bf16[2,256,128]{2,1,0:T(8,128)(2,1)S(1)}, u32[]{:S(2)}, u32[]{:S(2)}) collective-permute-start(bf16[2,256,128]{2,1,0:T(8,128)(2,1)S(1)} %bitcast.11), channel_id=1, source_target_pairs={{0,8},{1,3},{2,10},{3,5},{4,12},{5,7},{6,14},{7,1},{8,16},{9,11},{... | collective-permute-start | bytes 393224 | tf_op jit(solution)/shard_map/ppermute | solution.py:29
  21.3 6.6 %collective-permute-start.1 = (bf16[2,256,128]{2,1,0:T(8,128)(2,1)S(1)}, bf16[2,256,128]{2,1,0:T(8,128)(2,1)S(1)}, u32[]{:S(2)}, u32[]{:S(2)}) collective-permute-start(bf16[2,256,128]{2,1,0:T(8,128)(2,1)S(1)} %bitcast.12), channel_id=1, source_target_pairs={{0,16},{1,5},{2,18},{3,7},{4,20},{5,1},{6,22},{7,3},{8,24},{9,13},... | collective-permute-start | bytes 393224 | tf_op jit(solution)/shard_map/ppermute | solution.py:29
  22.4 6.4 %collective-permute-start.2 = (bf16[2,256,128]{2,1,0:T(8,128)(2,1)S(1)}, bf16[2,256,128]{2,1,0:T(8,128)(2,1)S(1)}, u32[]{:S(2)}, u32[]{:S(2)}) collective-permute-start(bf16[2,256,128]{2,1,0:T(8,128)(2,1)S(1)} %bitcast.13), channel_id=1, source_target_pairs={{0,24},{1,7},{2,26},{3,1},{4,28},{5,3},{6,30},{7,5},{8,0},{9,15},{... | collective-permute-start | bytes 393224 | tf_op jit(solution)/shard_map/ppermute | solution.py:29
  28.8 7.7 %collective-permute-start.14 = (bf16[4,256,128]{2,1,0:T(8,128)(2,1)S(1)}, bf16[4,256,128]{2,1,0:T(8,128)(2,1)S(1)}, u32[]{:S(2)}, u32[]{:S(2)}) collective-permute-start(bf16[4,256,128]{2,1,0:T(8,128)(2,1)S(1)} %get-tuple-element.36.refs_0_), channel_id=1, source_target_pairs={{0,2},{1,9},{2,4},{3,11},{4,6},{5,13},{6,0},{7,15},{8,10},{9,17},{... | collective-permute-start | bytes 786440 | tf_op jit(solution)/shard_map/ppermute | solution.py:29
  30.4 10.2 %collective-permute-start.15 = (bf16[4,256,128]{2,1,0:T(8,128)(2,1)S(1)}, bf16[4,256,128]{2,1,0:T(8,128)(2,1)S(1)}, u32[]{:S(2)}, u32[]{:S(2)}) collective-permute-start(bf16[4,256,128]{2,1,0:T(8,128)(2,1)S(1)} %get-tuple-element.36.refs_0_), channel_id=1, source_target_pairs={{0,4},{1,17},{2,6},{3,19},{4,0},{5,21},{6,2},{7,23},{8,12},{9,25},... | collective-permute-start | bytes 786440 | tf_op jit(solution)/shard_map/ppermute | solution.py:29
  33.3 7.3 %collective-permute-start.16 = (bf16[4,256,128]{2,1,0:T(8,128)(2,1)S(1)}, bf16[4,256,128]{2,1,0:T(8,128)(2,1)S(1)}, u32[]{:S(2)}, u32[]{:S(2)}) collective-permute-start(bf16[4,256,128]{2,1,0:T(8,128)(2,1)S(1)} %get-tuple-element.36.refs_0_), channel_id=1, source_target_pairs={{0,6},{1,25},{2,0},{3,27},{4,2},{5,29},{6,4},{7,31},{8,14},{9,1},{... | collective-permute-start | bytes 786440 | tf_op jit(solution)/shard_map/ppermute | solution.py:29
  34.7 5.9 %collective-permute-start.17 = (bf16[4,256,128]{2,1,0:T(8,128)(2,1)S(1)}, bf16[4,256,128]{2,1,0:T(8,128)(2,1)S(1)}, u32[]{:S(2)}, u32[]{:S(2)}) collective-permute-start(bf16[4,256,128]{2,1,0:T(8,128)(2,1)S(1)} %get-tuple-element.36.refs_0_), channel_id=1, source_target_pairs={{0,1},{1,0},{2,3},{3,2},{4,5},{5,4},{6,7},{7,6},{8,9},{9,8},{10,11... | collective-permute-start | bytes 786440 | tf_op jit(solution)/shard_map/ppermute | solution.py:29
  34.7 8.6 %collective-permute-start.3 = (bf16[4,256,128]{2,1,0:T(8,128)(2,1)S(1)}, bf16[4,256,128]{2,1,0:T(8,128)(2,1)S(1)}, u32[]{:S(2)}, u32[]{:S(2)}) collective-permute-start(bf16[4,256,128]{2,1,0:T(8,128)(2,1)S(1)} %get-tuple-element.26.refs_0_), channel_id=1, source_target_pairs={{0,2},{1,9},{2,4},{3,11},{4,6},{5,13},{6,0},{7,15},{8,10},{9,17},{... | collective-permute-start | bytes 786440 | tf_op jit(solution)/shard_map/ppermute | solution.py:29
  36.4 11.9 %collective-permute-start.4 = (bf16[4,256,128]{2,1,0:T(8,128)(2,1)S(1)}, bf16[4,256,128]{2,1,0:T(8,128)(2,1)S(1)}, u32[]{:S(2)}, u32[]{:S(2)}) collective-permute-start(bf16[4,256,128]{2,1,0:T(8,128)(2,1)S(1)} %get-tuple-element.26.refs_0_), channel_id=1, source_target_pairs={{0,4},{1,17},{2,6},{3,19},{4,0},{5,21},{6,2},{7,23},{8,12},{9,25},... | collective-permute-start | bytes 786440 | tf_op jit(solution)/shard_map/ppermute | solution.py:29
  40.6 8.3 %collective-permute-start.5 = (bf16[4,256,128]{2,1,0:T(8,128)(2,1)S(1)}, bf16[4,256,128]{2,1,0:T(8,128)(2,1)S(1)}, u32[]{:S(2)}, u32[]{:S(2)}) collective-permute-start(bf16[4,256,128]{2,1,0:T(8,128)(2,1)S(1)} %get-tuple-element.26.refs_0_), channel_id=1, source_target_pairs={{0,6},{1,25},{2,0},{3,27},{4,2},{5,29},{6,4},{7,31},{8,14},{9,1},{... | collective-permute-start | bytes 786440 | tf_op jit(solution)/shard_map/ppermute | solution.py:29
  40.6 8.5 %collective-permute-start.18 = (bf16[4,256,128]{2,1,0:T(8,128)(2,1)S(1)}, bf16[4,256,128]{2,1,0:T(8,128)(2,1)S(1)}, u32[]{:S(2)}, u32[]{:S(2)}) collective-permute-start(bf16[4,256,128]{2,1,0:T(8,128)(2,1)S(1)} %collective-permute-done.14.refs_1_), channel_id=1, source_target_pairs={{0,1},{1,0},{2,3},{3,2},{4,5},{5,4},{6,7},{7,6},{8,9},{9,8},{10,11... | collective-permute-start | bytes 786440 | tf_op jit(solution)/shard_map/ppermute | solution.py:29
  40.6 8.8 %collective-permute-start.19 = (bf16[4,256,128]{2,1,0:T(8,128)(2,1)S(1)}, bf16[4,256,128]{2,1,0:T(8,128)(2,1)S(1)}, u32[]{:S(2)}, u32[]{:S(2)}) collective-permute-start(bf16[4,256,128]{2,1,0:T(8,128)(2,1)S(1)} %collective-permute-done.15.refs_2_), channel_id=1, source_target_pairs={{0,1},{1,0},{2,3},{3,2},{4,5},{5,4},{6,7},{7,6},{8,9},{9,8},{10,11... | collective-permute-start | bytes 786440 | tf_op jit(solution)/shard_map/ppermute | solution.py:29
  43.3 6.4 %collective-permute-start.20 = (bf16[4,256,128]{2,1,0:T(8,128)(2,1)S(1)}, bf16[4,256,128]{2,1,0:T(8,128)(2,1)S(1)}, u32[]{:S(2)}, u32[]{:S(2)}) collective-permute-start(bf16[4,256,128]{2,1,0:T(8,128)(2,1)S(1)} %collective-permute-done.16.refs_3_), channel_id=1, source_target_pairs={{0,1},{1,0},{2,3},{3,2},{4,5},{5,4},{6,7},{7,6},{8,9},{9,8},{10,11... | collective-permute-start | bytes 786440 | tf_op jit(solution)/shard_map/ppermute | solution.py:29
  48.3 6.9 %collective-permute-start.6 = (bf16[4,256,128]{2,1,0:T(8,128)(2,1)S(1)}, bf16[4,256,128]{2,1,0:T(8,128)(2,1)S(1)}, u32[]{:S(2)}, u32[]{:S(2)}) collective-permute-start(bf16[4,256,128]{2,1,0:T(8,128)(2,1)S(1)} %get-tuple-element.26.refs_0_), channel_id=1, source_target_pairs={{0,1},{1,0},{2,3},{3,2},{4,5},{5,4},{6,7},{7,6},{8,9},{9,8},{10,11... | collective-permute-start | bytes 786440 | tf_op jit(solution)/shard_map/ppermute | solution.py:29
  48.9 6.4 %collective-permute-start.7 = (bf16[4,256,128]{2,1,0:T(8,128)(2,1)S(1)}, bf16[4,256,128]{2,1,0:T(8,128)(2,1)S(1)}, u32[]{:S(2)}, u32[]{:S(2)}) collective-permute-start(bf16[4,256,128]{2,1,0:T(8,128)(2,1)S(1)} %collective-permute-done.3.refs_1_), channel_id=1, source_target_pairs={{0,1},{1,0},{2,3},{3,2},{4,5},{5,4},{6,7},{7,6},{8,9},{9,8},{10,11... | collective-permute-start | bytes 786440 | tf_op jit(solution)/shard_map/ppermute | solution.py:29
  49.0 6.2 %collective-permute-start.8 = (bf16[4,256,128]{2,1,0:T(8,128)(2,1)S(1)}, bf16[4,256,128]{2,1,0:T(8,128)(2,1)S(1)}, u32[]{:S(2)}, u32[]{:S(2)}) collective-permute-start(bf16[4,256,128]{2,1,0:T(8,128)(2,1)S(1)} %collective-permute-done.4.refs_2_), channel_id=1, source_target_pairs={{0,1},{1,0},{2,3},{3,2},{4,5},{5,4},{6,7},{7,6},{8,9},{9,8},{10,11... | collective-permute-start | bytes 786440 | tf_op jit(solution)/shard_map/ppermute | solution.py:29
  49.5 5.8 %collective-permute-start.9 = (bf16[4,256,128]{2,1,0:T(8,128)(2,1)S(1)}, bf16[4,256,128]{2,1,0:T(8,128)(2,1)S(1)}, u32[]{:S(2)}, u32[]{:S(2)}) collective-permute-start(bf16[4,256,128]{2,1,0:T(8,128)(2,1)S(1)} %collective-permute-done.5.refs_3_), channel_id=1, source_target_pairs={{0,1},{1,0},{2,3},{3,2},{4,5},{5,4},{6,7},{7,6},{8,9},{9,8},{10,11... | collective-permute-start | bytes 786440 | tf_op jit(solution)/shard_map/ppermute | solution.py:29
  55.0 6.0 %collective-permute-start.21 = (f32[4,4,256,128]{3,2,1,0:T(8,128)S(1)}, f32[4,4,256,128]{3,2,1,0:T(8,128)S(1)}, u32[]{:S(2)}, u32[]{:S(2)}) collective-permute-start(f32[4,4,256,128]{3,2,1,0:T(8,128)S(1)} %get-tuple-element.38), channel_id=1, source_target_pairs={{0,1},{1,0},{2,3},{3,2},{4,5},{5,4},{6,7},{7,6},{8,9},{9,8},{10,11... | collective-permute-start | bytes 6291464 | tf_op jit(solution)/shard_map/ppermute | solution.py:29
  60.6 5.8 %collective-permute-start.10 = (f32[4,4,256,128]{3,2,1,0:T(8,128)S(1)}, f32[4,4,256,128]{3,2,1,0:T(8,128)S(1)}, u32[]{:S(2)}, u32[]{:S(2)}) collective-permute-start(f32[4,4,256,128]{3,2,1,0:T(8,128)S(1)} %get-tuple-element.31), channel_id=1, source_target_pairs={{0,1},{1,0},{2,3},{3,2},{4,5},{5,4},{6,7},{7,6},{8,9},{9,8},{10,11... | collective-permute-start | bytes 6291464 | tf_op jit(solution)/shard_map/ppermute | solution.py:29
  61.5 8.5 %collective-permute-start.22 = (s16[1040,128]{1,0:T(8,128)(2,1)S(1)}, s16[1040,128]{1,0:T(8,128)(2,1)S(1)}, u32[]{:S(2)}, u32[]{:S(2)}) collective-permute-start(s16[1040,128]{1,0:T(8,128)(2,1)S(1)} %get-tuple-element.40), channel_id=1, source_target_pairs={{0,8},{1,3},{2,10},{3,5},{4,12},{5,7},{6,14},{7,1},{8,16},{9,11},{... | collective-permute-start | bytes 798728 | tf_op jit(solution)/shard_map/ppermute | solution.py:29
  62.6 8.0 %collective-permute-start.23 = (s16[1040,128]{1,0:T(8,128)(2,1)S(1)}, s16[1040,128]{1,0:T(8,128)(2,1)S(1)}, u32[]{:S(2)}, u32[]{:S(2)}) collective-permute-start(s16[1040,128]{1,0:T(8,128)(2,1)S(1)} %get-tuple-element.41), channel_id=1, source_target_pairs={{0,16},{1,5},{2,18},{3,7},{4,20},{5,1},{6,22},{7,3},{8,24},{9,13},... | collective-permute-start | bytes 798728 | tf_op jit(solution)/shard_map/ppermute | solution.py:29
  64.4 9.0 %collective-permute-start.24 = (s16[1040,128]{1,0:T(8,128)(2,1)S(1)}, s16[1040,128]{1,0:T(8,128)(2,1)S(1)}, u32[]{:S(2)}, u32[]{:S(2)}) collective-permute-start(s16[1040,128]{1,0:T(8,128)(2,1)S(1)} %get-tuple-element.42), channel_id=1, source_target_pairs={{0,24},{1,7},{2,26},{3,1},{4,28},{5,3},{6,30},{7,5},{8,0},{9,15},{... | collective-permute-start | bytes 798728 | tf_op jit(solution)/shard_map/ppermute | solution.py:29
  66.4 34.3 %copy-start = (s32[128,2]{0,1:T(2,128)S(1)}, s32[128,2]{0,1:T(2,128)}, u32[]{:S(2)}) copy-start(s32[128,2]{0,1:T(2,128)} %param.11) | copy-start | bytes 3076
  66.4 34.3 %copy-start.1 = (s32[128]{0:T(128)S(1)}, s32[128]{0:T(128)}, u32[]{:S(2)}) copy-start(s32[128]{0:T(128)} %param.12) | copy-start | bytes 1540
  66.4 34.3 %copy-start.2 = (f32[128,2]{0,1:T(2,128)S(1)}, f32[128,2]{0,1:T(2,128)}, u32[]{:S(2)}) copy-start(f32[128,2]{0,1:T(2,128)} %param.10) | copy-start | bytes 3076
  67.0 6.7 %collective-permute-start.11 = (s16[1040,128]{1,0:T(8,128)(2,1)S(1)}, s16[1040,128]{1,0:T(8,128)(2,1)S(1)}, u32[]{:S(2)}, u32[]{:S(2)}) collective-permute-start(s16[1040,128]{1,0:T(8,128)(2,1)S(1)} %get-tuple-element.33), channel_id=1, source_target_pairs={{0,8},{1,3},{2,10},{3,5},{4,12},{5,7},{6,14},{7,1},{8,16},{9,11},{... | collective-permute-start | bytes 798728 | tf_op jit(solution)/shard_map/ppermute | solution.py:29
  67.1 9.3 %collective-permute-start.12 = (s16[1040,128]{1,0:T(8,128)(2,1)S(1)}, s16[1040,128]{1,0:T(8,128)(2,1)S(1)}, u32[]{:S(2)}, u32[]{:S(2)}) collective-permute-start(s16[1040,128]{1,0:T(8,128)(2,1)S(1)} %get-tuple-element.34), channel_id=1, source_target_pairs={{0,16},{1,5},{2,18},{3,7},{4,20},{5,1},{6,22},{7,3},{8,24},{9,13},... | collective-permute-start | bytes 798728 | tf_op jit(solution)/shard_map/ppermute | solution.py:29
  70.0 9.1 %collective-permute-start.13 = (s16[1040,128]{1,0:T(8,128)(2,1)S(1)}, s16[1040,128]{1,0:T(8,128)(2,1)S(1)}, u32[]{:S(2)}, u32[]{:S(2)}) collective-permute-start(s16[1040,128]{1,0:T(8,128)(2,1)S(1)} %get-tuple-element.35), channel_id=1, source_target_pairs={{0,24},{1,7},{2,26},{3,1},{4,28},{5,3},{6,30},{7,5},{8,0},{9,15},{... | collective-permute-start | bytes 798728 | tf_op jit(solution)/shard_map/ppermute | solution.py:29
  80.1 7.7 %collective-permute-start.25 = (s16[528,128]{1,0:T(8,128)(2,1)S(1)}, s16[528,128]{1,0:T(8,128)(2,1)S(1)}, u32[]{:S(2)}, u32[]{:S(2)}) collective-permute-start(s16[528,128]{1,0:T(8,128)(2,1)S(1)} %get-tuple-element.44), channel_id=1, source_target_pairs={{0,2},{1,9},{2,4},{3,11},{4,6},{5,13},{6,0},{7,15},{8,10},{9,17},{... | collective-permute-start | bytes 405512 | tf_op jit(solution)/shard_map/ppermute | solution.py:29
  80.1 7.7 %collective-permute-start.26 = (s16[528,128]{1,0:T(8,128)(2,1)S(1)}, s16[528,128]{1,0:T(8,128)(2,1)S(1)}, u32[]{:S(2)}, u32[]{:S(2)}) collective-permute-start(s16[528,128]{1,0:T(8,128)(2,1)S(1)} %get-tuple-element.45), channel_id=1, source_target_pairs={{0,4},{1,17},{2,6},{3,19},{4,0},{5,21},{6,2},{7,23},{8,12},{9,25},... | collective-permute-start | bytes 405512 | tf_op jit(solution)/shard_map/ppermute | solution.py:29
  82.2 6.5 %collective-permute-start.27 = (s16[528,128]{1,0:T(8,128)(2,1)S(1)}, s16[528,128]{1,0:T(8,128)(2,1)S(1)}, u32[]{:S(2)}, u32[]{:S(2)}) collective-permute-start(s16[528,128]{1,0:T(8,128)(2,1)S(1)} %get-tuple-element.46), channel_id=1, source_target_pairs={{0,6},{1,25},{2,0},{3,27},{4,2},{5,29},{6,4},{7,31},{8,14},{9,1},{... | collective-permute-start | bytes 405512 | tf_op jit(solution)/shard_map/ppermute | solution.py:29
where the time goes:
time: 102 us
  blocking collectives  29 us (28%)
  starting transfers between devices  27.6 us (27%)
  waiting for transfers between devices  23.6 us (23%)
  Pallas kernels  20.8 us (20%)
    ppermute x28, starting transfers between devices, moved(): return lax.ppermute(array, TP, pairs)  27.6 us
    ppermute x28, waiting for transfers between devices, moved(): return lax.ppermute(array, TP, pairs)  23.6 us
    all_to_all x1, blocking collectives, local(): lax.all_to_all(sent, 'expert', split_axis=0, concat_axis=0, tiled=True)  17.6 us
    all_to_all x1, blocking collectives, local(): lax.all_to_all(returning, 'expert', split_axis=0, concat_axis=0, tiled=True)  11.5 us
    pallas_call x2, Pallas kernels, experts_of(): pl.pallas_call(functools.partial(expert_kernel, n), out_shape=(out, out),...  10.5 us
    pallas_call x1, Pallas kernels, loaded(): pl.pallas_call(functools.partial(load_kernel, len(after)), out_shape=[jax...  4.23 us
    pallas_call x1, Pallas kernels, local(): pl.pallas_call(functools.partial(dispatch_kernel, seat_limit, groups), ou...  2.2 us
  transfers between devices with their start and end apart: 28, of which 13 were waited for; matrix products, arithmetic and copies ran while one was open for 1% of the time, Pallas kernels for 15%

commit v1 on v0

--- a/solution.py
+++ b/solution.py
@@ -13,7 +13,7 @@
 epsilon = 1e-05
 F32, BF16 = jnp.float32, jnp.bfloat16
 MIB = 1024 * 1024
-CHUNKS = 2
+STEP_ORDER = (2, 1, 3, 0)
 LOAD_MIB = 41
 
 
@@ -84,42 +84,51 @@
     out_ref[...] = total.astype(BF16)
 
 
-def expert_kernel(n, where_ref, *refs):
+def hidden_kernel(n, where_ref, *refs):
     own, partner = refs[:n], refs[n : 2 * n]
-    gain_ref, gate_ref, up_ref, down_ref, keep_ref, send_ref, normed_ref = refs[2 * n :]
+    gain_ref, gate_ref, up_ref, hidden_ref, normed_ref = refs[2 * n :]
     x, y, core = where_ref[0], where_ref[1], where_ref[2]
-    rows = normed_ref.shape[0]
+    rows, _ = normed_ref.shape
     width = own[0].shape[-1]
-    squares = jnp.zeros((rows, width), F32)
-    for pieces in (own, partner):
-        for k2 in range(n):
-            for k1 in range(n):
-                value = pieces[k2][k1].astype(F32)
-                squares = squares + value * value
-    mean_square = jnp.sum(squares, axis=1, keepdims=True) / (2 * n * n * width)
-    scale = lax.rsqrt(mean_square + epsilon)
-    for pieces, parity in ((own, core), (partner, 1 - core)):
-        for k2 in range(n):
-            for k1 in range(n):
-                at_x = lax.rem(x - jnp.where(parity == 0, k1, k2) + n, n)
-                at_y = lax.rem(y - jnp.where(parity == 0, k2, k1) + n, n)
-                t = (at_x * n + at_y) * 2 + parity
-                value = pieces[k2][k1].astype(F32) * scale * gain_ref[:, pl.ds(pl.multiple_of(t * width, width), width)].astype(F32)
-                normed_ref[:, pl.ds(pl.multiple_of(t * width, width), width)] = value.astype(BF16)
-    normed = normed_ref[...]
     dims = (((1,), (1,)), ((), ()))
-    gate = lax.dot_general(normed, gate_ref[...], dims, preferred_element_type=F32)
-    up = lax.dot_general(normed, up_ref[...], dims, preferred_element_type=F32)
-    hidden = (gate / (1.0 + jnp.exp(-gate)) * up).astype(BF16)
-    for dx in range(n):
-        for dy in range(n):
-            q = lax.rem(x + dx, n) * n + lax.rem(y + dy, n)
-            part = down_ref[:, pl.ds(pl.multiple_of(q * 2 * width, 2 * width), 2 * width)]
-            both = jnp.dot(hidden, part, preferred_element_type=F32)
-            low, high = both[:, :width], both[:, width:]
-            one, two = jnp.where(core == 0, dx, dy), jnp.where(core == 0, dy, dx)
-            keep_ref[one, two] = jnp.where(core == 0, low, high)
-            send_ref[two, one] = jnp.where(core == 0, high, low)
+    for half in range(own[0].shape[1] // rows):
+        span = slice(half * rows, (half + 1) * rows)
+        squares = jnp.zeros((rows, width), F32)
+        for pieces in (own, partner):
+            for k2 in range(n):
+                for k1 in range(n):
+                    value = pieces[k2][k1, span].astype(F32)
+                    squares = squares + value * value
+        mean_square = jnp.sum(squares, axis=1, keepdims=True) / (2 * n * n * width)
+        scale = lax.rsqrt(mean_square + epsilon)
+        for pieces, parity in ((own, core), (partner, 1 - core)):
+            for k2 in range(n):
+                for k1 in range(n):
+                    at = place(x - jnp.where(parity == 0, k1, k2), y - jnp.where(parity == 0, k2, k1), parity, n, width)
+                    value = pieces[k2][k1, span].astype(F32) * scale * gain_ref[:, at].astype(F32)
+                    normed_ref[:, at] = value.astype(BF16)
+        normed = normed_ref[...]
+        gate = lax.dot_general(normed, gate_ref[...], dims, preferred_element_type=F32)
+        up = lax.dot_general(normed, up_ref[...], dims, preferred_element_type=F32)
+        hidden_ref[span, :] = (gate / (1.0 + jnp.exp(-gate)) * up).astype(BF16)
+
+
+def place(x, y, parity, n, width):
+    t = (lax.rem(x + n, n) * n + lax.rem(y + n, n)) * 2 + parity
+    return pl.ds(pl.multiple_of(t * width, width), width)
+
+
+def down_kernel(n, step, where_ref, hidden_ref, down_ref, keep_ref, send_ref):
+    x, y, core = where_ref[0], where_ref[1], where_ref[2]
+    width = keep_ref.shape[-1]
+    hidden = hidden_ref[...]
+    for k2 in range(n):
+        parts = [
+            down_ref[:, place(x + jnp.where(p == 0, step, k2), y + jnp.where(p == 0, k2, step), p, n, width)]
+            for p in (core, 1 - core)
+        ]
+        both = jnp.dot(hidden, jnp.concatenate(parts, axis=1), preferred_element_type=F32)
+        keep_ref[k2], send_ref[k2] = both[:, :width], both[:, width:]
 
 
 def load_kernel(skipped, *refs):
@@ -145,37 +154,52 @@
     )(*after, *weights)
 
 
+VMEM = pl.BlockSpec(memory_space=pltpu.VMEM)
+SMEM = pl.BlockSpec(memory_space=pltpu.SMEM)
+
+
+def cost(flops):
+    return pl.CostEstimate(flops=flops, transcendentals=0, bytes_accessed=0)
+
+
 def stack_kernel(*refs):
-    half = len(refs) - CHUNKS
-    for chunk, out_ref in enumerate(refs[half:]):
-        for k, ref in enumerate(refs[:half]):
-            out_ref[k] = ref[chunk]
+    for k, ref in enumerate(refs[:-1]):
+        refs[-1][k] = ref[...]
 
 
 def stacked(pieces):
-    out = jax.ShapeDtypeStruct((len(pieces),) + pieces[0].shape[1:], BF16)
     return pl.pallas_call(
         stack_kernel,
-        out_shape=[out] * CHUNKS,
+        out_shape=jax.ShapeDtypeStruct((len(pieces),) + pieces[0].shape, BF16),
         compiler_params=pltpu.CompilerParams(vmem_limit_bytes=4 * MIB),
     )(*pieces)
 
 
-def experts_of(where, own, partner, gains, gate, up, down):
+def hidden_of(where, own, partner, gains, gate, up):
     n = len(own)
-    _, rows, width = own[0].shape
-    model = gate.shape[1]
-    vmem = pl.BlockSpec(memory_space=pltpu.VMEM)
-    out = jax.ShapeDtypeStruct((n, n, rows, width), F32)
-    return pl.pallas_call(
-        functools.partial(expert_kernel, n),
+    rows = own[0].shape[1]
+    units, model = gate.shape
+    return pl.pallas_call(
+        functools.partial(hidden_kernel, n),
+        out_shape=jax.ShapeDtypeStruct((rows, units), BF16),
+        in_specs=[SMEM] + [VMEM] * (2 * n + 3),
+        out_specs=VMEM,
+        scratch_shapes=[pltpu.VMEM((rows // 2, model), BF16)],
+        compiler_params=pltpu.CompilerParams(vmem_limit_bytes=10 * MIB),
+        cost_estimate=cost(4000000000),
+    )(where, *own, *partner, gains, gate, up)
+
+
+def down_of(step, where, hidden, down, n, width):
+    out = jax.ShapeDtypeStruct((n, hidden.shape[0], width), F32)
+    return pl.pallas_call(
+        functools.partial(down_kernel, n, step),
         out_shape=(out, out),
-        in_specs=[pl.BlockSpec(memory_space=pltpu.SMEM)] + [vmem] * (2 * n + 4),
-        out_specs=(vmem, vmem),
-        scratch_shapes=[pltpu.VMEM((rows, model), BF16)],
-        compiler_params=pltpu.CompilerParams(vmem_limit_bytes=10 * MIB),
-        cost_estimate=pl.CostEstimate(flops=3000000000, transcendentals=0, bytes_accessed=0),
-    )(where, *own, *partner, gains, gate, up, down)
+        in_specs=[SMEM, VMEM, VMEM],
+        out_specs=(VMEM, VMEM),
+        compiler_params=pltpu.CompilerParams(vmem_limit_bytes=6 * MIB),
+        cost_estimate=cost(500000000),
+    )(where, hidden, down)
 
 
 STEPS = 8
@@ -212,28 +236,20 @@
     return ref[pl.ds(i * rows, rows), :].astype(jnp.int32).astype(F32)
 
 
-def first_kernel(keep_ref, got_ref, own_ref, *out_refs):
-    n = keep_ref.shape[0]
+def first_kernel(keep_ref, got_ref, out_ref):
+    scaled([[keep_ref[k2] + got_ref[k2] for k2 in range(keep_ref.shape[0])]], [out_ref])
+
+
+def second_kernel(n, keep_ref, got_ref, *refs):
+    got_refs, sum_ref, out_refs = refs[: n - 1], refs[n - 1], refs[n:]
+    rows = keep_ref.shape[1]
+    by = [factors(got, n, rows) for got in got_refs]
+    totals = []
     for k2 in range(n):
-        own_ref[k2] = keep_ref[0, k2] + got_ref[0, k2]
-    blocks = [[keep_ref[k1, k2] + got_ref[k1, k2] for k2 in range(n)] for k1 in range(1, n)]
-    scaled(blocks, out_refs)
-
-
-def second_kernel(chunks, *refs):
-    ins, sum_ref, out_refs = refs[: 4 * chunks], refs[4 * chunks], refs[4 * chunks + 1 :]
-    n, rows, _ = ins[0].shape
-    totals = []
-    for chunk in range(chunks):
-        own_ref, *got_refs = ins[4 * chunk : 4 * chunk + 4]
-        by = [factors(got, n, rows) for got in got_refs]
-        totals.append([])
-        for k2 in range(n):
-            total = own_ref[k2]
-            for got, factor in zip(got_refs, by):
-                total = total + widened(got, k2, rows) * factor
-            totals[-1].append(total)
-    totals = [jnp.concatenate(parts, axis=0) for parts in zip(*totals)]
+        total = keep_ref[k2] + got_ref[k2]
+        for got, factor in zip(got_refs, by):
+            total = total + widened(got, k2, rows) * factor
+        totals.append(total)
     sum_ref[...] = totals[0]
     scaled([[total] for total in totals[1:]], out_refs)
 
@@ -251,24 +267,22 @@
     return jax.ShapeDtypeStruct((blocks * rows + SPARE, width), jnp.int16)
 
 
-def started(keep, send):
-    n, _, rows, width = keep.shape
+def first_sum(keep, got):
+    return pl.pallas_call(
+        first_kernel,
+        out_shape=coded(*keep.shape),
+        compiler_params=pltpu.CompilerParams(vmem_limit_bytes=6 * MIB),
+        cost_estimate=cost(100000000),
+    )(keep, got)
+
+
+def finished(keep, got, parts):
+    n, rows, width = keep.shape
     own, *parts = pl.pallas_call(
-        first_kernel,
-        out_shape=[jax.ShapeDtypeStruct((n, rows, width), F32)] + [coded(n, rows, width)] * (n - 1),
-        compiler_params=pltpu.CompilerParams(vmem_limit_bytes=8 * MIB),
-    )(keep, swapped(send))
-    return [own] + [along(part, 0, k + 1) for k, part in enumerate(parts)]
-
-
-def finished(chunks):
-    n, rows, width = chunks[0][0].shape
-    rows = rows * len(chunks)
-    own, *parts = pl.pallas_call(
-        functools.partial(second_kernel, len(chunks)),
+        functools.partial(second_kernel, n),
         out_shape=[jax.ShapeDtypeStruct((rows, width), F32)] + [coded(1, rows, width)] * (n - 1),
         compiler_params=pltpu.CompilerParams(vmem_limit_bytes=4 * MIB),
-    )(*[a for chunk in chunks for a in chunk])
+    )(keep, got, *parts)
     parts = [along(part, 1, k + 1) for k, part in enumerate(parts)]
     return pl.pallas_call(
         third_kernel,
@@ -281,6 +295,7 @@
     groups = lax.axis_size("expert")
     count, width = tokens.shape
     seat_limit = count // 2
+    n = lax.axis_size(TP[0])
     model = norm_gain.shape[0]
     where = jnp.stack([lax.axis_index(a) for a in TP]).astype(jnp.int32)
     gains = norm_gain.reshape(1, model)
@@ -292,18 +307,21 @@
     )(ids, active_row, tokens)
     arriving = lax.all_to_all(sent, "expert", split_axis=0, concat_axis=0, tiled=True)
     n = lax.axis_size(TP[0])
-    rows = arriving.reshape(CHUNKS, -1, width)
-    first = [rows] + [along(rows, 0, k) for k in range(1, n)]
-    weights = loaded((rows, gains, where), (gate_weight[0], up_weight[0], down_weight[0]))
-    owns = []
-    for stack in stacked(first):
-        owns.append([stack] + [along(stack, 1, k) for k in range(1, n)])
-    chunks = []
-    for own in owns:
-        partner = [swapped(a) for a in own]
-        keep, send = experts_of(where, own, partner, gains, *weights)
-        chunks.append(started(keep, send))
-    returning = finished(chunks).reshape(groups, seat_limit, width)
+    rows = arriving.reshape(-1, width)
+    stack = stacked([rows] + [along(rows, 0, k) for k in range(1, n)])
+    own = [stack] + [along(stack, 1, k) for k in range(1, n)]
+    gate, up, down = loaded((rows, gains, where), (gate_weight[0], up_weight[0], down_weight[0]))
+    partner = [swapped(a) for a in own]
+    hidden = hidden_of(where, own, partner, gains, gate, up)
+    keeps, gots = {}, {}
+    for step in STEP_ORDER:
+        keeps[step], send = down_of(step, where, hidden, down, n, width)
+        gots[step] = swapped(send)
+    parts = []
+    for step in range(1, n):
+        part = first_sum(keeps[step], gots[step])
+        parts.append(along(part, 0, step))
+    returning = finished(keeps[0], gots[0], parts).reshape(groups, seat_limit, width)
     arrived = lax.all_to_all(returning, "expert", split_axis=0, concat_axis=0, tiled=True)
     return pl.pallas_call(
         functools.partial(combine_kernel, seat_limit, groups),

time: 102 us -> 110 us (1.078); the launches traced: 102 us -> 109 us
  waiting for transfers between devices: 23.6 us -> 35 us
  starting transfers between devices: 27.6 us -> 19.9 us
  Pallas kernels: 20.8 us -> 23.7 us
    ppermute x28 -> x20, waiting for transfers between devices: 23.6 us -> 35 us  [moved(): return lax.ppermute(array, TP, pairs)]
    ppermute x28 -> x20, starting transfers between devices: 27.6 us -> 19.9 us  [moved(): return lax.ppermute(array, TP, pairs)]
    pallas_call x6 -> x10, Pallas kernels: 12.6 us -> 15.4 us  [the longest x1 7.98 us: hidden_of(): pl.pallas_call(functools.partial(hidden_kernel, n), out_shape=jax.ShapeDt...]
  transfers between devices with their start and end apart: 28 -> 20, of which waited for: 13 -> 10; matrix products, arithmetic and copies ran while one was open for 1% -> 1% of each run, Pallas kernels for 15% -> 7%
where the time goes in v1:
time: 110 us; the launch traced here: 109 us
  waiting for transfers between devices  35 us (32%)
  blocking collectives  29 us (26%)
  Pallas kernels  23.7 us (22%)
  starting transfers between devices  19.9 us (18%)
    ppermute x20, waiting for transfers between devices, moved(): return lax.ppermute(array, TP, pairs)  35 us
    ppermute x20, starting transfers between devices, moved(): return lax.ppermute(array, TP, pairs)  19.9 us
    all_to_all x1, blocking collectives, local(): lax.all_to_all(sent, 'expert', split_axis=0, concat_axis=0, tiled=True)  17.6 us
    all_to_all x1, blocking collectives, local(): lax.all_to_all(returning, 'expert', split_axis=0, concat_axis=0, tiled=True)  11.5 us
    pallas_call x1, Pallas kernels, hidden_of(): pl.pallas_call(functools.partial(hidden_kernel, n), out_shape=jax.ShapeDt...  7.98 us
    pallas_call x4, Pallas kernels, down_of(): pl.pallas_call(functools.partial(down_kernel, n, step), out_shape=(out, o...  5.22 us
    pallas_call x1, Pallas kernels, loaded(): pl.pallas_call(functools.partial(load_kernel, len(after)), out_shape=[jax...  4.23 us
    pallas_call x1, Pallas kernels, local(): pl.pallas_call(functools.partial(dispatch_kernel, seat_limit, groups), ou...  2.22 us
  transfers between devices with their start and end apart: 20, of which 10 were waited for; matrix products, arithmetic and copies ran while one was open for 1% of the time, Pallas kernels for 7%

profile of v1, /device:TPU:2, one launch (start us, length us, event | category | flops | bytes accessed | tf_op | source)
XLA Modules:
  0.0 108.5 jit_solution(8148482256124364010)
XLA Ops:
  0.0 2.2 %shard_map.82 = bf16[8,64,128]{2,1,0:T(8,128)(2,1)} custom-call(s32[2,128]{1,0:T(2,128)} %bitcast.17, s32[1,128]{1,0:T(1,128)} %bitcast.19, bf16[128,128]{1,0:T(8,128)(2,1)} %tokens_ref.1), custom_call_target="tpu_custom_call" | custom-call | tf_op jit(solution)/shard_map/pallas_call | solution.py:303
  2.2 17.6 %all_to_all.10 = bf16[8,64,128]{2,1,0:T(8,128)(2,1)S(1)} all-to-all(bf16[8,64,128]{2,1,0:T(8,128)(2,1)} %shard_map.82), channel_id=1, replica_groups=mesh['expert'=8,'tp_0'=4,'tp_1'=4,'tp_2'=2] {'expert'}, dimensions={0} | all-to-all | bytes 262144 | tf_op jit(solution)/shard_map/all_to_all | solution.py:308
  19.8 0.5 collective-permute-start.2
  20.3 2.4 %collective-permute-start.1 = (bf16[512,128]{1,0:T(8,128)(2,1)S(1)}, bf16[512,128]{1,0:T(8,128)(2,1)S(1)}, u32[]{:S(2)}, u32[]{:S(2)}) collective-permute-start(bf16[512,128]{1,0:T(8,128)(2,1)S(1)} %bitcast.12), channel_id=1, source_target_pairs={{0,16},{1,5},{2,18},{3,7},{4,20},{5,1},{6,22},{7,3},{8,24},{9,13},... | collective-permute-start | bytes 393224 | tf_op jit(solution)/shard_map/ppermute | solution.py:29
  22.7 1.8 %collective-permute-start = (bf16[512,128]{1,0:T(8,128)(2,1)S(1)}, bf16[512,128]{1,0:T(8,128)(2,1)S(1)}, u32[]{:S(2)}, u32[]{:S(2)}) collective-permute-start(bf16[512,128]{1,0:T(8,128)(2,1)S(1)} %bitcast.13), channel_id=1, source_target_pairs={{0,8},{1,3},{2,10},{3,5},{4,12},{5,7},{6,14},{7,1},{8,16},{9,11},{... | collective-permute-start | bytes 393224 | tf_op jit(solution)/shard_map/ppermute | solution.py:29
  24.7 2.3 %collective-permute-done.1.refs_2_ = bf16[512,128]{1,0:T(8,128)(2,1)S(1)} collective-permute-done((bf16[512,128]{1,0:T(8,128)(2,1)S(1)}, bf16[512,128]{1,0:T(8,128)(2,1)S(1)}, u32[]{:S(2)}, u32[]{:S(2)}) %collective-permute-start.1) | collective-permute-done | bytes 131104 | tf_op jit(solution)/shard_map/ppermute | solution.py:29
  27.1 1.1 %collective-permute-done.refs_1_ = bf16[512,128]{1,0:T(8,128)(2,1)S(1)} collective-permute-done((bf16[512,128]{1,0:T(8,128)(2,1)S(1)}, bf16[512,128]{1,0:T(8,128)(2,1)S(1)}, u32[]{:S(2)}, u32[]{:S(2)}) %collective-permute-start) | collective-permute-done | bytes 131104 | tf_op jit(solution)/shard_map/ppermute | solution.py:29
  28.3 3.1 %collective-permute-start.5 = (bf16[4,512,128]{2,1,0:T(8,128)(2,1)S(1)}, bf16[4,512,128]{2,1,0:T(8,128)(2,1)S(1)}, u32[]{:S(2)}, u32[]{:S(2)}) collective-permute-start(bf16[4,512,128]{2,1,0:T(8,128)(2,1)S(1)} %shard_map.83.refs_0_), channel_id=1, source_target_pairs={{0,6},{1,25},{2,0},{3,27},{4,2},{5,29},{6,4},{7,31},{8,14},{9,1},{... | collective-permute-start | bytes 1572872 | tf_op jit(solution)/shard_map/ppermute | solution.py:29
  31.4 0.6 collective-permute-start.4
  32.0 1.0 collective-permute-start.3
  33.0 10.7 %collective-permute-done.5.refs_3_ = bf16[4,512,128]{2,1,0:T(8,128)(2,1)S(1)} collective-permute-done((bf16[4,512,128]{2,1,0:T(8,128)(2,1)S(1)}, bf16[4,512,128]{2,1,0:T(8,128)(2,1)S(1)}, u32[]{:S(2)}, u32[]{:S(2)}) %collective-permute-start.5) | collective-permute-done | bytes 524320 | tf_op jit(solution)/shard_map/ppermute | solution.py:29
  44.2 3.5 %collective-permute-done.3.refs_1_ = bf16[4,512,128]{2,1,0:T(8,128)(2,1)S(1)} collective-permute-done((bf16[4,512,128]{2,1,0:T(8,128)(2,1)S(1)}, bf16[4,512,128]{2,1,0:T(8,128)(2,1)S(1)}, u32[]{:S(2)}, u32[]{:S(2)}) %collective-permute-start.3) | collective-permute-done | bytes 524320 | tf_op jit(solution)/shard_map/ppermute | solution.py:29
  47.7 0.7 reshape.14.refs_1_.refs_8_
  48.5 4.2 %shard_map.84 = (bf16[448,4096]{1,0:T(8,128)(2,1)S(1)}, bf16[448,4096]{1,0:T(8,128)(2,1)S(1)}, bf16[448,4096]{1,0:T(8,128)(2,1)S(1)}) custom-call(bf16[512,128]{1,0:T(8,128)(2,1)S(1)} %bitcast.15, bf16[1,4096]{1,0:T(2,128)(2,1)S(1)} %reshape.14.refs_1_.refs_8_, s32[3]{0:T(128)S(1)} %pad_add_fusion.refs_2_.where_ref, bf16[448,4096]{1,0:T(8,128)(2,1)} %bitcast.22, ...), custom_call_target="tpu_custom_call" | custom-call | flops 1500000000 | tf_op jit(solution)/shard_map/pallas_call | solution.py:146
  52.7 8.0 %shard_map.85.hidden_ref = bf16[512,448]{1,0:T(8,128)(2,1)S(1)} custom-call(s32[3]{0:T(128)S(1)} %pad_add_fusion.refs_2_.where_ref, bf16[4,512,128]{2,1,0:T(8,128)(2,1)S(1)} %shard_map.83.refs_0_, bf16[4,512,128]{2,1,0:T(8,128)(2,1)S(1)} %collective-permute-done.3.refs_1_, bf16[4,512,128]{2,1,0:T(8,128)(2,1)S(1)} %collective-permute-done.4.refs_2_, ...), custom_call_target="tpu_custom_call" | custom-call | flops 4000000000 | tf_op jit(solution)/shard_map/pallas_call | solution.py:182
  60.7 1.3 %shard_map.91 = (f32[4,512,128]{2,1,0:T(8,128)S(1)}, f32[4,512,128]{2,1,0:T(8,128)S(1)}) custom-call(s32[3]{0:T(128)S(1)} %pad_add_fusion.refs_2_.where_ref, bf16[512,448]{1,0:T(8,128)(2,1)S(1)} %shard_map.85.hidden_ref, bf16[448,4096]{1,0:T(8,128)(2,1)S(1)} %get-tuple-element.22.down_ref), custom_call_target="tpu_custom_call" | custom-call | flops 500000000 | tf_op jit(solution)/shard_map/pallas_call | solution.py:195
  62.0 1.3 %shard_map.89 = (f32[4,512,128]{2,1,0:T(8,128)S(1)}, f32[4,512,128]{2,1,0:T(8,128)S(1)}) custom-call(s32[3]{0:T(128)S(1)} %pad_add_fusion.refs_2_.where_ref, bf16[512,448]{1,0:T(8,128)(2,1)S(1)} %shard_map.85.hidden_ref, bf16[448,4096]{1,0:T(8,128)(2,1)S(1)} %get-tuple-element.22.down_ref), custom_call_target="tpu_custom_call" | custom-call | flops 500000000 | tf_op jit(solution)/shard_map/pallas_call | solution.py:195
  63.3 0.6 collective-permute-start.15
  64.0 1.3 %shard_map.87 = (f32[4,512,128]{2,1,0:T(8,128)S(1)}, f32[4,512,128]{2,1,0:T(8,128)S(1)}) custom-call(s32[3]{0:T(128)S(1)} %pad_add_fusion.refs_2_.where_ref, bf16[512,448]{1,0:T(8,128)(2,1)S(1)} %shard_map.85.hidden_ref, bf16[448,4096]{1,0:T(8,128)(2,1)S(1)} %get-tuple-element.22.down_ref), custom_call_target="tpu_custom_call" | custom-call | flops 500000000 | tf_op jit(solution)/shard_map/pallas_call | solution.py:195
  65.8 1.3 %shard_map.86 = (f32[4,512,128]{2,1,0:T(8,128)S(1)}, f32[4,512,128]{2,1,0:T(8,128)S(1)}) custom-call(s32[3]{0:T(128)S(1)} %pad_add_fusion.refs_2_.where_ref, bf16[512,448]{1,0:T(8,128)(2,1)S(1)} %shard_map.85.hidden_ref, bf16[448,4096]{1,0:T(8,128)(2,1)S(1)} %get-tuple-element.22.down_ref), custom_call_target="tpu_custom_call" | custom-call | flops 500000000 | tf_op jit(solution)/shard_map/pallas_call | solution.py:195
  67.7 2.8 %collective-permute-start.16 = (s16[2064,128]{1,0:T(8,128)(2,1)S(1)}, s16[2064,128]{1,0:T(8,128)(2,1)S(1)}, u32[]{:S(2)}, u32[]{:S(2)}) collective-permute-start(s16[2064,128]{1,0:T(8,128)(2,1)S(1)} %shard_map.92), channel_id=1, source_target_pairs={{0,24},{1,7},{2,26},{3,1},{4,28},{5,3},{6,30},{7,5},{8,0},{9,15},{... | collective-permute-start | bytes 1585160 | tf_op jit(solution)/shard_map/ppermute | solution.py:29
  71.8 1.9 %collective-permute-start.12 = (s16[2064,128]{1,0:T(8,128)(2,1)S(1)}, s16[2064,128]{1,0:T(8,128)(2,1)S(1)}, u32[]{:S(2)}, u32[]{:S(2)}) collective-permute-start(s16[2064,128]{1,0:T(8,128)(2,1)S(1)} %shard_map.88), channel_id=1, source_target_pairs={{0,8},{1,3},{2,10},{3,5},{4,12},{5,7},{6,14},{7,1},{8,16},{9,11},{... | collective-permute-start | bytes 1585160 | tf_op jit(solution)/shard_map/ppermute | solution.py:29
  73.7 3.6 %collective-permute-done.16.refs_2_ = s16[2064,128]{1,0:T(8,128)(2,1)S(1)} collective-permute-done((s16[2064,128]{1,0:T(8,128)(2,1)S(1)}, s16[2064,128]{1,0:T(8,128)(2,1)S(1)}, u32[]{:S(2)}, u32[]{:S(2)}) %collective-permute-start.16) | collective-permute-done | bytes 528416 | tf_op jit(solution)/shard_map/ppermute | solution.py:29
  77.3 6.3 %collective-permute-done.14.refs_1_ = s16[2064,128]{1,0:T(8,128)(2,1)S(1)} collective-permute-done((s16[2064,128]{1,0:T(8,128)(2,1)S(1)}, s16[2064,128]{1,0:T(8,128)(2,1)S(1)}, u32[]{:S(2)}, u32[]{:S(2)}) %collective-permute-start.14) | collective-permute-done | bytes 528416 | tf_op jit(solution)/shard_map/ppermute | solution.py:29
  83.6 1.9 %collective-permute-done.12.refs_0_ = s16[2064,128]{1,0:T(8,128)(2,1)S(1)} collective-permute-done((s16[2064,128]{1,0:T(8,128)(2,1)S(1)}, s16[2064,128]{1,0:T(8,128)(2,1)S(1)}, u32[]{:S(2)}, u32[]{:S(2)}) %collective-permute-start.12) | collective-permute-done | bytes 528416 | tf_op jit(solution)/shard_map/ppermute | solution.py:29
  85.5 1.1 shard_map.93
  86.6 2.1 %collective-permute-start.18 = (s16[528,128]{1,0:T(8,128)(2,1)S(1)}, s16[528,128]{1,0:T(8,128)(2,1)S(1)}, u32[]{:S(2)}, u32[]{:S(2)}) collective-permute-start(s16[528,128]{1,0:T(8,128)(2,1)S(1)} %get-tuple-element.33), channel_id=1, source_target_pairs={{0,4},{1,17},{2,6},{3,19},{4,0},{5,21},{6,2},{7,23},{8,12},{9,25},... | collective-permute-start | bytes 405512 | tf_op jit(solution)/shard_map/ppermute | solution.py:29
  88.7 1.2 %collective-permute-start.19 = (s16[528,128]{1,0:T(8,128)(2,1)S(1)}, s16[528,128]{1,0:T(8,128)(2,1)S(1)}, u32[]{:S(2)}, u32[]{:S(2)}) collective-permute-start(s16[528,128]{1,0:T(8,128)(2,1)S(1)} %get-tuple-element.34), channel_id=1, source_target_pairs={{0,6},{1,25},{2,0},{3,27},{4,2},{5,29},{6,4},{7,31},{8,14},{9,1},{... | collective-permute-start | bytes 405512 | tf_op jit(solution)/shard_map/ppermute | solution.py:29
  89.9 4.4 %collective-permute-done.17.refs_0_ = s16[528,128]{1,0:T(8,128)(2,1)S(1)} collective-permute-done((s16[528,128]{1,0:T(8,128)(2,1)S(1)}, s16[528,128]{1,0:T(8,128)(2,1)S(1)}, u32[]{:S(2)}, u32[]{:S(2)}) %collective-permute-start.17) | collective-permute-done | bytes 135200 | tf_op jit(solution)/shard_map/ppermute | solution.py:29
  94.3 0.9 collective-permute-done.19.refs_2_
  95.7 11.5 %all_to_all.11.arrived_ref = bf16[8,64,128]{2,1,0:T(8,128)(2,1)S(1)} all-to-all(bf16[8,64,128]{2,1,0:T(8,128)(2,1)S(1)} %bitcast.16), channel_id=1, replica_groups=mesh['expert'=8,'tp_0'=4,'tp_1'=4,'tp_2'=2] {'expert'}, dimensions={0} | all-to-all | bytes 262144 | tf_op jit(solution)/shard_map/all_to_all | solution.py:325
  107.2 1.3 %shard_map.95 = bf16[128,128]{1,0:T(8,128)(2,1)} custom-call(s32[2,128]{1,0:T(2,128)S(1)} %bitcast.18, s32[1,128]{1,0:T(1,128)S(1)} %bitcast.20, f32[2,128]{1,0:T(2,128)S(1)} %bitcast.21, bf16[8,64,128]{2,1,0:T(8,128)(2,1)S(1)} %all_to_all.11.arrived_ref), custom_call_target="tpu_custom_call" | custom-call | tf_op jit(solution)/shard_map/pallas_call | solution.py:326
  (32 shorter events, 3.9 us)
Async XLA Ops:
  19.8 5.0 %collective-permute-start.2 = (bf16[512,128]{1,0:T(8,128)(2,1)S(1)}, bf16[512,128]{1,0:T(8,128)(2,1)S(1)}, u32[]{:S(2)}, u32[]{:S(2)}) collective-permute-start(bf16[512,128]{1,0:T(8,128)(2,1)S(1)} %bitcast.11), channel_id=1, source_target_pairs={{0,24},{1,7},{2,26},{3,1},{4,28},{5,3},{6,30},{7,5},{8,0},{9,15},{... | collective-permute-start | bytes 393224 | tf_op jit(solution)/shard_map/ppermute | solution.py:29
  20.3 6.8 %collective-permute-start.1 = (bf16[512,128]{1,0:T(8,128)(2,1)S(1)}, bf16[512,128]{1,0:T(8,128)(2,1)S(1)}, u32[]{:S(2)}, u32[]{:S(2)}) collective-permute-start(bf16[512,128]{1,0:T(8,128)(2,1)S(1)} %bitcast.12), channel_id=1, source_target_pairs={{0,16},{1,5},{2,18},{3,7},{4,20},{5,1},{6,22},{7,3},{8,24},{9,13},... | collective-permute-start | bytes 393224 | tf_op jit(solution)/shard_map/ppermute | solution.py:29
  22.7 5.5 %collective-permute-start = (bf16[512,128]{1,0:T(8,128)(2,1)S(1)}, bf16[512,128]{1,0:T(8,128)(2,1)S(1)}, u32[]{:S(2)}, u32[]{:S(2)}) collective-permute-start(bf16[512,128]{1,0:T(8,128)(2,1)S(1)} %bitcast.13), channel_id=1, source_target_pairs={{0,8},{1,3},{2,10},{3,5},{4,12},{5,7},{6,14},{7,1},{8,16},{9,11},{... | collective-permute-start | bytes 393224 | tf_op jit(solution)/shard_map/ppermute | solution.py:29
  28.3 15.4 %collective-permute-start.5 = (bf16[4,512,128]{2,1,0:T(8,128)(2,1)S(1)}, bf16[4,512,128]{2,1,0:T(8,128)(2,1)S(1)}, u32[]{:S(2)}, u32[]{:S(2)}) collective-permute-start(bf16[4,512,128]{2,1,0:T(8,128)(2,1)S(1)} %shard_map.83.refs_0_), channel_id=1, source_target_pairs={{0,6},{1,25},{2,0},{3,27},{4,2},{5,29},{6,4},{7,31},{8,14},{9,1},{... | collective-permute-start | bytes 1572872 | tf_op jit(solution)/shard_map/ppermute | solution.py:29
  31.4 12.3 %collective-permute-start.4 = (bf16[4,512,128]{2,1,0:T(8,128)(2,1)S(1)}, bf16[4,512,128]{2,1,0:T(8,128)(2,1)S(1)}, u32[]{:S(2)}, u32[]{:S(2)}) collective-permute-start(bf16[4,512,128]{2,1,0:T(8,128)(2,1)S(1)} %shard_map.83.refs_0_), channel_id=1, source_target_pairs={{0,4},{1,17},{2,6},{3,19},{4,0},{5,21},{6,2},{7,23},{8,12},{9,25},... | collective-permute-start | bytes 1572872 | tf_op jit(solution)/shard_map/ppermute | solution.py:29
  32.0 15.7 %collective-permute-start.3 = (bf16[4,512,128]{2,1,0:T(8,128)(2,1)S(1)}, bf16[4,512,128]{2,1,0:T(8,128)(2,1)S(1)}, u32[]{:S(2)}, u32[]{:S(2)}) collective-permute-start(bf16[4,512,128]{2,1,0:T(8,128)(2,1)S(1)} %shard_map.83.refs_0_), channel_id=1, source_target_pairs={{0,2},{1,9},{2,4},{3,11},{4,6},{5,13},{6,0},{7,15},{8,10},{9,17},{... | collective-permute-start | bytes 1572872 | tf_op jit(solution)/shard_map/ppermute | solution.py:29
  33.0 19.7 %collective-permute-start.6 = (bf16[4,512,128]{2,1,0:T(8,128)(2,1)S(1)}, bf16[4,512,128]{2,1,0:T(8,128)(2,1)S(1)}, u32[]{:S(2)}, u32[]{:S(2)}) collective-permute-start(bf16[4,512,128]{2,1,0:T(8,128)(2,1)S(1)} %shard_map.83.refs_0_), channel_id=1, source_target_pairs={{0,1},{1,0},{2,3},{3,2},{4,5},{5,4},{6,7},{7,6},{8,9},{9,8},{10,11... | collective-permute-start | bytes 1572872 | tf_op jit(solution)/shard_map/ppermute | solution.py:29
  43.7 9.0 %collective-permute-start.9 = (bf16[4,512,128]{2,1,0:T(8,128)(2,1)S(1)}, bf16[4,512,128]{2,1,0:T(8,128)(2,1)S(1)}, u32[]{:S(2)}, u32[]{:S(2)}) collective-permute-start(bf16[4,512,128]{2,1,0:T(8,128)(2,1)S(1)} %collective-permute-done.5.refs_3_), channel_id=1, source_target_pairs={{0,1},{1,0},{2,3},{3,2},{4,5},{5,4},{6,7},{7,6},{8,9},{9,8},{10,11... | collective-permute-start | bytes 1572872 | tf_op jit(solution)/shard_map/ppermute | solution.py:29
  43.7 9.0 %collective-permute-start.8 = (bf16[4,512,128]{2,1,0:T(8,128)(2,1)S(1)}, bf16[4,512,128]{2,1,0:T(8,128)(2,1)}, u32[]{:S(2)}, u32[]{:S(2)}) collective-permute-start(bf16[4,512,128]{2,1,0:T(8,128)(2,1)S(1)} %collective-permute-done.4.refs_2_), channel_id=1, source_target_pairs={{0,1},{1,0},{2,3},{3,2},{4,5},{5,4},{6,7},{7,6},{8,9},{9,8},{10,11... | collective-permute-start | bytes 1572872 | tf_op jit(solution)/shard_map/ppermute | solution.py:29
  47.7 5.1 %collective-permute-start.7 = (bf16[4,512,128]{2,1,0:T(8,128)(2,1)S(1)}, bf16[4,512,128]{2,1,0:T(8,128)(2,1)}, u32[]{:S(2)}, u32[]{:S(2)}) collective-permute-start(bf16[4,512,128]{2,1,0:T(8,128)(2,1)S(1)} %collective-permute-done.3.refs_1_), channel_id=1, source_target_pairs={{0,1},{1,0},{2,3},{3,2},{4,5},{5,4},{6,7},{7,6},{8,9},{9,8},{10,11... | collective-permute-start | bytes 1572872 | tf_op jit(solution)/shard_map/ppermute | solution.py:29
  63.3 4.0 %collective-permute-start.15 = (f32[4,512,128]{2,1,0:T(8,128)S(1)}, f32[4,512,128]{2,1,0:T(8,128)S(1)}, u32[]{:S(2)}, u32[]{:S(2)}) collective-permute-start(f32[4,512,128]{2,1,0:T(8,128)S(1)} %get-tuple-element.30), channel_id=1, source_target_pairs={{0,1},{1,0},{2,3},{3,2},{4,5},{5,4},{6,7},{7,6},{8,9},{9,8},{10,11... | collective-permute-start | bytes 3145736 | tf_op jit(solution)/shard_map/ppermute | solution.py:29
  63.9 6.6 %collective-permute-start.13 = (f32[4,512,128]{2,1,0:T(8,128)S(1)}, f32[4,512,128]{2,1,0:T(8,128)S(1)}, u32[]{:S(2)}, u32[]{:S(2)}) collective-permute-start(f32[4,512,128]{2,1,0:T(8,128)S(1)} %get-tuple-element.28), channel_id=1, source_target_pairs={{0,1},{1,0},{2,3},{3,2},{4,5},{5,4},{6,7},{7,6},{8,9},{9,8},{10,11... | collective-permute-start | bytes 3145736 | tf_op jit(solution)/shard_map/ppermute | solution.py:29
  65.3 6.1 %collective-permute-start.11 = (f32[4,512,128]{2,1,0:T(8,128)S(1)}, f32[4,512,128]{2,1,0:T(8,128)S(1)}, u32[]{:S(2)}, u32[]{:S(2)}) collective-permute-start(f32[4,512,128]{2,1,0:T(8,128)S(1)} %get-tuple-element.26), channel_id=1, source_target_pairs={{0,1},{1,0},{2,3},{3,2},{4,5},{5,4},{6,7},{7,6},{8,9},{9,8},{10,11... | collective-permute-start | bytes 3145736 | tf_op jit(solution)/shard_map/ppermute | solution.py:29
  67.1 6.6 %collective-permute-start.10 = (f32[4,512,128]{2,1,0:T(8,128)S(1)}, f32[4,512,128]{2,1,0:T(8,128)S(1)}, u32[]{:S(2)}, u32[]{:S(2)}) collective-permute-start(f32[4,512,128]{2,1,0:T(8,128)S(1)} %get-tuple-element.24), channel_id=1, source_target_pairs={{0,1},{1,0},{2,3},{3,2},{4,5},{5,4},{6,7},{7,6},{8,9},{9,8},{10,11... | collective-permute-start | bytes 3145736 | tf_op jit(solution)/shard_map/ppermute | solution.py:29
  67.7 9.6 %collective-permute-start.16 = (s16[2064,128]{1,0:T(8,128)(2,1)S(1)}, s16[2064,128]{1,0:T(8,128)(2,1)S(1)}, u32[]{:S(2)}, u32[]{:S(2)}) collective-permute-start(s16[2064,128]{1,0:T(8,128)(2,1)S(1)} %shard_map.92), channel_id=1, source_target_pairs={{0,24},{1,7},{2,26},{3,1},{4,28},{5,3},{6,30},{7,5},{8,0},{9,15},{... | collective-permute-start | bytes 1585160 | tf_op jit(solution)/shard_map/ppermute | solution.py:29
  70.9 12.7 %collective-permute-start.14 = (s16[2064,128]{1,0:T(8,128)(2,1)S(1)}, s16[2064,128]{1,0:T(8,128)(2,1)S(1)}, u32[]{:S(2)}, u32[]{:S(2)}) collective-permute-start(s16[2064,128]{1,0:T(8,128)(2,1)S(1)} %shard_map.90), channel_id=1, source_target_pairs={{0,16},{1,5},{2,18},{3,7},{4,20},{5,1},{6,22},{7,3},{8,24},{9,13},... | collective-permute-start | bytes 1585160 | tf_op jit(solution)/shard_map/ppermute | solution.py:29
  71.4 35.8 %copy-start = (s32[128,2]{0,1:T(2,128)S(1)}, s32[128,2]{0,1:T(2,128)}, u32[]{:S(2)}) copy-start(s32[128,2]{0,1:T(2,128)} %param.11) | copy-start | bytes 3076
  71.4 35.8 %copy-start.1 = (s32[128]{0:T(128)S(1)}, s32[128]{0:T(128)}, u32[]{:S(2)}) copy-start(s32[128]{0:T(128)} %param.12) | copy-start | bytes 1540
  71.4 35.8 %copy-start.2 = (f32[128,2]{0,1:T(2,128)S(1)}, f32[128,2]{0,1:T(2,128)}, u32[]{:S(2)}) copy-start(f32[128,2]{0,1:T(2,128)} %param.10) | copy-start | bytes 3076
  71.8 13.7 %collective-permute-start.12 = (s16[2064,128]{1,0:T(8,128)(2,1)S(1)}, s16[2064,128]{1,0:T(8,128)(2,1)S(1)}, u32[]{:S(2)}, u32[]{:S(2)}) collective-permute-start(s16[2064,128]{1,0:T(8,128)(2,1)S(1)} %shard_map.88), channel_id=1, source_target_pairs={{0,8},{1,3},{2,10},{3,5},{4,12},{5,7},{6,14},{7,1},{8,16},{9,11},{... | collective-permute-start | bytes 1585160 | tf_op jit(solution)/shard_map/ppermute | solution.py:29
  86.5 7.7 %collective-permute-start.17 = (s16[528,128]{1,0:T(8,128)(2,1)S(1)}, s16[528,128]{1,0:T(8,128)(2,1)S(1)}, u32[]{:S(2)}, u32[]{:S(2)}) collective-permute-start(s16[528,128]{1,0:T(8,128)(2,1)S(1)} %get-tuple-element.32), channel_id=1, source_target_pairs={{0,2},{1,9},{2,4},{3,11},{4,6},{5,13},{6,0},{7,15},{8,10},{9,17},{... | collective-permute-start | bytes 405512 | tf_op jit(solution)/shard_map/ppermute | solution.py:29
  86.6 7.7 %collective-permute-start.18 = (s16[528,128]{1,0:T(8,128)(2,1)S(1)}, s16[528,128]{1,0:T(8,128)(2,1)S(1)}, u32[]{:S(2)}, u32[]{:S(2)}) collective-permute-start(s16[528,128]{1,0:T(8,128)(2,1)S(1)} %get-tuple-element.33), channel_id=1, source_target_pairs={{0,4},{1,17},{2,6},{3,19},{4,0},{5,21},{6,2},{7,23},{8,12},{9,25},... | collective-permute-start | bytes 405512 | tf_op jit(solution)/shard_map/ppermute | solution.py:29
  88.7 6.5 %collective-permute-start.19 = (s16[528,128]{1,0:T(8,128)(2,1)S(1)}, s16[528,128]{1,0:T(8,128)(2,1)S(1)}, u32[]{:S(2)}, u32[]{:S(2)}) collective-permute-start(s16[528,128]{1,0:T(8,128)(2,1)S(1)} %get-tuple-element.34), channel_id=1, source_target_pairs={{0,6},{1,25},{2,0},{3,27},{4,2},{5,29},{6,4},{7,31},{8,14},{9,1},{... | collective-permute-start | bytes 405512 | tf_op jit(solution)/shard_map/ppermute | solution.py:29

commit v2 on v1

--- a/solution.py
+++ b/solution.py
@@ -13,7 +13,6 @@
 epsilon = 1e-05
 F32, BF16 = jnp.float32, jnp.bfloat16
 MIB = 1024 * 1024
-STEP_ORDER = (2, 1, 3, 0)
 LOAD_MIB = 41
 
 
@@ -85,28 +84,31 @@
 
 
 def hidden_kernel(n, where_ref, *refs):
-    own, partner = refs[:n], refs[n : 2 * n]
-    gain_ref, gate_ref, up_ref, hidden_ref, normed_ref = refs[2 * n :]
+    own, partner = refs[: 2 * n], refs[2 * n : 4 * n]
+    gain_ref, gate_ref, up_ref, hidden_ref, normed_ref = refs[4 * n :]
     x, y, core = where_ref[0], where_ref[1], where_ref[2]
     rows, _ = normed_ref.shape
     width = own[0].shape[-1]
+    steps = [(k1, k2) for k2 in range(n) for k1 in range(n)]
     dims = (((1,), (1,)), ((), ()))
+
+    def piece(pieces, k1, k2):
+        return pieces[2 * k2 + k1 // (n // 2)][k1 % (n // 2), span].astype(F32)
+
     for half in range(own[0].shape[1] // rows):
         span = slice(half * rows, (half + 1) * rows)
         squares = jnp.zeros((rows, width), F32)
         for pieces in (own, partner):
-            for k2 in range(n):
-                for k1 in range(n):
-                    value = pieces[k2][k1, span].astype(F32)
-                    squares = squares + value * value
+            for k1, k2 in steps:
+                value = piece(pieces, k1, k2)
+                squares = squares + value * value
         mean_square = jnp.sum(squares, axis=1, keepdims=True) / (2 * n * n * width)
         scale = lax.rsqrt(mean_square + epsilon)
         for pieces, parity in ((own, core), (partner, 1 - core)):
-            for k2 in range(n):
-                for k1 in range(n):
-                    at = place(x - jnp.where(parity == 0, k1, k2), y - jnp.where(parity == 0, k2, k1), parity, n, width)
-                    value = pieces[k2][k1, span].astype(F32) * scale * gain_ref[:, at].astype(F32)
-                    normed_ref[:, at] = value.astype(BF16)
+            for k1, k2 in steps:
+                at = place(x - jnp.where(parity == 0, k1, k2), y - jnp.where(parity == 0, k2, k1), parity, n, width)
+                value = piece(pieces, k1, k2) * scale * gain_ref[:, at].astype(F32)
+                normed_ref[:, at] = value.astype(BF16)
         normed = normed_ref[...]
         gate = lax.dot_general(normed, gate_ref[...], dims, preferred_element_type=F32)
         up = lax.dot_general(normed, up_ref[...], dims, preferred_element_type=F32)
@@ -163,26 +165,28 @@
 
 
 def stack_kernel(*refs):
-    for k, ref in enumerate(refs[:-1]):
-        refs[-1][k] = ref[...]
+    half = (len(refs) - 2) // 2
+    for k, ref in enumerate(refs[:-2]):
+        refs[-2 + k // half][k % half] = ref[...]
 
 
 def stacked(pieces):
+    out = jax.ShapeDtypeStruct((len(pieces) // 2,) + pieces[0].shape, BF16)
     return pl.pallas_call(
         stack_kernel,
-        out_shape=jax.ShapeDtypeStruct((len(pieces),) + pieces[0].shape, BF16),
+        out_shape=(out, out),
         compiler_params=pltpu.CompilerParams(vmem_limit_bytes=4 * MIB),
     )(*pieces)
 
 
 def hidden_of(where, own, partner, gains, gate, up):
-    n = len(own)
+    n = len(own) // 2
     rows = own[0].shape[1]
     units, model = gate.shape
     return pl.pallas_call(
         functools.partial(hidden_kernel, n),
         out_shape=jax.ShapeDtypeStruct((rows, units), BF16),
-        in_specs=[SMEM] + [VMEM] * (2 * n + 3),
+        in_specs=[SMEM] + [VMEM] * (4 * n + 3),
         out_specs=VMEM,
         scratch_shapes=[pltpu.VMEM((rows // 2, model), BF16)],
         compiler_params=pltpu.CompilerParams(vmem_limit_bytes=10 * MIB),
@@ -236,19 +240,31 @@
     return ref[pl.ds(i * rows, rows), :].astype(jnp.int32).astype(F32)
 
 
-def first_kernel(keep_ref, got_ref, out_ref):
-    scaled([[keep_ref[k2] + got_ref[k2] for k2 in range(keep_ref.shape[0])]], [out_ref])
+def first_kernel(halves, keep_ref, got_ref, *out_refs):
+    half = keep_ref.shape[0] // 2
+    scaled([[keep_ref[half * h + i] + got_ref[half * h + i] for i in range(half)] for h in halves], out_refs)
+
+
+def relay_kernel(h, keep_ref, got_ref, passed_ref, out_ref):
+    half, rows = keep_ref.shape[0] // 2, keep_ref.shape[1]
+    factor = factors(passed_ref, half, rows)
+    blocks = [
+        keep_ref[half * h + i] + got_ref[half * h + i] + widened(passed_ref, i, rows) * factor
+        for i in range(half)
+    ]
+    scaled([blocks], [out_ref])
 
 
 def second_kernel(n, keep_ref, got_ref, *refs):
-    got_refs, sum_ref, out_refs = refs[: n - 1], refs[n - 1], refs[n:]
-    rows = keep_ref.shape[1]
-    by = [factors(got, n, rows) for got in got_refs]
+    got_refs, sum_ref, out_refs = refs[:4], refs[4], refs[5:]
+    half, rows = n // 2, keep_ref.shape[1]
+    by = [factors(got, half, rows) for got in got_refs]
     totals = []
     for k2 in range(n):
         total = keep_ref[k2] + got_ref[k2]
-        for got, factor in zip(got_refs, by):
-            total = total + widened(got, k2, rows) * factor
+        for side in range(2):
+            i = 2 * side + k2 // half
+            total = total + widened(got_refs[i], k2 % half, rows) * by[i]
         totals.append(total)
     sum_ref[...] = totals[0]
     scaled([[total] for total in totals[1:]], out_refs)
@@ -267,13 +283,24 @@
     return jax.ShapeDtypeStruct((blocks * rows + SPARE, width), jnp.int16)
 
 
-def first_sum(keep, got):
-    return pl.pallas_call(
-        first_kernel,
-        out_shape=coded(*keep.shape),
+def first_sum(halves, keep, got):
+    n, rows, width = keep.shape
+    return pl.pallas_call(
+        functools.partial(first_kernel, halves),
+        out_shape=[coded(n // 2, rows, width)] * len(halves),
         compiler_params=pltpu.CompilerParams(vmem_limit_bytes=6 * MIB),
         cost_estimate=cost(100000000),
     )(keep, got)
+
+
+def relayed(half, keep, got, passed):
+    n, rows, width = keep.shape
+    return pl.pallas_call(
+        functools.partial(relay_kernel, half),
+        out_shape=coded(n // 2, rows, width),
+        compiler_params=pltpu.CompilerParams(vmem_limit_bytes=6 * MIB),
+        cost_estimate=cost(100000000),
+    )(keep, got, passed)
 
 
 def finished(keep, got, parts):
@@ -308,20 +335,27 @@
     arriving = lax.all_to_all(sent, "expert", split_axis=0, concat_axis=0, tiled=True)
     n = lax.axis_size(TP[0])
     rows = arriving.reshape(-1, width)
-    stack = stacked([rows] + [along(rows, 0, k) for k in range(1, n)])
-    own = [stack] + [along(stack, 1, k) for k in range(1, n)]
+    spread = [along(rows, 0, k) for k in range(1, n)]
     gate, up, down = loaded((rows, gains, where), (gate_weight[0], up_weight[0], down_weight[0]))
+    low, high = stacked([rows] + spread)
+    low_1, high_3 = along(low, 1, 1), along(high, 1, -1)
+    high_1, low_3 = along(high, 1, 1), along(low, 1, -1)
+    low_2, high_2 = along(low_1, 1, 1), along(high_3, 1, -1)
+    own = [low, high, low_1, high_1, low_2, high_2, low_3, high_3]
     partner = [swapped(a) for a in own]
     hidden = hidden_of(where, own, partner, gains, gate, up)
     keeps, gots = {}, {}
-    for step in STEP_ORDER:
+    for step in (2, 1, 3, 0):
         keeps[step], send = down_of(step, where, hidden, down, n, width)
         gots[step] = swapped(send)
-    parts = []
-    for step in range(1, n):
-        part = first_sum(keeps[step], gots[step])
-        parts.append(along(part, 0, step))
-    returning = finished(keeps[0], gots[0], parts).reshape(groups, seat_limit, width)
+    low, high = first_sum((0, 1), keeps[2], gots[2])
+    low, high = along(low, 0, 1), along(high, 0, -1)
+    (high_1,), (low_3,) = first_sum((1,), keeps[1], gots[1]), first_sum((0,), keeps[3], gots[3])
+    high_1, low_3 = along(high_1, 0, 1), along(low_3, 0, -1)
+    low_1, high_3 = relayed(0, keeps[1], gots[1], low), relayed(1, keeps[3], gots[3], high)
+    low_1, high_3 = along(low_1, 0, 1), along(high_3, 0, -1)
+    returning = finished(keeps[0], gots[0], [low_1, high_1, low_3, high_3])
+    returning = returning.reshape(groups, seat_limit, width)
     arrived = lax.all_to_all(returning, "expert", split_axis=0, concat_axis=0, tiled=True)
     return pl.pallas_call(
         functools.partial(combine_kernel, seat_limit, groups),

time: 110 us -> 109 us (level)
  waiting for transfers between devices: 35 us -> 23.3 us
  starting transfers between devices: 19.9 us -> 29.9 us
    ppermute x20 -> x30, waiting for transfers between devices: 35 us -> 23.3 us  [moved(): return lax.ppermute(array, TP, pairs)]
    ppermute x20 -> x30, starting transfers between devices: 19.9 us -> 29.9 us  [moved(): return lax.ppermute(array, TP, pairs)]
  transfers between devices with their start and end apart: 20 -> 30, of which waited for: 10 -> 13; matrix products, arithmetic and copies ran while one was open for 1% -> 1% of each run, Pallas kernels for 7% -> 9%
where the time goes in v2:
time: 109 us; the launch traced here: 108 us
  starting transfers between devices  29.9 us (27%)
  blocking collectives  29.3 us (27%)
  Pallas kernels  24.2 us (22%)
  waiting for transfers between devices  23.3 us (21%)
    ppermute x30, starting transfers between devices, moved(): return lax.ppermute(array, TP, pairs)  29.9 us
    ppermute x30, waiting for transfers between devices, moved(): return lax.ppermute(array, TP, pairs)  23.3 us
    all_to_all x1, blocking collectives, local(): lax.all_to_all(sent, 'expert', split_axis=0, concat_axis=0, tiled=True)  17.6 us
    all_to_all x1, blocking collectives, local(): lax.all_to_all(returning, 'expert', split_axis=0, concat_axis=0, tiled=True)  11.7 us
    pallas_call x1, Pallas kernels, hidden_of(): pl.pallas_call(functools.partial(hidden_kernel, n), out_shape=jax.ShapeDt...  7.89 us
    pallas_call x4, Pallas kernels, down_of(): pl.pallas_call(functools.partial(down_kernel, n, step), out_shape=(out, o...  5.23 us
    pallas_call x1, Pallas kernels, loaded(): pl.pallas_call(functools.partial(load_kernel, len(after)), out_shape=[jax...  4.23 us
    pallas_call x1, Pallas kernels, local(): pl.pallas_call(functools.partial(dispatch_kernel, seat_limit, groups), ou...  2.21 us
  transfers between devices with their start and end apart: 30, of which 13 were waited for; matrix products, arithmetic and copies ran while one was open for 1% of the time, Pallas kernels for 9%

profile of v2, /device:TPU:2, one launch (start us, length us, event | category | flops | bytes accessed | tf_op | source)
XLA Modules:
  0.0 107.8 jit_solution(2009159000933987951)
XLA Ops:
  0.0 2.2 %shard_map.82 = bf16[8,64,128]{2,1,0:T(8,128)(2,1)} custom-call(s32[2,128]{1,0:T(2,128)} %bitcast.17, s32[1,128]{1,0:T(1,128)} %bitcast.19, bf16[128,128]{1,0:T(8,128)(2,1)} %tokens_ref.1), custom_call_target="tpu_custom_call" | custom-call | tf_op jit(solution)/shard_map/pallas_call | solution.py:330
  2.2 17.6 %all_to_all.10 = bf16[8,64,128]{2,1,0:T(8,128)(2,1)S(1)} all-to-all(bf16[8,64,128]{2,1,0:T(8,128)(2,1)} %shard_map.82), channel_id=1, replica_groups=mesh['expert'=8,'tp_0'=4,'tp_1'=4,'tp_2'=2] {'expert'}, dimensions={0} | all-to-all | bytes 262144 | tf_op jit(solution)/shard_map/all_to_all | solution.py:335
  20.3 2.4 %collective-permute-start.1 = (bf16[512,128]{1,0:T(8,128)(2,1)S(1)}, bf16[512,128]{1,0:T(8,128)(2,1)S(1)}, u32[]{:S(2)}, u32[]{:S(2)}) collective-permute-start(bf16[512,128]{1,0:T(8,128)(2,1)S(1)} %bitcast.12), channel_id=1, source_target_pairs={{0,16},{1,5},{2,18},{3,7},{4,20},{5,1},{6,22},{7,3},{8,24},{9,13},... | collective-permute-start | bytes 393224 | tf_op jit(solution)/shard_map/ppermute | solution.py:28
  22.7 1.8 %collective-permute-start = (bf16[512,128]{1,0:T(8,128)(2,1)S(1)}, bf16[512,128]{1,0:T(8,128)(2,1)S(1)}, u32[]{:S(2)}, u32[]{:S(2)}) collective-permute-start(bf16[512,128]{1,0:T(8,128)(2,1)S(1)} %bitcast.13), channel_id=1, source_target_pairs={{0,8},{1,3},{2,10},{3,5},{4,12},{5,7},{6,14},{7,1},{8,16},{9,11},{... | collective-permute-start | bytes 393224 | tf_op jit(solution)/shard_map/ppermute | solution.py:28
  24.7 2.3 %collective-permute-done.1.refs_2_ = bf16[512,128]{1,0:T(8,128)(2,1)S(1)} collective-permute-done((bf16[512,128]{1,0:T(8,128)(2,1)S(1)}, bf16[512,128]{1,0:T(8,128)(2,1)S(1)}, u32[]{:S(2)}, u32[]{:S(2)}) %collective-permute-start.1) | collective-permute-done | bytes 131104 | tf_op jit(solution)/shard_map/ppermute | solution.py:28
  27.1 1.1 %collective-permute-done.refs_1_ = bf16[512,128]{1,0:T(8,128)(2,1)S(1)} collective-permute-done((bf16[512,128]{1,0:T(8,128)(2,1)S(1)}, bf16[512,128]{1,0:T(8,128)(2,1)S(1)}, u32[]{:S(2)}, u32[]{:S(2)}) %collective-permute-start) | collective-permute-done | bytes 131104 | tf_op jit(solution)/shard_map/ppermute | solution.py:28
  28.3 3.1 %collective-permute-start.8 = (bf16[2,512,128]{2,1,0:T(8,128)(2,1)S(1)}, bf16[2,512,128]{2,1,0:T(8,128)(2,1)S(1)}, u32[]{:S(2)}, u32[]{:S(2)}) collective-permute-start(bf16[2,512,128]{2,1,0:T(8,128)(2,1)S(1)} %get-tuple-element.24.refs_0_), channel_id=1, source_target_pairs={{0,6},{1,25},{2,0},{3,27},{4,2},{5,29},{6,4},{7,31},{8,14},{9,1},{... | collective-permute-start | bytes 786440 | tf_op jit(solution)/shard_map/ppermute | solution.py:28
  31.4 3.2 %collective-permute-start.6 = (bf16[2,512,128]{2,1,0:T(8,128)(2,1)S(1)}, bf16[2,512,128]{2,1,0:T(8,128)(2,1)S(1)}, u32[]{:S(2)}, u32[]{:S(2)}) collective-permute-start(bf16[2,512,128]{2,1,0:T(8,128)(2,1)S(1)} %get-tuple-element.25.refs_1_), channel_id=1, source_target_pairs={{0,6},{1,25},{2,0},{3,27},{4,2},{5,29},{6,4},{7,31},{8,14},{9,1},{... | collective-permute-start | bytes 786440 | tf_op jit(solution)/shard_map/ppermute | solution.py:28
  35.3 1.0 collective-permute-start.15
  36.4 2.6 %collective-permute-done.3.refs_2_ = bf16[2,512,128]{2,1,0:T(8,128)(2,1)S(1)} collective-permute-done((bf16[2,512,128]{2,1,0:T(8,128)(2,1)S(1)}, bf16[2,512,128]{2,1,0:T(8,128)(2,1)S(1)}, u32[]{:S(2)}, u32[]{:S(2)}) %collective-permute-start.3) | collective-permute-done | bytes 262176 | tf_op jit(solution)/shard_map/ppermute | solution.py:28
  39.0 3.2 %collective-permute-start.7 = (bf16[2,512,128]{2,1,0:T(8,128)(2,1)S(1)}, bf16[2,512,128]{2,1,0:T(8,128)(2,1)S(1)}, u32[]{:S(2)}, u32[]{:S(2)}) collective-permute-start(bf16[2,512,128]{2,1,0:T(8,128)(2,1)S(1)} %collective-permute-done.6.refs_7_), channel_id=1, source_target_pairs={{0,6},{1,25},{2,0},{3,27},{4,2},{5,29},{6,4},{7,31},{8,14},{9,1},{... | collective-permute-start | bytes 786440 | tf_op jit(solution)/shard_map/ppermute | solution.py:28
  42.9 3.7 %collective-permute-done.5.refs_4_ = bf16[2,512,128]{2,1,0:T(8,128)(2,1)S(1)} collective-permute-done((bf16[2,512,128]{2,1,0:T(8,128)(2,1)S(1)}, bf16[2,512,128]{2,1,0:T(8,128)(2,1)S(1)}, u32[]{:S(2)}, u32[]{:S(2)}) %collective-permute-start.5) | collective-permute-done | bytes 262176 | tf_op jit(solution)/shard_map/ppermute | solution.py:28
  47.1 0.7 reshape.14.refs_1_.refs_16_
  47.9 4.2 %shard_map.84 = (bf16[448,4096]{1,0:T(8,128)(2,1)S(1)}, bf16[448,4096]{1,0:T(8,128)(2,1)S(1)}, bf16[448,4096]{1,0:T(8,128)(2,1)S(1)}) custom-call(bf16[512,128]{1,0:T(8,128)(2,1)S(1)} %bitcast.15, bf16[1,4096]{1,0:T(2,128)(2,1)S(1)} %reshape.14.refs_1_.refs_16_, s32[3]{0:T(128)S(1)} %pad_add_fusion.refs_2_.where_ref, bf16[448,4096]{1,0:T(8,128)(2,1)} %bitcast.22, ...), custom_call_target="tpu_custom_call" | custom-call | flops 1500000000 | tf_op jit(solution)/shard_map/pallas_call | solution.py:148
  52.2 7.9 %shard_map.85.hidden_ref = bf16[512,448]{1,0:T(8,128)(2,1)S(1)} custom-call(s32[3]{0:T(128)S(1)} %pad_add_fusion.refs_2_.where_ref, bf16[2,512,128]{2,1,0:T(8,128)(2,1)S(1)} %get-tuple-element.24.refs_0_, bf16[2,512,128]{2,1,0:T(8,128)(2,1)S(1)} %get-tuple-element.25.refs_1_, bf16[2,512,128]{2,1,0:T(8,128)(2,1)S(1)} %collective-permute-done.3.refs_2_, ...), custom_call_target="tpu_custom_call" | custom-call | flops 4000000000 | tf_op jit(solution)/shard_map/pallas_call | solution.py:186
  60.1 1.3 %shard_map.88 = (f32[4,512,128]{2,1,0:T(8,128)S(1)}, f32[4,512,128]{2,1,0:T(8,128)S(1)}) custom-call(s32[3]{0:T(128)S(1)} %pad_add_fusion.refs_2_.where_ref, bf16[512,448]{1,0:T(8,128)(2,1)S(1)} %shard_map.85.hidden_ref, bf16[448,4096]{1,0:T(8,128)(2,1)S(1)} %get-tuple-element.28.down_ref), custom_call_target="tpu_custom_call" | custom-call | flops 500000000 | tf_op jit(solution)/shard_map/pallas_call | solution.py:199
  61.5 1.3 %shard_map.92 = (f32[4,512,128]{2,1,0:T(8,128)S(1)}, f32[4,512,128]{2,1,0:T(8,128)S(1)}) custom-call(s32[3]{0:T(128)S(1)} %pad_add_fusion.refs_2_.where_ref, bf16[512,448]{1,0:T(8,128)(2,1)S(1)} %shard_map.85.hidden_ref, bf16[448,4096]{1,0:T(8,128)(2,1)S(1)} %get-tuple-element.28.down_ref), custom_call_target="tpu_custom_call" | custom-call | flops 500000000 | tf_op jit(solution)/shard_map/pallas_call | solution.py:199
  63.4 1.3 %shard_map.87 = (f32[4,512,128]{2,1,0:T(8,128)S(1)}, f32[4,512,128]{2,1,0:T(8,128)S(1)}) custom-call(s32[3]{0:T(128)S(1)} %pad_add_fusion.refs_2_.where_ref, bf16[512,448]{1,0:T(8,128)(2,1)S(1)} %shard_map.85.hidden_ref, bf16[448,4096]{1,0:T(8,128)(2,1)S(1)} %get-tuple-element.28.down_ref), custom_call_target="tpu_custom_call" | custom-call | flops 500000000 | tf_op jit(solution)/shard_map/pallas_call | solution.py:199
  64.8 1.3 %shard_map.86 = (f32[4,512,128]{2,1,0:T(8,128)S(1)}, f32[4,512,128]{2,1,0:T(8,128)S(1)}) custom-call(s32[3]{0:T(128)S(1)} %pad_add_fusion.refs_2_.where_ref, bf16[512,448]{1,0:T(8,128)(2,1)S(1)} %shard_map.85.hidden_ref, bf16[448,4096]{1,0:T(8,128)(2,1)S(1)} %get-tuple-element.28.down_ref), custom_call_target="tpu_custom_call" | custom-call | flops 500000000 | tf_op jit(solution)/shard_map/pallas_call | solution.py:199
  67.1 2.8 %collective-permute-start.25 = (s16[1040,128]{1,0:T(8,128)(2,1)S(1)}, s16[1040,128]{1,0:T(8,128)(2,1)S(1)}, u32[]{:S(2)}, u32[]{:S(2)}) collective-permute-start(s16[1040,128]{1,0:T(8,128)(2,1)S(1)} %get-tuple-element.38), channel_id=1, source_target_pairs={{0,24},{1,7},{2,26},{3,1},{4,28},{5,3},{6,30},{7,5},{8,0},{9,15},{... | collective-permute-start | bytes 798728 | tf_op jit(solution)/shard_map/ppermute | solution.py:28
  70.2 2.1 %collective-permute-start.24 = (s16[1040,128]{1,0:T(8,128)(2,1)S(1)}, s16[1040,128]{1,0:T(8,128)(2,1)S(1)}, u32[]{:S(2)}, u32[]{:S(2)}) collective-permute-start(s16[1040,128]{1,0:T(8,128)(2,1)S(1)} %shard_map.93), channel_id=1, source_target_pairs={{0,24},{1,7},{2,26},{3,1},{4,28},{5,3},{6,30},{7,5},{8,0},{9,15},{... | collective-permute-start | bytes 798728 | tf_op jit(solution)/shard_map/ppermute | solution.py:28
  72.6 1.2 %collective-permute-done.25.passed_ref = s16[1040,128]{1,0:T(8,128)(2,1)S(1)} collective-permute-done((s16[1040,128]{1,0:T(8,128)(2,1)S(1)}, s16[1040,128]{1,0:T(8,128)(2,1)S(1)}, u32[]{:S(2)}, u32[]{:S(2)}) %collective-permute-start.25) | collective-permute-done | bytes 266272 | tf_op jit(solution)/shard_map/ppermute | solution.py:28
  74.4 2.6 %collective-permute-start.26 = (s16[1040,128]{1,0:T(8,128)(2,1)S(1)}, s16[1040,128]{1,0:T(8,128)(2,1)S(1)}, u32[]{:S(2)}, u32[]{:S(2)}) collective-permute-start(s16[1040,128]{1,0:T(8,128)(2,1)S(1)} %shard_map.94), channel_id=1, source_target_pairs={{0,24},{1,7},{2,26},{3,1},{4,28},{5,3},{6,30},{7,5},{8,0},{9,15},{... | collective-permute-start | bytes 798728 | tf_op jit(solution)/shard_map/ppermute | solution.py:28
  77.5 1.7 %collective-permute-done.22.refs_1_ = s16[1040,128]{1,0:T(8,128)(2,1)S(1)} collective-permute-done((s16[1040,128]{1,0:T(8,128)(2,1)S(1)}, s16[1040,128]{1,0:T(8,128)(2,1)S(1)}, u32[]{:S(2)}, u32[]{:S(2)}) %collective-permute-start.22) | collective-permute-done | bytes 266272 | tf_op jit(solution)/shard_map/ppermute | solution.py:28
  79.2 1.7 %collective-permute-done.26.refs_3_ = s16[1040,128]{1,0:T(8,128)(2,1)S(1)} collective-permute-done((s16[1040,128]{1,0:T(8,128)(2,1)S(1)}, s16[1040,128]{1,0:T(8,128)(2,1)S(1)}, u32[]{:S(2)}, u32[]{:S(2)}) %collective-permute-start.26) | collective-permute-done | bytes 266272 | tf_op jit(solution)/shard_map/ppermute | solution.py:28
  80.9 3.0 %collective-permute-done.21.refs_0_ = s16[1040,128]{1,0:T(8,128)(2,1)S(1)} collective-permute-done((s16[1040,128]{1,0:T(8,128)(2,1)S(1)}, s16[1040,128]{1,0:T(8,128)(2,1)S(1)}, u32[]{:S(2)}, u32[]{:S(2)}) %collective-permute-start.21) | collective-permute-done | bytes 266272 | tf_op jit(solution)/shard_map/ppermute | solution.py:28
  83.9 1.0 shard_map.95
  85.0 4.2 %collective-permute-start.28 = (s16[528,128]{1,0:T(8,128)(2,1)S(1)}, s16[528,128]{1,0:T(8,128)(2,1)S(1)}, u32[]{:S(2)}, u32[]{:S(2)}) collective-permute-start(s16[528,128]{1,0:T(8,128)(2,1)S(1)} %get-tuple-element.41), channel_id=1, source_target_pairs={{0,4},{1,17},{2,6},{3,19},{4,0},{5,21},{6,2},{7,23},{8,12},{9,25},... | collective-permute-start | bytes 405512 | tf_op jit(solution)/shard_map/ppermute | solution.py:28
  89.2 2.0 %collective-permute-done.27.refs_0_ = s16[528,128]{1,0:T(8,128)(2,1)S(1)} collective-permute-done((s16[528,128]{1,0:T(8,128)(2,1)S(1)}, s16[528,128]{1,0:T(8,128)(2,1)S(1)}, u32[]{:S(2)}, u32[]{:S(2)}) %collective-permute-start.27) | collective-permute-done | bytes 135200 | tf_op jit(solution)/shard_map/ppermute | solution.py:28
  91.2 2.4 %collective-permute-done.28.refs_1_ = s16[528,128]{1,0:T(8,128)(2,1)S(1)} collective-permute-done((s16[528,128]{1,0:T(8,128)(2,1)S(1)}, s16[528,128]{1,0:T(8,128)(2,1)S(1)}, u32[]{:S(2)}, u32[]{:S(2)}) %collective-permute-start.28) | collective-permute-done | bytes 135200 | tf_op jit(solution)/shard_map/ppermute | solution.py:28
  94.7 11.7 %all_to_all.11.arrived_ref = bf16[8,64,128]{2,1,0:T(8,128)(2,1)S(1)} all-to-all(bf16[8,64,128]{2,1,0:T(8,128)(2,1)S(1)} %bitcast.16), channel_id=1, replica_groups=mesh['expert'=8,'tp_0'=4,'tp_1'=4,'tp_2'=2] {'expert'}, dimensions={0} | all-to-all | bytes 262144 | tf_op jit(solution)/shard_map/all_to_all | solution.py:359
  106.5 1.3 %shard_map.97 = bf16[128,128]{1,0:T(8,128)(2,1)} custom-call(s32[2,128]{1,0:T(2,128)S(1)} %bitcast.18, s32[1,128]{1,0:T(1,128)S(1)} %bitcast.20, f32[2,128]{1,0:T(2,128)S(1)} %bitcast.21, bf16[8,64,128]{2,1,0:T(8,128)(2,1)S(1)} %all_to_all.11.arrived_ref), custom_call_target="tpu_custom_call" | custom-call | tf_op jit(solution)/shard_map/pallas_call | solution.py:360
  (54 shorter events, 7.3 us)
Async XLA Ops:
  19.8 5.0 %collective-permute-start.2 = (bf16[512,128]{1,0:T(8,128)(2,1)S(1)}, bf16[512,128]{1,0:T(8,128)(2,1)S(1)}, u32[]{:S(2)}, u32[]{:S(2)}) collective-permute-start(bf16[512,128]{1,0:T(8,128)(2,1)S(1)} %bitcast.11), channel_id=1, source_target_pairs={{0,24},{1,7},{2,26},{3,1},{4,28},{5,3},{6,30},{7,5},{8,0},{9,15},{... | collective-permute-start | bytes 393224 | tf_op jit(solution)/shard_map/ppermute | solution.py:28
  20.3 6.8 %collective-permute-start.1 = (bf16[512,128]{1,0:T(8,128)(2,1)S(1)}, bf16[512,128]{1,0:T(8,128)(2,1)S(1)}, u32[]{:S(2)}, u32[]{:S(2)}) collective-permute-start(bf16[512,128]{1,0:T(8,128)(2,1)S(1)} %bitcast.12), channel_id=1, source_target_pairs={{0,16},{1,5},{2,18},{3,7},{4,20},{5,1},{6,22},{7,3},{8,24},{9,13},... | collective-permute-start | bytes 393224 | tf_op jit(solution)/shard_map/ppermute | solution.py:28
  22.7 5.5 %collective-permute-start = (bf16[512,128]{1,0:T(8,128)(2,1)S(1)}, bf16[512,128]{1,0:T(8,128)(2,1)S(1)}, u32[]{:S(2)}, u32[]{:S(2)}) collective-permute-start(bf16[512,128]{1,0:T(8,128)(2,1)S(1)} %bitcast.13), channel_id=1, source_target_pairs={{0,8},{1,3},{2,10},{3,5},{4,12},{5,7},{6,14},{7,1},{8,16},{9,11},{... | collective-permute-start | bytes 393224 | tf_op jit(solution)/shard_map/ppermute | solution.py:28
  28.2 6.4 %collective-permute-start.9 = (bf16[2,512,128]{2,1,0:T(8,128)(2,1)S(1)}, bf16[2,512,128]{2,1,0:T(8,128)(2,1)S(1)}, u32[]{:S(2)}, u32[]{:S(2)}) collective-permute-start(bf16[2,512,128]{2,1,0:T(8,128)(2,1)S(1)} %get-tuple-element.24.refs_0_), channel_id=1, source_target_pairs={{0,1},{1,0},{2,3},{3,2},{4,5},{5,4},{6,7},{7,6},{8,9},{9,8},{10,11... | collective-permute-start | bytes 786440 | tf_op jit(solution)/shard_map/ppermute | solution.py:28
  28.3 7.0 %collective-permute-start.8 = (bf16[2,512,128]{2,1,0:T(8,128)(2,1)S(1)}, bf16[2,512,128]{2,1,0:T(8,128)(2,1)S(1)}, u32[]{:S(2)}, u32[]{:S(2)}) collective-permute-start(bf16[2,512,128]{2,1,0:T(8,128)(2,1)S(1)} %get-tuple-element.24.refs_0_), channel_id=1, source_target_pairs={{0,6},{1,25},{2,0},{3,27},{4,2},{5,29},{6,4},{7,31},{8,14},{9,1},{... | collective-permute-start | bytes 786440 | tf_op jit(solution)/shard_map/ppermute | solution.py:28
  31.4 7.6 %collective-permute-start.3 = (bf16[2,512,128]{2,1,0:T(8,128)(2,1)S(1)}, bf16[2,512,128]{2,1,0:T(8,128)(2,1)S(1)}, u32[]{:S(2)}, u32[]{:S(2)}) collective-permute-start(bf16[2,512,128]{2,1,0:T(8,128)(2,1)S(1)} %get-tuple-element.24.refs_0_), channel_id=1, source_target_pairs={{0,2},{1,9},{2,4},{3,11},{4,6},{5,13},{6,0},{7,15},{8,10},{9,17},{... | collective-permute-start | bytes 786440 | tf_op jit(solution)/shard_map/ppermute | solution.py:28
  31.4 7.6 %collective-permute-start.6 = (bf16[2,512,128]{2,1,0:T(8,128)(2,1)S(1)}, bf16[2,512,128]{2,1,0:T(8,128)(2,1)S(1)}, u32[]{:S(2)}, u32[]{:S(2)}) collective-permute-start(bf16[2,512,128]{2,1,0:T(8,128)(2,1)S(1)} %get-tuple-element.25.refs_1_), channel_id=1, source_target_pairs={{0,6},{1,25},{2,0},{3,27},{4,2},{5,29},{6,4},{7,31},{8,14},{9,1},{... | collective-permute-start | bytes 786440 | tf_op jit(solution)/shard_map/ppermute | solution.py:28
  34.7 7.6 %collective-permute-start.10 = (bf16[2,512,128]{2,1,0:T(8,128)(2,1)S(1)}, bf16[2,512,128]{2,1,0:T(8,128)(2,1)S(1)}, u32[]{:S(2)}, u32[]{:S(2)}) collective-permute-start(bf16[2,512,128]{2,1,0:T(8,128)(2,1)S(1)} %get-tuple-element.25.refs_1_), channel_id=1, source_target_pairs={{0,1},{1,0},{2,3},{3,2},{4,5},{5,4},{6,7},{7,6},{8,9},{9,8},{10,11... | collective-permute-start | bytes 786440 | tf_op jit(solution)/shard_map/ppermute | solution.py:28
  34.7 7.6 %collective-permute-start.4 = (bf16[2,512,128]{2,1,0:T(8,128)(2,1)S(1)}, bf16[2,512,128]{2,1,0:T(8,128)(2,1)S(1)}, u32[]{:S(2)}, u32[]{:S(2)}) collective-permute-start(bf16[2,512,128]{2,1,0:T(8,128)(2,1)S(1)} %get-tuple-element.25.refs_1_), channel_id=1, source_target_pairs={{0,2},{1,9},{2,4},{3,11},{4,6},{5,13},{6,0},{7,15},{8,10},{9,17},{... | collective-permute-start | bytes 786440 | tf_op jit(solution)/shard_map/ppermute | solution.py:28
  35.3 7.5 %collective-permute-start.15 = (bf16[2,512,128]{2,1,0:T(8,128)(2,1)S(1)}, bf16[2,512,128]{2,1,0:T(8,128)(2,1)S(1)}, u32[]{:S(2)}, u32[]{:S(2)}) collective-permute-start(bf16[2,512,128]{2,1,0:T(8,128)(2,1)S(1)} %collective-permute-done.8.refs_6_), channel_id=1, source_target_pairs={{0,1},{1,0},{2,3},{3,2},{4,5},{5,4},{6,7},{7,6},{8,9},{9,8},{10,11... | collective-permute-start | bytes 786440 | tf_op jit(solution)/shard_map/ppermute | solution.py:28
  39.0 7.6 %collective-permute-start.5 = (bf16[2,512,128]{2,1,0:T(8,128)(2,1)S(1)}, bf16[2,512,128]{2,1,0:T(8,128)(2,1)S(1)}, u32[]{:S(2)}, u32[]{:S(2)}) collective-permute-start(bf16[2,512,128]{2,1,0:T(8,128)(2,1)S(1)} %collective-permute-done.3.refs_2_), channel_id=1, source_target_pairs={{0,2},{1,9},{2,4},{3,11},{4,6},{5,13},{6,0},{7,15},{8,10},{9,17},{... | collective-permute-start | bytes 786440 | tf_op jit(solution)/shard_map/ppermute | solution.py:28
  39.0 7.6 %collective-permute-start.7 = (bf16[2,512,128]{2,1,0:T(8,128)(2,1)S(1)}, bf16[2,512,128]{2,1,0:T(8,128)(2,1)S(1)}, u32[]{:S(2)}, u32[]{:S(2)}) collective-permute-start(bf16[2,512,128]{2,1,0:T(8,128)(2,1)S(1)} %collective-permute-done.6.refs_7_), channel_id=1, source_target_pairs={{0,6},{1,25},{2,0},{3,27},{4,2},{5,29},{6,4},{7,31},{8,14},{9,1},{... | collective-permute-start | bytes 786440 | tf_op jit(solution)/shard_map/ppermute | solution.py:28
  42.3 9.9 %collective-permute-start.11 = (bf16[2,512,128]{2,1,0:T(8,128)(2,1)S(1)}, bf16[2,512,128]{2,1,0:T(8,128)(2,1)S(1)}, u32[]{:S(2)}, u32[]{:S(2)}) collective-permute-start(bf16[2,512,128]{2,1,0:T(8,128)(2,1)S(1)} %collective-permute-done.3.refs_2_), channel_id=1, source_target_pairs={{0,1},{1,0},{2,3},{3,2},{4,5},{5,4},{6,7},{7,6},{8,9},{9,8},{10,11... | collective-permute-start | bytes 786440 | tf_op jit(solution)/shard_map/ppermute | solution.py:28
  42.3 9.9 %collective-permute-start.16 = (bf16[2,512,128]{2,1,0:T(8,128)(2,1)S(1)}, bf16[2,512,128]{2,1,0:T(8,128)(2,1)S(1)}, u32[]{:S(2)}, u32[]{:S(2)}) collective-permute-start(bf16[2,512,128]{2,1,0:T(8,128)(2,1)S(1)} %collective-permute-done.6.refs_7_), channel_id=1, source_target_pairs={{0,1},{1,0},{2,3},{3,2},{4,5},{5,4},{6,7},{7,6},{8,9},{9,8},{10,11... | collective-permute-start | bytes 786440 | tf_op jit(solution)/shard_map/ppermute | solution.py:28
  42.8 9.4 %collective-permute-start.12 = (bf16[2,512,128]{2,1,0:T(8,128)(2,1)S(1)}, bf16[2,512,128]{2,1,0:T(8,128)(2,1)}, u32[]{:S(2)}, u32[]{:S(2)}) collective-permute-start(bf16[2,512,128]{2,1,0:T(8,128)(2,1)S(1)} %collective-permute-done.4.refs_3_), channel_id=1, source_target_pairs={{0,1},{1,0},{2,3},{3,2},{4,5},{5,4},{6,7},{7,6},{8,9},{9,8},{10,11... | collective-permute-start | bytes 786440 | tf_op jit(solution)/shard_map/ppermute | solution.py:28
  46.6 5.6 %collective-permute-start.13 = (bf16[2,512,128]{2,1,0:T(8,128)(2,1)S(1)}, bf16[2,512,128]{2,1,0:T(8,128)(2,1)}, u32[]{:S(2)}, u32[]{:S(2)}) collective-permute-start(bf16[2,512,128]{2,1,0:T(8,128)(2,1)S(1)} %collective-permute-done.5.refs_4_), channel_id=1, source_target_pairs={{0,1},{1,0},{2,3},{3,2},{4,5},{5,4},{6,7},{7,6},{8,9},{9,8},{10,11... | collective-permute-start | bytes 786440 | tf_op jit(solution)/shard_map/ppermute | solution.py:28
  46.6 5.6 %collective-permute-start.14 = (bf16[2,512,128]{2,1,0:T(8,128)(2,1)S(1)}, bf16[2,512,128]{2,1,0:T(8,128)(2,1)}, u32[]{:S(2)}, u32[]{:S(2)}) collective-permute-start(bf16[2,512,128]{2,1,0:T(8,128)(2,1)S(1)} %collective-permute-done.7.refs_5_), channel_id=1, source_target_pairs={{0,1},{1,0},{2,3},{3,2},{4,5},{5,4},{6,7},{7,6},{8,9},{9,8},{10,11... | collective-permute-start | bytes 786440 | tf_op jit(solution)/shard_map/ppermute | solution.py:28
  61.4 5.3 %collective-permute-start.19 = (f32[4,512,128]{2,1,0:T(8,128)S(1)}, f32[4,512,128]{2,1,0:T(8,128)S(1)}, u32[]{:S(2)}, u32[]{:S(2)}) collective-permute-start(f32[4,512,128]{2,1,0:T(8,128)S(1)} %get-tuple-element.34), channel_id=1, source_target_pairs={{0,1},{1,0},{2,3},{3,2},{4,5},{5,4},{6,7},{7,6},{8,9},{9,8},{10,11... | collective-permute-start | bytes 3145736 | tf_op jit(solution)/shard_map/ppermute | solution.py:28
  62.8 7.1 %collective-permute-start.23 = (f32[4,512,128]{2,1,0:T(8,128)S(1)}, f32[4,512,128]{2,1,0:T(8,128)S(1)}, u32[]{:S(2)}, u32[]{:S(2)}) collective-permute-start(f32[4,512,128]{2,1,0:T(8,128)S(1)} %get-tuple-element.37), channel_id=1, source_target_pairs={{0,1},{1,0},{2,3},{3,2},{4,5},{5,4},{6,7},{7,6},{8,9},{9,8},{10,11... | collective-permute-start | bytes 3145736 | tf_op jit(solution)/shard_map/ppermute | solution.py:28
  64.7 7.6 %collective-permute-start.18 = (f32[4,512,128]{2,1,0:T(8,128)S(1)}, f32[4,512,128]{2,1,0:T(8,128)S(1)}, u32[]{:S(2)}, u32[]{:S(2)}) collective-permute-start(f32[4,512,128]{2,1,0:T(8,128)S(1)} %get-tuple-element.32), channel_id=1, source_target_pairs={{0,1},{1,0},{2,3},{3,2},{4,5},{5,4},{6,7},{7,6},{8,9},{9,8},{10,11... | collective-permute-start | bytes 3145736 | tf_op jit(solution)/shard_map/ppermute | solution.py:28
  66.1 11.4 %collective-permute-start.17 = (f32[4,512,128]{2,1,0:T(8,128)S(1)}, f32[4,512,128]{2,1,0:T(8,128)S(1)}, u32[]{:S(2)}, u32[]{:S(2)}) collective-permute-start(f32[4,512,128]{2,1,0:T(8,128)S(1)} %get-tuple-element.30), channel_id=1, source_target_pairs={{0,1},{1,0},{2,3},{3,2},{4,5},{5,4},{6,7},{7,6},{8,9},{9,8},{10,11... | collective-permute-start | bytes 3145736 | tf_op jit(solution)/shard_map/ppermute | solution.py:28
  67.1 6.8 %collective-permute-start.25 = (s16[1040,128]{1,0:T(8,128)(2,1)S(1)}, s16[1040,128]{1,0:T(8,128)(2,1)S(1)}, u32[]{:S(2)}, u32[]{:S(2)}) collective-permute-start(s16[1040,128]{1,0:T(8,128)(2,1)S(1)} %get-tuple-element.38), channel_id=1, source_target_pairs={{0,24},{1,7},{2,26},{3,1},{4,28},{5,3},{6,30},{7,5},{8,0},{9,15},{... | collective-permute-start | bytes 798728 | tf_op jit(solution)/shard_map/ppermute | solution.py:28
  69.9 7.0 %collective-permute-start.20 = (s16[1040,128]{1,0:T(8,128)(2,1)S(1)}, s16[1040,128]{1,0:T(8,128)(2,1)S(1)}, u32[]{:S(2)}, u32[]{:S(2)}) collective-permute-start(s16[1040,128]{1,0:T(8,128)(2,1)S(1)} %get-tuple-element.35), channel_id=1, source_target_pairs={{0,8},{1,3},{2,10},{3,5},{4,12},{5,7},{6,14},{7,1},{8,16},{9,11},{... | collective-permute-start | bytes 798728 | tf_op jit(solution)/shard_map/ppermute | solution.py:28
  70.2 7.3 %collective-permute-start.24 = (s16[1040,128]{1,0:T(8,128)(2,1)S(1)}, s16[1040,128]{1,0:T(8,128)(2,1)S(1)}, u32[]{:S(2)}, u32[]{:S(2)}) collective-permute-start(s16[1040,128]{1,0:T(8,128)(2,1)S(1)} %shard_map.93), channel_id=1, source_target_pairs={{0,24},{1,7},{2,26},{3,1},{4,28},{5,3},{6,30},{7,5},{8,0},{9,15},{... | collective-permute-start | bytes 798728 | tf_op jit(solution)/shard_map/ppermute | solution.py:28
  72.5 6.7 %collective-permute-start.22 = (s16[1040,128]{1,0:T(8,128)(2,1)S(1)}, s16[1040,128]{1,0:T(8,128)(2,1)S(1)}, u32[]{:S(2)}, u32[]{:S(2)}) collective-permute-start(s16[1040,128]{1,0:T(8,128)(2,1)S(1)} %shard_map.91), channel_id=1, source_target_pairs={{0,8},{1,3},{2,10},{3,5},{4,12},{5,7},{6,14},{7,1},{8,16},{9,11},{... | collective-permute-start | bytes 798728 | tf_op jit(solution)/shard_map/ppermute | solution.py:28
  74.3 32.1 %copy-start = (s32[128,2]{0,1:T(2,128)S(1)}, s32[128,2]{0,1:T(2,128)}, u32[]{:S(2)}) copy-start(s32[128,2]{0,1:T(2,128)} %param.11) | copy-start | bytes 3076
  74.3 32.1 %copy-start.1 = (s32[128]{0:T(128)S(1)}, s32[128]{0:T(128)}, u32[]{:S(2)}) copy-start(s32[128]{0:T(128)} %param.12) | copy-start | bytes 1540
  74.4 6.5 %collective-permute-start.26 = (s16[1040,128]{1,0:T(8,128)(2,1)S(1)}, s16[1040,128]{1,0:T(8,128)(2,1)S(1)}, u32[]{:S(2)}, u32[]{:S(2)}) collective-permute-start(s16[1040,128]{1,0:T(8,128)(2,1)S(1)} %shard_map.94), channel_id=1, source_target_pairs={{0,24},{1,7},{2,26},{3,1},{4,28},{5,3},{6,30},{7,5},{8,0},{9,15},{... | collective-permute-start | bytes 798728 | tf_op jit(solution)/shard_map/ppermute | solution.py:28
  77.4 6.5 %collective-permute-start.21 = (s16[1040,128]{1,0:T(8,128)(2,1)S(1)}, s16[1040,128]{1,0:T(8,128)(2,1)S(1)}, u32[]{:S(2)}, u32[]{:S(2)}) collective-permute-start(s16[1040,128]{1,0:T(8,128)(2,1)S(1)} %shard_map.90), channel_id=1, source_target_pairs={{0,8},{1,3},{2,10},{3,5},{4,12},{5,7},{6,14},{7,1},{8,16},{9,11},{... | collective-permute-start | bytes 798728 | tf_op jit(solution)/shard_map/ppermute | solution.py:28
  84.9 6.3 %collective-permute-start.27 = (s16[528,128]{1,0:T(8,128)(2,1)S(1)}, s16[528,128]{1,0:T(8,128)(2,1)S(1)}, u32[]{:S(2)}, u32[]{:S(2)}) collective-permute-start(s16[528,128]{1,0:T(8,128)(2,1)S(1)} %get-tuple-element.40), channel_id=1, source_target_pairs={{0,2},{1,9},{2,4},{3,11},{4,6},{5,13},{6,0},{7,15},{8,10},{9,17},{... | collective-permute-start | bytes 405512 | tf_op jit(solution)/shard_map/ppermute | solution.py:28
  85.0 8.6 %collective-permute-start.28 = (s16[528,128]{1,0:T(8,128)(2,1)S(1)}, s16[528,128]{1,0:T(8,128)(2,1)S(1)}, u32[]{:S(2)}, u32[]{:S(2)}) collective-permute-start(s16[528,128]{1,0:T(8,128)(2,1)S(1)} %get-tuple-element.41), channel_id=1, source_target_pairs={{0,4},{1,17},{2,6},{3,19},{4,0},{5,21},{6,2},{7,23},{8,12},{9,25},... | collective-permute-start | bytes 405512 | tf_op jit(solution)/shard_map/ppermute | solution.py:28
  89.2 5.0 %collective-permute-start.29 = (s16[528,128]{1,0:T(8,128)(2,1)S(1)}, s16[528,128]{1,0:T(8,128)(2,1)S(1)}, u32[]{:S(2)}, u32[]{:S(2)}) collective-permute-start(s16[528,128]{1,0:T(8,128)(2,1)S(1)} %get-tuple-element.42), channel_id=1, source_target_pairs={{0,6},{1,25},{2,0},{3,27},{4,2},{5,29},{6,4},{7,31},{8,14},{9,1},{... | collective-permute-start | bytes 405512 | tf_op jit(solution)/shard_map/ppermute | solution.py:28
  (1 other events, 32.1 us)

commit v3 on v0

--- a/solution.py
+++ b/solution.py
@@ -14,7 +14,7 @@
 F32, BF16 = jnp.float32, jnp.bfloat16
 MIB = 1024 * 1024
 CHUNKS = 2
-LOAD_MIB = 41
+STACK_FLOPS = 5000000000
 
 
 def moved(array, target):
@@ -122,43 +122,25 @@
             send_ref[two, one] = jnp.where(core == 0, high, low)
 
 
-def load_kernel(skipped, *refs):
+def stack_kernel(skipped, *refs):
     refs = refs[skipped:]
-    sources, targets, sems = refs[:3], refs[3:6], refs[6]
-    copies = [pltpu.make_async_copy(a, b, sems.at[i]) for i, (a, b) in enumerate(zip(sources, targets))]
-    for copy in copies:
-        copy.start()
-    for copy in copies:
-        copy.wait()
-
-
-def loaded(after, weights):
-    hbm = pl.BlockSpec(memory_space=pltpu.HBM)
-    return pl.pallas_call(
-        functools.partial(load_kernel, len(after)),
-        out_shape=[jax.ShapeDtypeStruct(w.shape, w.dtype) for w in weights],
-        in_specs=[hbm] * (len(after) + len(weights)),
-        out_specs=[pl.BlockSpec(memory_space=pltpu.VMEM)] * len(weights),
-        scratch_shapes=[pltpu.SemaphoreType.DMA((len(weights),))],
-        compiler_params=pltpu.CompilerParams(vmem_limit_bytes=LOAD_MIB * MIB),
-        cost_estimate=pl.CostEstimate(flops=1500000000, transcendentals=0, bytes_accessed=0),
-    )(*after, *weights)
-
-
-def stack_kernel(*refs):
     half = len(refs) - CHUNKS
     for chunk, out_ref in enumerate(refs[half:]):
         for k, ref in enumerate(refs[:half]):
             out_ref[k] = ref[chunk]
 
 
-def stacked(pieces):
+def stacked(after, pieces):
     out = jax.ShapeDtypeStruct((len(pieces),) + pieces[0].shape[1:], BF16)
     return pl.pallas_call(
-        stack_kernel,
+        functools.partial(stack_kernel, len(after)),
         out_shape=[out] * CHUNKS,
+        in_specs=[pl.BlockSpec(memory_space=pltpu.HBM)] * len(after)
+        + [pl.BlockSpec(memory_space=pltpu.VMEM)] * len(pieces),
+        out_specs=[pl.BlockSpec(memory_space=pltpu.VMEM)] * CHUNKS,
         compiler_params=pltpu.CompilerParams(vmem_limit_bytes=4 * MIB),
-    )(*pieces)
+        cost_estimate=pl.CostEstimate(flops=STACK_FLOPS, transcendentals=0, bytes_accessed=0),
+    )(*after, *pieces)
 
 
 def experts_of(where, own, partner, gains, gate, up, down):
@@ -294,9 +276,9 @@
     n = lax.axis_size(TP[0])
     rows = arriving.reshape(CHUNKS, -1, width)
     first = [rows] + [along(rows, 0, k) for k in range(1, n)]
-    weights = loaded((rows, gains, where), (gate_weight[0], up_weight[0], down_weight[0]))
+    weights = (gate_weight[0], up_weight[0], down_weight[0])
     owns = []
-    for stack in stacked(first):
+    for stack in stacked((gains, where), first):
         owns.append([stack] + [along(stack, 1, k) for k in range(1, n)])
     chunks = []
     for own in owns:

time: 102 us -> 100 us (0.980)
  Pallas kernels: 20.8 us -> 16.6 us
  waiting for transfers between devices: 23.6 us -> 25.1 us
    pallas_call x2 -> x1, Pallas kernels: 4.26 us -> 0.03 us  [stacked(): pl.pallas_call(functools.partial(stack_kernel, len(after)), out_shape=[ou...]
    ppermute x28, waiting for transfers between devices: 23.6 us -> 25.1 us  [moved(): return lax.ppermute(array, TP, pairs)]
  transfers between devices with their start and end apart: 28 -> 28, of which waited for: 13 -> 15; matrix products, arithmetic and copies ran while one was open for 1% -> 1% of each run, Pallas kernels for 15% -> 12%
where the time goes in v3:
time: 100 us
  blocking collectives  29 us (29%)
  starting transfers between devices  28.3 us (28%)
  waiting for transfers between devices  25.1 us (25%)
  Pallas kernels  16.6 us (17%)
    ppermute x28, starting transfers between devices, moved(): return lax.ppermute(array, TP, pairs)  28.3 us
    ppermute x28, waiting for transfers between devices, moved(): return lax.ppermute(array, TP, pairs)  25.1 us
    all_to_all x1, blocking collectives, local(): lax.all_to_all(sent, 'expert', split_axis=0, concat_axis=0, tiled=True)  17.6 us
    all_to_all x1, blocking collectives, local(): lax.all_to_all(returning, 'expert', split_axis=0, concat_axis=0, tiled=True)  11.5 us
    pallas_call x2, Pallas kernels, experts_of(): pl.pallas_call(functools.partial(expert_kernel, n), out_shape=(out, out),...  10.5 us
    pallas_call x1, Pallas kernels, local(): pl.pallas_call(functools.partial(dispatch_kernel, seat_limit, groups), ou...  2.19 us
  transfers between devices with their start and end apart: 28, of which 15 were waited for; matrix products, arithmetic and copies ran while one was open for 1% of the time, Pallas kernels for 12%

profile of v3, /device:TPU:2, one launch (start us, length us, event | category | flops | bytes accessed | tf_op | source)
XLA Modules:
  0.0 100.0 jit_solution(12247884882738138962)
XLA Ops:
  0.0 2.2 %shard_map.82 = bf16[8,64,128]{2,1,0:T(8,128)(2,1)} custom-call(s32[2,128]{1,0:T(2,128)} %bitcast.22, s32[1,128]{1,0:T(1,128)} %bitcast.24, bf16[128,128]{1,0:T(8,128)(2,1)} %tokens_ref.1), custom_call_target="tpu_custom_call" | custom-call | tf_op jit(solution)/shard_map/pallas_call | solution.py:270
  2.2 17.6 %all_to_all.10 = bf16[8,64,128]{2,1,0:T(8,128)(2,1)S(1)} all-to-all(bf16[8,64,128]{2,1,0:T(8,128)(2,1)} %shard_map.82), channel_id=1, replica_groups=mesh['expert'=8,'tp_0'=4,'tp_1'=4,'tp_2'=2] {'expert'}, dimensions={0} | all-to-all | bytes 262144 | tf_op jit(solution)/shard_map/all_to_all | solution.py:275
  19.8 1.5 %collective-permute-start = (bf16[2,256,128]{2,1,0:T(8,128)(2,1)S(1)}, bf16[2,256,128]{2,1,0:T(8,128)(2,1)S(1)}, u32[]{:S(2)}, u32[]{:S(2)}) collective-permute-start(bf16[2,256,128]{2,1,0:T(8,128)(2,1)S(1)} %bitcast.18), channel_id=1, source_target_pairs={{0,8},{1,3},{2,10},{3,5},{4,12},{5,7},{6,14},{7,1},{8,16},{9,11},{... | collective-permute-start | bytes 393224 | tf_op jit(solution)/shard_map/ppermute | solution.py:29
  21.2 1.1 %collective-permute-start.1 = (bf16[2,256,128]{2,1,0:T(8,128)(2,1)S(1)}, bf16[2,256,128]{2,1,0:T(8,128)(2,1)S(1)}, u32[]{:S(2)}, u32[]{:S(2)}) collective-permute-start(bf16[2,256,128]{2,1,0:T(8,128)(2,1)S(1)} %bitcast.19), channel_id=1, source_target_pairs={{0,16},{1,5},{2,18},{3,7},{4,20},{5,1},{6,22},{7,3},{8,24},{9,13},... | collective-permute-start | bytes 393224 | tf_op jit(solution)/shard_map/ppermute | solution.py:29
  22.4 2.2 %collective-permute-start.2 = (bf16[2,256,128]{2,1,0:T(8,128)(2,1)S(1)}, bf16[2,256,128]{2,1,0:T(8,128)(2,1)S(1)}, u32[]{:S(2)}, u32[]{:S(2)}) collective-permute-start(bf16[2,256,128]{2,1,0:T(8,128)(2,1)S(1)} %bitcast.20), channel_id=1, source_target_pairs={{0,24},{1,7},{2,26},{3,1},{4,28},{5,3},{6,30},{7,5},{8,0},{9,15},{... | collective-permute-start | bytes 393224 | tf_op jit(solution)/shard_map/ppermute | solution.py:29
  25.3 2.5 %collective-permute-done.1.refs_4_ = bf16[2,256,128]{2,1,0:T(8,128)(2,1)S(1)} collective-permute-done((bf16[2,256,128]{2,1,0:T(8,128)(2,1)S(1)}, bf16[2,256,128]{2,1,0:T(8,128)(2,1)S(1)}, u32[]{:S(2)}, u32[]{:S(2)}) %collective-permute-start.1) | collective-permute-done | bytes 131104 | tf_op jit(solution)/shard_map/ppermute | solution.py:29
  27.8 0.9 collective-permute-done.2.refs_5_
  28.8 1.7 %collective-permute-start.14 = (bf16[4,256,128]{2,1,0:T(8,128)(2,1)S(1)}, bf16[4,256,128]{2,1,0:T(8,128)(2,1)S(1)}, u32[]{:S(2)}, u32[]{:S(2)}) collective-permute-start(bf16[4,256,128]{2,1,0:T(8,128)(2,1)S(1)} %get-tuple-element.30.refs_0_), channel_id=1, source_target_pairs={{0,2},{1,9},{2,4},{3,11},{4,6},{5,13},{6,0},{7,15},{8,10},{9,17},{... | collective-permute-start | bytes 786440 | tf_op jit(solution)/shard_map/ppermute | solution.py:29
  30.4 2.9 %collective-permute-start.15 = (bf16[4,256,128]{2,1,0:T(8,128)(2,1)S(1)}, bf16[4,256,128]{2,1,0:T(8,128)(2,1)S(1)}, u32[]{:S(2)}, u32[]{:S(2)}) collective-permute-start(bf16[4,256,128]{2,1,0:T(8,128)(2,1)S(1)} %get-tuple-element.30.refs_0_), channel_id=1, source_target_pairs={{0,4},{1,17},{2,6},{3,19},{4,0},{5,21},{6,2},{7,23},{8,12},{9,25},... | collective-permute-start | bytes 786440 | tf_op jit(solution)/shard_map/ppermute | solution.py:29
  33.3 1.3 %collective-permute-start.16 = (bf16[4,256,128]{2,1,0:T(8,128)(2,1)S(1)}, bf16[4,256,128]{2,1,0:T(8,128)(2,1)S(1)}, u32[]{:S(2)}, u32[]{:S(2)}) collective-permute-start(bf16[4,256,128]{2,1,0:T(8,128)(2,1)S(1)} %get-tuple-element.30.refs_0_), channel_id=1, source_target_pairs={{0,6},{1,25},{2,0},{3,27},{4,2},{5,29},{6,4},{7,31},{8,14},{9,1},{... | collective-permute-start | bytes 786440 | tf_op jit(solution)/shard_map/ppermute | solution.py:29
  35.4 1.1 %collective-permute-done.14.refs_1_ = bf16[4,256,128]{2,1,0:T(8,128)(2,1)S(1)} collective-permute-done((bf16[4,256,128]{2,1,0:T(8,128)(2,1)S(1)}, bf16[4,256,128]{2,1,0:T(8,128)(2,1)S(1)}, u32[]{:S(2)}, u32[]{:S(2)}) %collective-permute-start.14) | collective-permute-done | bytes 262176 | tf_op jit(solution)/shard_map/ppermute | solution.py:29
  36.4 2.0 %collective-permute-start.4 = (bf16[4,256,128]{2,1,0:T(8,128)(2,1)S(1)}, bf16[4,256,128]{2,1,0:T(8,128)(2,1)S(1)}, u32[]{:S(2)}, u32[]{:S(2)}) collective-permute-start(bf16[4,256,128]{2,1,0:T(8,128)(2,1)S(1)} %get-tuple-element.23.refs_0_), channel_id=1, source_target_pairs={{0,4},{1,17},{2,6},{3,19},{4,0},{5,21},{6,2},{7,23},{8,12},{9,25},... | collective-permute-start | bytes 786440 | tf_op jit(solution)/shard_map/ppermute | solution.py:29
  38.4 2.2 %collective-permute-done.15.refs_2_ = bf16[4,256,128]{2,1,0:T(8,128)(2,1)S(1)} collective-permute-done((bf16[4,256,128]{2,1,0:T(8,128)(2,1)S(1)}, bf16[4,256,128]{2,1,0:T(8,128)(2,1)S(1)}, u32[]{:S(2)}, u32[]{:S(2)}) %collective-permute-start.15) | collective-permute-done | bytes 262176 | tf_op jit(solution)/shard_map/ppermute | solution.py:29
  41.1 2.2 %collective-permute-done.3.refs_1_ = bf16[4,256,128]{2,1,0:T(8,128)(2,1)S(1)} collective-permute-done((bf16[4,256,128]{2,1,0:T(8,128)(2,1)S(1)}, bf16[4,256,128]{2,1,0:T(8,128)(2,1)S(1)}, u32[]{:S(2)}, u32[]{:S(2)}) %collective-permute-start.3) | collective-permute-done | bytes 262176 | tf_op jit(solution)/shard_map/ppermute | solution.py:29
  43.3 2.8 %collective-permute-done.4.refs_2_ = bf16[4,256,128]{2,1,0:T(8,128)(2,1)S(1)} collective-permute-done((bf16[4,256,128]{2,1,0:T(8,128)(2,1)S(1)}, bf16[4,256,128]{2,1,0:T(8,128)(2,1)S(1)}, u32[]{:S(2)}, u32[]{:S(2)}) %collective-permute-start.4) | collective-permute-done | bytes 262176 | tf_op jit(solution)/shard_map/ppermute | solution.py:29
  47.8 5.3 %shard_map.86 = (f32[4,4,256,128]{3,2,1,0:T(8,128)S(1)}, f32[4,4,256,128]{3,2,1,0:T(8,128)S(1)}) custom-call(s32[3]{0:T(128)S(1)} %pad_add_fusion.refs_1_.where_ref, bf16[4,256,128]{2,1,0:T(8,128)(2,1)S(1)} %get-tuple-element.30.refs_0_, bf16[4,256,128]{2,1,0:T(8,128)(2,1)S(1)} %collective-permute-done.14.refs_1_, ...), custom_call_target="tpu_custom_call" | custom-call | flops 3000000000 | tf_op jit(solution)/shard_map/pallas_call | solution.py:152
  53.4 5.2 %shard_map.84 = (f32[4,4,256,128]{3,2,1,0:T(8,128)S(1)}, f32[4,4,256,128]{3,2,1,0:T(8,128)S(1)}) custom-call(s32[3]{0:T(128)S(1)} %pad_add_fusion.refs_1_.where_ref, bf16[4,256,128]{2,1,0:T(8,128)(2,1)S(1)} %get-tuple-element.23.refs_0_, bf16[4,256,128]{2,1,0:T(8,128)(2,1)S(1)} %collective-permute-done.3.refs_1_, ...), custom_call_target="tpu_custom_call" | custom-call | flops 3000000000 | tf_op jit(solution)/shard_map/pallas_call | solution.py:152
  59.5 1.1 %collective-permute-start.22 = (s16[1040,128]{1,0:T(8,128)(2,1)S(1)}, s16[1040,128]{1,0:T(8,128)(2,1)S(1)}, u32[]{:S(2)}, u32[]{:S(2)}) collective-permute-start(s16[1040,128]{1,0:T(8,128)(2,1)S(1)} %get-tuple-element.34), channel_id=1, source_target_pairs={{0,8},{1,3},{2,10},{3,5},{4,12},{5,7},{6,14},{7,1},{8,16},{9,11},{... | collective-permute-start | bytes 798728 | tf_op jit(solution)/shard_map/ppermute | solution.py:29
  60.6 1.8 %collective-permute-start.23 = (s16[1040,128]{1,0:T(8,128)(2,1)S(1)}, s16[1040,128]{1,0:T(8,128)(2,1)S(1)}, u32[]{:S(2)}, u32[]{:S(2)}) collective-permute-start(s16[1040,128]{1,0:T(8,128)(2,1)S(1)} %get-tuple-element.35), channel_id=1, source_target_pairs={{0,16},{1,5},{2,18},{3,7},{4,20},{5,1},{6,22},{7,3},{8,24},{9,13},... | collective-permute-start | bytes 798728 | tf_op jit(solution)/shard_map/ppermute | solution.py:29
  62.4 2.0 %collective-permute-start.24 = (s16[1040,128]{1,0:T(8,128)(2,1)S(1)}, s16[1040,128]{1,0:T(8,128)(2,1)S(1)}, u32[]{:S(2)}, u32[]{:S(2)}) collective-permute-start(s16[1040,128]{1,0:T(8,128)(2,1)S(1)} %get-tuple-element.36), channel_id=1, source_target_pairs={{0,24},{1,7},{2,26},{3,1},{4,28},{5,3},{6,30},{7,5},{8,0},{9,15},{... | collective-permute-start | bytes 798728 | tf_op jit(solution)/shard_map/ppermute | solution.py:29
  65.1 2.9 %collective-permute-start.12 = (s16[1040,128]{1,0:T(8,128)(2,1)S(1)}, s16[1040,128]{1,0:T(8,128)(2,1)S(1)}, u32[]{:S(2)}, u32[]{:S(2)}) collective-permute-start(s16[1040,128]{1,0:T(8,128)(2,1)S(1)} %get-tuple-element.28), channel_id=1, source_target_pairs={{0,16},{1,5},{2,18},{3,7},{4,20},{5,1},{6,22},{7,3},{8,24},{9,13},... | collective-permute-start | bytes 798728 | tf_op jit(solution)/shard_map/ppermute | solution.py:29
  68.6 2.8 %collective-permute-done.24.refs_7_ = s16[1040,128]{1,0:T(8,128)(2,1)S(1)} collective-permute-done((s16[1040,128]{1,0:T(8,128)(2,1)S(1)}, s16[1040,128]{1,0:T(8,128)(2,1)S(1)}, u32[]{:S(2)}, u32[]{:S(2)}) %collective-permute-start.24) | collective-permute-done | bytes 266272 | tf_op jit(solution)/shard_map/ppermute | solution.py:29
  71.7 2.6 %collective-permute-done.12.refs_2_ = s16[1040,128]{1,0:T(8,128)(2,1)S(1)} collective-permute-done((s16[1040,128]{1,0:T(8,128)(2,1)S(1)}, s16[1040,128]{1,0:T(8,128)(2,1)S(1)}, u32[]{:S(2)}, u32[]{:S(2)}) %collective-permute-start.12) | collective-permute-done | bytes 266272 | tf_op jit(solution)/shard_map/ppermute | solution.py:29
  74.4 2.8 %collective-permute-done.13.refs_3_ = s16[1040,128]{1,0:T(8,128)(2,1)S(1)} collective-permute-done((s16[1040,128]{1,0:T(8,128)(2,1)S(1)}, s16[1040,128]{1,0:T(8,128)(2,1)S(1)}, u32[]{:S(2)}, u32[]{:S(2)}) %collective-permute-start.13) | collective-permute-done | bytes 266272 | tf_op jit(solution)/shard_map/ppermute | solution.py:29
  77.1 1.0 shard_map.88
  78.1 1.5 %collective-permute-start.25 = (s16[528,128]{1,0:T(8,128)(2,1)S(1)}, s16[528,128]{1,0:T(8,128)(2,1)S(1)}, u32[]{:S(2)}, u32[]{:S(2)}) collective-permute-start(s16[528,128]{1,0:T(8,128)(2,1)S(1)} %get-tuple-element.38), channel_id=1, source_target_pairs={{0,2},{1,9},{2,4},{3,11},{4,6},{5,13},{6,0},{7,15},{8,10},{9,17},{... | collective-permute-start | bytes 405512 | tf_op jit(solution)/shard_map/ppermute | solution.py:29
  79.6 2.0 %collective-permute-start.26 = (s16[528,128]{1,0:T(8,128)(2,1)S(1)}, s16[528,128]{1,0:T(8,128)(2,1)S(1)}, u32[]{:S(2)}, u32[]{:S(2)}) collective-permute-start(s16[528,128]{1,0:T(8,128)(2,1)S(1)} %get-tuple-element.39), channel_id=1, source_target_pairs={{0,4},{1,17},{2,6},{3,19},{4,0},{5,21},{6,2},{7,23},{8,12},{9,25},... | collective-permute-start | bytes 405512 | tf_op jit(solution)/shard_map/ppermute | solution.py:29
  81.6 1.3 %collective-permute-start.27 = (s16[528,128]{1,0:T(8,128)(2,1)S(1)}, s16[528,128]{1,0:T(8,128)(2,1)S(1)}, u32[]{:S(2)}, u32[]{:S(2)}) collective-permute-start(s16[528,128]{1,0:T(8,128)(2,1)S(1)} %get-tuple-element.40), channel_id=1, source_target_pairs={{0,6},{1,25},{2,0},{3,27},{4,2},{5,29},{6,4},{7,31},{8,14},{9,1},{... | collective-permute-start | bytes 405512 | tf_op jit(solution)/shard_map/ppermute | solution.py:29
  82.9 1.5 %collective-permute-done.25.refs_0_ = s16[528,128]{1,0:T(8,128)(2,1)S(1)} collective-permute-done((s16[528,128]{1,0:T(8,128)(2,1)S(1)}, s16[528,128]{1,0:T(8,128)(2,1)S(1)}, u32[]{:S(2)}, u32[]{:S(2)}) %collective-permute-start.25) | collective-permute-done | bytes 135200 | tf_op jit(solution)/shard_map/ppermute | solution.py:29
  84.4 1.7 %collective-permute-done.26.refs_1_ = s16[528,128]{1,0:T(8,128)(2,1)S(1)} collective-permute-done((s16[528,128]{1,0:T(8,128)(2,1)S(1)}, s16[528,128]{1,0:T(8,128)(2,1)S(1)}, u32[]{:S(2)}, u32[]{:S(2)}) %collective-permute-start.26) | collective-permute-done | bytes 135200 | tf_op jit(solution)/shard_map/ppermute | solution.py:29
  87.3 11.5 %all_to_all.11.arrived_ref = bf16[8,64,128]{2,1,0:T(8,128)(2,1)S(1)} all-to-all(bf16[8,64,128]{2,1,0:T(8,128)(2,1)S(1)} %bitcast.17), channel_id=1, replica_groups=mesh['expert'=8,'tp_0'=4,'tp_1'=4,'tp_2'=2] {'expert'}, dimensions={0} | all-to-all | bytes 262144 | tf_op jit(solution)/shard_map/all_to_all | solution.py:289
  98.8 1.3 %shard_map.90 = bf16[128,128]{1,0:T(8,128)(2,1)} custom-call(s32[2,128]{1,0:T(2,128)S(1)} %bitcast.23, s32[1,128]{1,0:T(1,128)S(1)} %bitcast.25, f32[2,128]{1,0:T(2,128)S(1)} %bitcast.26, bf16[8,64,128]{2,1,0:T(8,128)(2,1)S(1)} %all_to_all.11.arrived_ref), custom_call_target="tpu_custom_call" | custom-call | tf_op jit(solution)/shard_map/pallas_call | solution.py:290
  (49 shorter events, 7.6 us)
Async XLA Ops:
  19.8 5.6 %collective-permute-start = (bf16[2,256,128]{2,1,0:T(8,128)(2,1)S(1)}, bf16[2,256,128]{2,1,0:T(8,128)(2,1)S(1)}, u32[]{:S(2)}, u32[]{:S(2)}) collective-permute-start(bf16[2,256,128]{2,1,0:T(8,128)(2,1)S(1)} %bitcast.18), channel_id=1, source_target_pairs={{0,8},{1,3},{2,10},{3,5},{4,12},{5,7},{6,14},{7,1},{8,16},{9,11},{... | collective-permute-start | bytes 393224 | tf_op jit(solution)/shard_map/ppermute | solution.py:29
  21.2 6.6 %collective-permute-start.1 = (bf16[2,256,128]{2,1,0:T(8,128)(2,1)S(1)}, bf16[2,256,128]{2,1,0:T(8,128)(2,1)S(1)}, u32[]{:S(2)}, u32[]{:S(2)}) collective-permute-start(bf16[2,256,128]{2,1,0:T(8,128)(2,1)S(1)} %bitcast.19), channel_id=1, source_target_pairs={{0,16},{1,5},{2,18},{3,7},{4,20},{5,1},{6,22},{7,3},{8,24},{9,13},... | collective-permute-start | bytes 393224 | tf_op jit(solution)/shard_map/ppermute | solution.py:29
  22.4 6.4 %collective-permute-start.2 = (bf16[2,256,128]{2,1,0:T(8,128)(2,1)S(1)}, bf16[2,256,128]{2,1,0:T(8,128)(2,1)S(1)}, u32[]{:S(2)}, u32[]{:S(2)}) collective-permute-start(bf16[2,256,128]{2,1,0:T(8,128)(2,1)S(1)} %bitcast.20), channel_id=1, source_target_pairs={{0,24},{1,7},{2,26},{3,1},{4,28},{5,3},{6,30},{7,5},{8,0},{9,15},{... | collective-permute-start | bytes 393224 | tf_op jit(solution)/shard_map/ppermute | solution.py:29
  25.3 22.4 %copy-start.2 = (bf16[1,448,4096]{2,1,0:T(8,128)(2,1)S(1)}, bf16[1,448,4096]{2,1,0:T(8,128)(2,1)}, u32[]{:S(2)}) copy-start(bf16[1,448,4096]{2,1,0:T(8,128)(2,1)} %param.15) | copy-start | bytes 11010052
  28.8 7.7 %collective-permute-start.14 = (bf16[4,256,128]{2,1,0:T(8,128)(2,1)S(1)}, bf16[4,256,128]{2,1,0:T(8,128)(2,1)S(1)}, u32[]{:S(2)}, u32[]{:S(2)}) collective-permute-start(bf16[4,256,128]{2,1,0:T(8,128)(2,1)S(1)} %get-tuple-element.30.refs_0_), channel_id=1, source_target_pairs={{0,2},{1,9},{2,4},{3,11},{4,6},{5,13},{6,0},{7,15},{8,10},{9,17},{... | collective-permute-start | bytes 786440 | tf_op jit(solution)/shard_map/ppermute | solution.py:29
  30.4 10.2 %collective-permute-start.15 = (bf16[4,256,128]{2,1,0:T(8,128)(2,1)S(1)}, bf16[4,256,128]{2,1,0:T(8,128)(2,1)S(1)}, u32[]{:S(2)}, u32[]{:S(2)}) collective-permute-start(bf16[4,256,128]{2,1,0:T(8,128)(2,1)S(1)} %get-tuple-element.30.refs_0_), channel_id=1, source_target_pairs={{0,4},{1,17},{2,6},{3,19},{4,0},{5,21},{6,2},{7,23},{8,12},{9,25},... | collective-permute-start | bytes 786440 | tf_op jit(solution)/shard_map/ppermute | solution.py:29
  33.3 7.3 %collective-permute-start.16 = (bf16[4,256,128]{2,1,0:T(8,128)(2,1)S(1)}, bf16[4,256,128]{2,1,0:T(8,128)(2,1)S(1)}, u32[]{:S(2)}, u32[]{:S(2)}) collective-permute-start(bf16[4,256,128]{2,1,0:T(8,128)(2,1)S(1)} %get-tuple-element.30.refs_0_), channel_id=1, source_target_pairs={{0,6},{1,25},{2,0},{3,27},{4,2},{5,29},{6,4},{7,31},{8,14},{9,1},{... | collective-permute-start | bytes 786440 | tf_op jit(solution)/shard_map/ppermute | solution.py:29
  34.7 5.9 %collective-permute-start.17 = (bf16[4,256,128]{2,1,0:T(8,128)(2,1)S(1)}, bf16[4,256,128]{2,1,0:T(8,128)(2,1)S(1)}, u32[]{:S(2)}, u32[]{:S(2)}) collective-permute-start(bf16[4,256,128]{2,1,0:T(8,128)(2,1)S(1)} %get-tuple-element.30.refs_0_), channel_id=1, source_target_pairs={{0,1},{1,0},{2,3},{3,2},{4,5},{5,4},{6,7},{7,6},{8,9},{9,8},{10,11... | collective-permute-start | bytes 786440 | tf_op jit(solution)/shard_map/ppermute | solution.py:29
  34.7 8.6 %collective-permute-start.3 = (bf16[4,256,128]{2,1,0:T(8,128)(2,1)S(1)}, bf16[4,256,128]{2,1,0:T(8,128)(2,1)S(1)}, u32[]{:S(2)}, u32[]{:S(2)}) collective-permute-start(bf16[4,256,128]{2,1,0:T(8,128)(2,1)S(1)} %get-tuple-element.23.refs_0_), channel_id=1, source_target_pairs={{0,2},{1,9},{2,4},{3,11},{4,6},{5,13},{6,0},{7,15},{8,10},{9,17},{... | collective-permute-start | bytes 786440 | tf_op jit(solution)/shard_map/ppermute | solution.py:29
  36.4 9.7 %collective-permute-start.4 = (bf16[4,256,128]{2,1,0:T(8,128)(2,1)S(1)}, bf16[4,256,128]{2,1,0:T(8,128)(2,1)S(1)}, u32[]{:S(2)}, u32[]{:S(2)}) collective-permute-start(bf16[4,256,128]{2,1,0:T(8,128)(2,1)S(1)} %get-tuple-element.23.refs_0_), channel_id=1, source_target_pairs={{0,4},{1,17},{2,6},{3,19},{4,0},{5,21},{6,2},{7,23},{8,12},{9,25},... | collective-permute-start | bytes 786440 | tf_op jit(solution)/shard_map/ppermute | solution.py:29
  40.6 6.4 %collective-permute-start.5 = (bf16[4,256,128]{2,1,0:T(8,128)(2,1)S(1)}, bf16[4,256,128]{2,1,0:T(8,128)(2,1)S(1)}, u32[]{:S(2)}, u32[]{:S(2)}) collective-permute-start(bf16[4,256,128]{2,1,0:T(8,128)(2,1)S(1)} %get-tuple-element.23.refs_0_), channel_id=1, source_target_pairs={{0,6},{1,25},{2,0},{3,27},{4,2},{5,29},{6,4},{7,31},{8,14},{9,1},{... | collective-permute-start | bytes 786440 | tf_op jit(solution)/shard_map/ppermute | solution.py:29
  40.6 6.4 %collective-permute-start.18 = (bf16[4,256,128]{2,1,0:T(8,128)(2,1)S(1)}, bf16[4,256,128]{2,1,0:T(8,128)(2,1)S(1)}, u32[]{:S(2)}, u32[]{:S(2)}) collective-permute-start(bf16[4,256,128]{2,1,0:T(8,128)(2,1)S(1)} %collective-permute-done.14.refs_1_), channel_id=1, source_target_pairs={{0,1},{1,0},{2,3},{3,2},{4,5},{5,4},{6,7},{7,6},{8,9},{9,8},{10,11... | collective-permute-start | bytes 786440 | tf_op jit(solution)/shard_map/ppermute | solution.py:29
  40.6 6.9 %collective-permute-start.19 = (bf16[4,256,128]{2,1,0:T(8,128)(2,1)S(1)}, bf16[4,256,128]{2,1,0:T(8,128)(2,1)S(1)}, u32[]{:S(2)}, u32[]{:S(2)}) collective-permute-start(bf16[4,256,128]{2,1,0:T(8,128)(2,1)S(1)} %collective-permute-done.15.refs_2_), channel_id=1, source_target_pairs={{0,1},{1,0},{2,3},{3,2},{4,5},{5,4},{6,7},{7,6},{8,9},{9,8},{10,11... | collective-permute-start | bytes 786440 | tf_op jit(solution)/shard_map/ppermute | solution.py:29
  43.3 4.5 %collective-permute-start.20 = (bf16[4,256,128]{2,1,0:T(8,128)(2,1)S(1)}, bf16[4,256,128]{2,1,0:T(8,128)(2,1)S(1)}, u32[]{:S(2)}, u32[]{:S(2)}) collective-permute-start(bf16[4,256,128]{2,1,0:T(8,128)(2,1)S(1)} %collective-permute-done.16.refs_3_), channel_id=1, source_target_pairs={{0,1},{1,0},{2,3},{3,2},{4,5},{5,4},{6,7},{7,6},{8,9},{9,8},{10,11... | collective-permute-start | bytes 786440 | tf_op jit(solution)/shard_map/ppermute | solution.py:29
  46.1 7.2 %collective-permute-start.6 = (bf16[4,256,128]{2,1,0:T(8,128)(2,1)S(1)}, bf16[4,256,128]{2,1,0:T(8,128)(2,1)S(1)}, u32[]{:S(2)}, u32[]{:S(2)}) collective-permute-start(bf16[4,256,128]{2,1,0:T(8,128)(2,1)S(1)} %get-tuple-element.23.refs_0_), channel_id=1, source_target_pairs={{0,1},{1,0},{2,3},{3,2},{4,5},{5,4},{6,7},{7,6},{8,9},{9,8},{10,11... | collective-permute-start | bytes 786440 | tf_op jit(solution)/shard_map/ppermute | solution.py:29
  46.9 6.4 %collective-permute-start.7 = (bf16[4,256,128]{2,1,0:T(8,128)(2,1)S(1)}, bf16[4,256,128]{2,1,0:T(8,128)(2,1)S(1)}, u32[]{:S(2)}, u32[]{:S(2)}) collective-permute-start(bf16[4,256,128]{2,1,0:T(8,128)(2,1)S(1)} %collective-permute-done.3.refs_1_), channel_id=1, source_target_pairs={{0,1},{1,0},{2,3},{3,2},{4,5},{5,4},{6,7},{7,6},{8,9},{9,8},{10,11... | collective-permute-start | bytes 786440 | tf_op jit(solution)/shard_map/ppermute | solution.py:29
  47.0 6.4 %collective-permute-start.8 = (bf16[4,256,128]{2,1,0:T(8,128)(2,1)S(1)}, bf16[4,256,128]{2,1,0:T(8,128)(2,1)S(1)}, u32[]{:S(2)}, u32[]{:S(2)}) collective-permute-start(bf16[4,256,128]{2,1,0:T(8,128)(2,1)S(1)} %collective-permute-done.4.refs_2_), channel_id=1, source_target_pairs={{0,1},{1,0},{2,3},{3,2},{4,5},{5,4},{6,7},{7,6},{8,9},{9,8},{10,11... | collective-permute-start | bytes 786440 | tf_op jit(solution)/shard_map/ppermute | solution.py:29
  47.5 5.9 %collective-permute-start.9 = (bf16[4,256,128]{2,1,0:T(8,128)(2,1)S(1)}, bf16[4,256,128]{2,1,0:T(8,128)(2,1)S(1)}, u32[]{:S(2)}, u32[]{:S(2)}) collective-permute-start(bf16[4,256,128]{2,1,0:T(8,128)(2,1)S(1)} %collective-permute-done.5.refs_3_), channel_id=1, source_target_pairs={{0,1},{1,0},{2,3},{3,2},{4,5},{5,4},{6,7},{7,6},{8,9},{9,8},{10,11... | collective-permute-start | bytes 786440 | tf_op jit(solution)/shard_map/ppermute | solution.py:29
  53.0 6.0 %collective-permute-start.21 = (f32[4,4,256,128]{3,2,1,0:T(8,128)S(1)}, f32[4,4,256,128]{3,2,1,0:T(8,128)S(1)}, u32[]{:S(2)}, u32[]{:S(2)}) collective-permute-start(f32[4,4,256,128]{3,2,1,0:T(8,128)S(1)} %get-tuple-element.32), channel_id=1, source_target_pairs={{0,1},{1,0},{2,3},{3,2},{4,5},{5,4},{6,7},{7,6},{8,9},{9,8},{10,11... | collective-permute-start | bytes 6291464 | tf_op jit(solution)/shard_map/ppermute | solution.py:29
  58.6 5.8 %collective-permute-start.10 = (f32[4,4,256,128]{3,2,1,0:T(8,128)S(1)}, f32[4,4,256,128]{3,2,1,0:T(8,128)S(1)}, u32[]{:S(2)}, u32[]{:S(2)}) collective-permute-start(f32[4,4,256,128]{3,2,1,0:T(8,128)S(1)} %get-tuple-element.25), channel_id=1, source_target_pairs={{0,1},{1,0},{2,3},{3,2},{4,5},{5,4},{6,7},{7,6},{8,9},{9,8},{10,11... | collective-permute-start | bytes 6291464 | tf_op jit(solution)/shard_map/ppermute | solution.py:29
  59.5 8.5 %collective-permute-start.22 = (s16[1040,128]{1,0:T(8,128)(2,1)S(1)}, s16[1040,128]{1,0:T(8,128)(2,1)S(1)}, u32[]{:S(2)}, u32[]{:S(2)}) collective-permute-start(s16[1040,128]{1,0:T(8,128)(2,1)S(1)} %get-tuple-element.34), channel_id=1, source_target_pairs={{0,8},{1,3},{2,10},{3,5},{4,12},{5,7},{6,14},{7,1},{8,16},{9,11},{... | collective-permute-start | bytes 798728 | tf_op jit(solution)/shard_map/ppermute | solution.py:29
  60.6 8.0 %collective-permute-start.23 = (s16[1040,128]{1,0:T(8,128)(2,1)S(1)}, s16[1040,128]{1,0:T(8,128)(2,1)S(1)}, u32[]{:S(2)}, u32[]{:S(2)}) collective-permute-start(s16[1040,128]{1,0:T(8,128)(2,1)S(1)} %get-tuple-element.35), channel_id=1, source_target_pairs={{0,16},{1,5},{2,18},{3,7},{4,20},{5,1},{6,22},{7,3},{8,24},{9,13},... | collective-permute-start | bytes 798728 | tf_op jit(solution)/shard_map/ppermute | solution.py:29
  62.4 9.0 %collective-permute-start.24 = (s16[1040,128]{1,0:T(8,128)(2,1)S(1)}, s16[1040,128]{1,0:T(8,128)(2,1)S(1)}, u32[]{:S(2)}, u32[]{:S(2)}) collective-permute-start(s16[1040,128]{1,0:T(8,128)(2,1)S(1)} %get-tuple-element.36), channel_id=1, source_target_pairs={{0,24},{1,7},{2,26},{3,1},{4,28},{5,3},{6,30},{7,5},{8,0},{9,15},{... | collective-permute-start | bytes 798728 | tf_op jit(solution)/shard_map/ppermute | solution.py:29
  65.0 33.7 %copy-start.3 = (s32[128,2]{0,1:T(2,128)S(1)}, s32[128,2]{0,1:T(2,128)}, u32[]{:S(2)}) copy-start(s32[128,2]{0,1:T(2,128)} %param.11) | copy-start | bytes 3076
  65.0 33.7 %copy-start.4 = (s32[128]{0:T(128)S(1)}, s32[128]{0:T(128)}, u32[]{:S(2)}) copy-start(s32[128]{0:T(128)} %param.12) | copy-start | bytes 1540
  65.0 33.7 %copy-start.5 = (f32[128,2]{0,1:T(2,128)S(1)}, f32[128,2]{0,1:T(2,128)}, u32[]{:S(2)}) copy-start(f32[128,2]{0,1:T(2,128)} %param.10) | copy-start | bytes 3076
  65.0 6.7 %collective-permute-start.11 = (s16[1040,128]{1,0:T(8,128)(2,1)S(1)}, s16[1040,128]{1,0:T(8,128)(2,1)S(1)}, u32[]{:S(2)}, u32[]{:S(2)}) collective-permute-start(s16[1040,128]{1,0:T(8,128)(2,1)S(1)} %get-tuple-element.27), channel_id=1, source_target_pairs={{0,8},{1,3},{2,10},{3,5},{4,12},{5,7},{6,14},{7,1},{8,16},{9,11},{... | collective-permute-start | bytes 798728 | tf_op jit(solution)/shard_map/ppermute | solution.py:29
  65.1 9.2 %collective-permute-start.12 = (s16[1040,128]{1,0:T(8,128)(2,1)S(1)}, s16[1040,128]{1,0:T(8,128)(2,1)S(1)}, u32[]{:S(2)}, u32[]{:S(2)}) collective-permute-start(s16[1040,128]{1,0:T(8,128)(2,1)S(1)} %get-tuple-element.28), channel_id=1, source_target_pairs={{0,16},{1,5},{2,18},{3,7},{4,20},{5,1},{6,22},{7,3},{8,24},{9,13},... | collective-permute-start | bytes 798728 | tf_op jit(solution)/shard_map/ppermute | solution.py:29
  68.0 9.1 %collective-permute-start.13 = (s16[1040,128]{1,0:T(8,128)(2,1)S(1)}, s16[1040,128]{1,0:T(8,128)(2,1)S(1)}, u32[]{:S(2)}, u32[]{:S(2)}) collective-permute-start(s16[1040,128]{1,0:T(8,128)(2,1)S(1)} %get-tuple-element.29), channel_id=1, source_target_pairs={{0,24},{1,7},{2,26},{3,1},{4,28},{5,3},{6,30},{7,5},{8,0},{9,15},{... | collective-permute-start | bytes 798728 | tf_op jit(solution)/shard_map/ppermute | solution.py:29
  78.1 6.3 %collective-permute-start.25 = (s16[528,128]{1,0:T(8,128)(2,1)S(1)}, s16[528,128]{1,0:T(8,128)(2,1)S(1)}, u32[]{:S(2)}, u32[]{:S(2)}) collective-permute-start(s16[528,128]{1,0:T(8,128)(2,1)S(1)} %get-tuple-element.38), channel_id=1, source_target_pairs={{0,2},{1,9},{2,4},{3,11},{4,6},{5,13},{6,0},{7,15},{8,10},{9,17},{... | collective-permute-start | bytes 405512 | tf_op jit(solution)/shard_map/ppermute | solution.py:29
  79.6 6.5 %collective-permute-start.26 = (s16[528,128]{1,0:T(8,128)(2,1)S(1)}, s16[528,128]{1,0:T(8,128)(2,1)S(1)}, u32[]{:S(2)}, u32[]{:S(2)}) collective-permute-start(s16[528,128]{1,0:T(8,128)(2,1)S(1)} %get-tuple-element.39), channel_id=1, source_target_pairs={{0,4},{1,17},{2,6},{3,19},{4,0},{5,21},{6,2},{7,23},{8,12},{9,25},... | collective-permute-start | bytes 405512 | tf_op jit(solution)/shard_map/ppermute | solution.py:29
  81.6 5.1 %collective-permute-start.27 = (s16[528,128]{1,0:T(8,128)(2,1)S(1)}, s16[528,128]{1,0:T(8,128)(2,1)S(1)}, u32[]{:S(2)}, u32[]{:S(2)}) collective-permute-start(s16[528,128]{1,0:T(8,128)(2,1)S(1)} %get-tuple-element.40), channel_id=1, source_target_pairs={{0,6},{1,25},{2,0},{3,27},{4,2},{5,29},{6,4},{7,31},{8,14},{9,1},{... | collective-permute-start | bytes 405512 | tf_op jit(solution)/shard_map/ppermute | solution.py:29
  (2 other events, 44.9 us)

commit v4 on v3

--- a/solution.py
+++ b/solution.py
@@ -29,9 +29,9 @@
     return lax.ppermute(array, TP, pairs)
 
 
-def along(array, stage, step):
+def along(array, stage, step, other=0):
     def target(x, y, core):
-        return (x + step, y, core) if core == stage else (x, y + step, core)
+        return (x + step, y, core) if core ^ other == stage else (x, y + step, core)
 
     return moved(array, target)
 
@@ -84,7 +84,7 @@
     out_ref[...] = total.astype(BF16)
 
 
-def expert_kernel(n, where_ref, *refs):
+def expert_kernel(n, crossed, where_ref, *refs):
     own, partner = refs[:n], refs[n : 2 * n]
     gain_ref, gate_ref, up_ref, down_ref, keep_ref, send_ref, normed_ref = refs[2 * n :]
     x, y, core = where_ref[0], where_ref[1], where_ref[2]
@@ -117,9 +117,19 @@
             part = down_ref[:, pl.ds(pl.multiple_of(q * 2 * width, 2 * width), 2 * width)]
             both = jnp.dot(hidden, part, preferred_element_type=F32)
             low, high = both[:, :width], both[:, width:]
-            one, two = jnp.where(core == 0, dx, dy), jnp.where(core == 0, dy, dx)
-            keep_ref[one, two] = jnp.where(core == 0, low, high)
-            send_ref[two, one] = jnp.where(core == 0, high, low)
+            if (dx == crossed) == (dy == crossed):
+                one, two = jnp.where(core == 0, dx, dy), jnp.where(core == 0, dy, dx)
+                kept, sent = (high, low) if dx == crossed else (low, high)
+                keep_ref[one, two] = jnp.where(core == 0, kept, sent)
+                send_ref[two, one] = jnp.where(core == 0, sent, kept)
+                continue
+            keeper = 1 if dx == crossed else 0
+            for ref, condition in ((keep_ref, core == keeper), (send_ref, core != keeper)):
+
+                @pl.when(condition)
+                def _(ref=ref, dx=dx, dy=dy, low=low, high=high):
+                    ref[dx, dy] = low
+                    ref[dy, dx] = high
 
 
 def stack_kernel(skipped, *refs):
@@ -143,14 +153,14 @@
     )(*after, *pieces)
 
 
-def experts_of(where, own, partner, gains, gate, up, down):
+def experts_of(crossed, where, own, partner, gains, gate, up, down):
     n = len(own)
     _, rows, width = own[0].shape
     model = gate.shape[1]
     vmem = pl.BlockSpec(memory_space=pltpu.VMEM)
     out = jax.ShapeDtypeStruct((n, n, rows, width), F32)
     return pl.pallas_call(
-        functools.partial(expert_kernel, n),
+        functools.partial(expert_kernel, n, crossed),
         out_shape=(out, out),
         in_specs=[pl.BlockSpec(memory_space=pltpu.SMEM)] + [vmem] * (2 * n + 4),
         out_specs=(vmem, vmem),
@@ -233,14 +243,19 @@
     return jax.ShapeDtypeStruct((blocks * rows + SPARE, width), jnp.int16)
 
 
-def started(keep, send):
+def started(crossed, keep, send):
     n, _, rows, width = keep.shape
+    got = swapped(send)
     own, *parts = pl.pallas_call(
         first_kernel,
         out_shape=[jax.ShapeDtypeStruct((n, rows, width), F32)] + [coded(n, rows, width)] * (n - 1),
         compiler_params=pltpu.CompilerParams(vmem_limit_bytes=8 * MIB),
-    )(keep, swapped(send))
-    return [own] + [along(part, 0, k + 1) for k, part in enumerate(parts)]
+    )(keep, got)
+    for step in range(1, n):
+        parts[step - 1] = along(parts[step - 1], 0, step, int(step == crossed))
+        if step == crossed:
+            parts[step - 1] = swapped(parts[step - 1])
+    return [own] + parts
 
 
 def finished(chunks):
@@ -281,10 +296,11 @@
     for stack in stacked((gains, where), first):
         owns.append([stack] + [along(stack, 1, k) for k in range(1, n)])
     chunks = []
-    for own in owns:
+    for chunk, own in enumerate(owns):
         partner = [swapped(a) for a in own]
-        keep, send = experts_of(where, own, partner, gains, *weights)
-        chunks.append(started(keep, send))
+        crossed = n // 2 if chunk % 2 else None
+        keep, send = experts_of(crossed, where, own, partner, gains, *weights)
+        chunks.append(started(crossed, keep, send))
     returning = finished(chunks).reshape(groups, seat_limit, width)
     arrived = lax.all_to_all(returning, "expert", split_axis=0, concat_axis=0, tiled=True)
     return pl.pallas_call(

time: 100 us -> 103 us (1.030)
  the two profiles are of different devices: /device:TPU:2 before, /device:TPU:14 now
where the time goes in v4:
time: 103 us; the launch traced here: 102 us
  waiting for transfers between devices  30 us (29%)
  blocking collectives  29 us (28%)
  starting transfers between devices  24.3 us (24%)
  Pallas kernels  18 us (17%)
    ppermute x29, waiting for transfers between devices, moved(): return lax.ppermute(array, TP, pairs)  30 us
    ppermute x29, starting transfers between devices, moved(): return lax.ppermute(array, TP, pairs)  24.3 us
    all_to_all x1, blocking collectives, local(): lax.all_to_all(sent, 'expert', split_axis=0, concat_axis=0, tiled=True)  17.6 us
    pallas_call x2, Pallas kernels, experts_of(): pl.pallas_call(functools.partial(expert_kernel, n, crossed), out_shape=(o...  11.9 us
    all_to_all x1, blocking collectives, local(): lax.all_to_all(returning, 'expert', split_axis=0, concat_axis=0, tiled=True)  11.5 us
    pallas_call x1, Pallas kernels, local(): pl.pallas_call(functools.partial(dispatch_kernel, seat_limit, groups), ou...  2.21 us
  transfers between devices with their start and end apart: 29, of which 13 were waited for; matrix products, arithmetic and copies ran while one was open for 1% of the time, Pallas kernels for 13%

profile of v4, /device:TPU:14, one launch (start us, length us, event | category | flops | bytes accessed | tf_op | source)
XLA Modules:
  0.0 102.3 jit_solution(7754350766828091919)
XLA Ops:
  0.0 2.2 %shard_map.82 = bf16[8,64,128]{2,1,0:T(8,128)(2,1)} custom-call(s32[2,128]{1,0:T(2,128)} %bitcast.22, s32[1,128]{1,0:T(1,128)} %bitcast.24, bf16[128,128]{1,0:T(8,128)(2,1)} %tokens_ref.1), custom_call_target="tpu_custom_call" | custom-call | tf_op jit(solution)/shard_map/pallas_call | solution.py:285
  2.2 17.6 %all_to_all.10 = bf16[8,64,128]{2,1,0:T(8,128)(2,1)S(1)} all-to-all(bf16[8,64,128]{2,1,0:T(8,128)(2,1)} %shard_map.82), channel_id=1, replica_groups=mesh['expert'=8,'tp_0'=4,'tp_1'=4,'tp_2'=2] {'expert'}, dimensions={0} | all-to-all | bytes 262144 | tf_op jit(solution)/shard_map/all_to_all | solution.py:290
  20.2 2.4 %collective-permute-start.1 = (bf16[2,256,128]{2,1,0:T(8,128)(2,1)S(1)}, bf16[2,256,128]{2,1,0:T(8,128)(2,1)S(1)}, u32[]{:S(2)}, u32[]{:S(2)}) collective-permute-start(bf16[2,256,128]{2,1,0:T(8,128)(2,1)S(1)} %bitcast.19), channel_id=1, source_target_pairs={{0,16},{1,5},{2,18},{3,7},{4,20},{5,1},{6,22},{7,3},{8,24},{9,13},... | collective-permute-start | bytes 393224 | tf_op jit(solution)/shard_map/ppermute | solution.py:29
  22.7 0.7 reshape.13.refs_0_.refs_8_
  23.5 1.3 %collective-permute-done.refs_3_ = bf16[2,256,128]{2,1,0:T(8,128)(2,1)S(1)} collective-permute-done((bf16[2,256,128]{2,1,0:T(8,128)(2,1)S(1)}, bf16[2,256,128]{2,1,0:T(8,128)(2,1)S(1)}, u32[]{:S(2)}, u32[]{:S(2)}) %collective-permute-start) | collective-permute-done | bytes 131104 | tf_op jit(solution)/shard_map/ppermute | solution.py:29
  24.7 2.0 %collective-permute-done.1.refs_4_ = bf16[2,256,128]{2,1,0:T(8,128)(2,1)S(1)} collective-permute-done((bf16[2,256,128]{2,1,0:T(8,128)(2,1)S(1)}, bf16[2,256,128]{2,1,0:T(8,128)(2,1)S(1)}, u32[]{:S(2)}, u32[]{:S(2)}) %collective-permute-start.1) | collective-permute-done | bytes 131104 | tf_op jit(solution)/shard_map/ppermute | solution.py:29
  26.7 2.1 %collective-permute-done.2.refs_5_ = bf16[2,256,128]{2,1,0:T(8,128)(2,1)S(1)} collective-permute-done((bf16[2,256,128]{2,1,0:T(8,128)(2,1)S(1)}, bf16[2,256,128]{2,1,0:T(8,128)(2,1)S(1)}, u32[]{:S(2)}, u32[]{:S(2)}) %collective-permute-start.2) | collective-permute-done | bytes 131104 | tf_op jit(solution)/shard_map/ppermute | solution.py:29
  28.9 1.7 %collective-permute-start.14 = (bf16[4,256,128]{2,1,0:T(8,128)(2,1)S(1)}, bf16[4,256,128]{2,1,0:T(8,128)(2,1)S(1)}, u32[]{:S(2)}, u32[]{:S(2)}) collective-permute-start(bf16[4,256,128]{2,1,0:T(8,128)(2,1)S(1)} %get-tuple-element.30.refs_0_), channel_id=1, source_target_pairs={{0,2},{1,9},{2,4},{3,11},{4,6},{5,13},{6,0},{7,15},{8,10},{9,17},{... | collective-permute-start | bytes 786440 | tf_op jit(solution)/shard_map/ppermute | solution.py:29
  30.5 0.9 collective-permute-start.15
  31.5 2.4 %collective-permute-start.16 = (bf16[4,256,128]{2,1,0:T(8,128)(2,1)S(1)}, bf16[4,256,128]{2,1,0:T(8,128)(2,1)S(1)}, u32[]{:S(2)}, u32[]{:S(2)}) collective-permute-start(bf16[4,256,128]{2,1,0:T(8,128)(2,1)S(1)} %get-tuple-element.30.refs_0_), channel_id=1, source_target_pairs={{0,6},{1,25},{2,0},{3,27},{4,2},{5,29},{6,4},{7,31},{8,14},{9,1},{... | collective-permute-start | bytes 786440 | tf_op jit(solution)/shard_map/ppermute | solution.py:29
  33.9 1.4 %collective-permute-done.14.refs_1_ = bf16[4,256,128]{2,1,0:T(8,128)(2,1)S(1)} collective-permute-done((bf16[4,256,128]{2,1,0:T(8,128)(2,1)S(1)}, bf16[4,256,128]{2,1,0:T(8,128)(2,1)S(1)}, u32[]{:S(2)}, u32[]{:S(2)}) %collective-permute-start.14) | collective-permute-done | bytes 262176 | tf_op jit(solution)/shard_map/ppermute | solution.py:29
  35.3 2.3 %collective-permute-start.4 = (bf16[4,256,128]{2,1,0:T(8,128)(2,1)S(1)}, bf16[4,256,128]{2,1,0:T(8,128)(2,1)S(1)}, u32[]{:S(2)}, u32[]{:S(2)}) collective-permute-start(bf16[4,256,128]{2,1,0:T(8,128)(2,1)S(1)} %get-tuple-element.23.refs_0_), channel_id=1, source_target_pairs={{0,4},{1,17},{2,6},{3,19},{4,0},{5,21},{6,2},{7,23},{8,12},{9,25},... | collective-permute-start | bytes 786440 | tf_op jit(solution)/shard_map/ppermute | solution.py:29
  37.6 0.9 collective-permute-done.15.refs_2_
  38.5 2.6 %collective-permute-start.5 = (bf16[4,256,128]{2,1,0:T(8,128)(2,1)S(1)}, bf16[4,256,128]{2,1,0:T(8,128)(2,1)S(1)}, u32[]{:S(2)}, u32[]{:S(2)}) collective-permute-start(bf16[4,256,128]{2,1,0:T(8,128)(2,1)S(1)} %get-tuple-element.23.refs_0_), channel_id=1, source_target_pairs={{0,6},{1,25},{2,0},{3,27},{4,2},{5,29},{6,4},{7,31},{8,14},{9,1},{... | collective-permute-start | bytes 786440 | tf_op jit(solution)/shard_map/ppermute | solution.py:29
  41.8 2.4 %collective-permute-done.4.refs_2_ = bf16[4,256,128]{2,1,0:T(8,128)(2,1)S(1)} collective-permute-done((bf16[4,256,128]{2,1,0:T(8,128)(2,1)S(1)}, bf16[4,256,128]{2,1,0:T(8,128)(2,1)S(1)}, u32[]{:S(2)}, u32[]{:S(2)}) %collective-permute-start.4) | collective-permute-done | bytes 262176 | tf_op jit(solution)/shard_map/ppermute | solution.py:29
  44.2 2.7 %collective-permute-done.5.refs_3_ = bf16[4,256,128]{2,1,0:T(8,128)(2,1)S(1)} collective-permute-done((bf16[4,256,128]{2,1,0:T(8,128)(2,1)S(1)}, bf16[4,256,128]{2,1,0:T(8,128)(2,1)S(1)}, u32[]{:S(2)}, u32[]{:S(2)}) %collective-permute-start.5) | collective-permute-done | bytes 262176 | tf_op jit(solution)/shard_map/ppermute | solution.py:29
  47.7 6.6 %shard_map.86 = (f32[4,4,256,128]{3,2,1,0:T(8,128)S(1)}, f32[4,4,256,128]{3,2,1,0:T(8,128)S(1)}) custom-call(s32[3]{0:T(128)S(1)} %pad_add_fusion.refs_1_.where_ref, bf16[4,256,128]{2,1,0:T(8,128)(2,1)S(1)} %get-tuple-element.30.refs_0_, bf16[4,256,128]{2,1,0:T(8,128)(2,1)S(1)} %collective-permute-done.14.refs_1_, ...), custom_call_target="tpu_custom_call" | custom-call | flops 3000000000 | tf_op jit(solution)/shard_map/pallas_call | solution.py:162
  54.7 5.3 %shard_map.84 = (f32[4,4,256,128]{3,2,1,0:T(8,128)S(1)}, f32[4,4,256,128]{3,2,1,0:T(8,128)S(1)}) custom-call(s32[3]{0:T(128)S(1)} %pad_add_fusion.refs_1_.where_ref, bf16[4,256,128]{2,1,0:T(8,128)(2,1)S(1)} %get-tuple-element.23.refs_0_, bf16[4,256,128]{2,1,0:T(8,128)(2,1)S(1)} %collective-permute-done.3.refs_1_, ...), custom_call_target="tpu_custom_call" | custom-call | flops 3000000000 | tf_op jit(solution)/shard_map/pallas_call | solution.py:162
  60.8 1.5 %collective-permute-start.23 = (s16[1040,128]{1,0:T(8,128)(2,1)S(1)}, s16[1040,128]{1,0:T(8,128)(2,1)S(1)}, u32[]{:S(2)}, u32[]{:S(2)}) collective-permute-start(s16[1040,128]{1,0:T(8,128)(2,1)S(1)} %get-tuple-element.35), channel_id=1, source_target_pairs={{0,4},{1,17},{2,6},{3,19},{4,0},{5,21},{6,2},{7,23},{8,12},{9,25},... | collective-permute-start | bytes 798728 | tf_op jit(solution)/shard_map/ppermute | solution.py:29
  62.9 1.4 %collective-permute-start.25 = (s16[1040,128]{1,0:T(8,128)(2,1)S(1)}, s16[1040,128]{1,0:T(8,128)(2,1)S(1)}, u32[]{:S(2)}, u32[]{:S(2)}) collective-permute-start(s16[1040,128]{1,0:T(8,128)(2,1)S(1)} %get-tuple-element.36), channel_id=1, source_target_pairs={{0,24},{1,7},{2,26},{3,1},{4,28},{5,3},{6,30},{7,5},{8,0},{9,15},{... | collective-permute-start | bytes 798728 | tf_op jit(solution)/shard_map/ppermute | solution.py:29
  64.9 1.9 %collective-permute-start.11 = (s16[1040,128]{1,0:T(8,128)(2,1)S(1)}, s16[1040,128]{1,0:T(8,128)(2,1)S(1)}, u32[]{:S(2)}, u32[]{:S(2)}) collective-permute-start(s16[1040,128]{1,0:T(8,128)(2,1)S(1)} %get-tuple-element.27), channel_id=1, source_target_pairs={{0,8},{1,3},{2,10},{3,5},{4,12},{5,7},{6,14},{7,1},{8,16},{9,11},{... | collective-permute-start | bytes 798728 | tf_op jit(solution)/shard_map/ppermute | solution.py:29
  67.3 4.5 %collective-permute-done.23 = s16[1040,128]{1,0:T(8,128)(2,1)S(1)} collective-permute-done((s16[1040,128]{1,0:T(8,128)(2,1)S(1)}, s16[1040,128]{1,0:T(8,128)(2,1)S(1)}, u32[]{:S(2)}, u32[]{:S(2)}) %collective-permute-start.23) | collective-permute-done | bytes 266272 | tf_op jit(solution)/shard_map/ppermute | solution.py:29
  71.9 2.8 %collective-permute-done.12.refs_2_ = s16[1040,128]{1,0:T(8,128)(2,1)S(1)} collective-permute-done((s16[1040,128]{1,0:T(8,128)(2,1)S(1)}, s16[1040,128]{1,0:T(8,128)(2,1)S(1)}, u32[]{:S(2)}, u32[]{:S(2)}) %collective-permute-start.12) | collective-permute-done | bytes 266272 | tf_op jit(solution)/shard_map/ppermute | solution.py:29
  74.7 4.7 %collective-permute-done.13.refs_3_ = s16[1040,128]{1,0:T(8,128)(2,1)S(1)} collective-permute-done((s16[1040,128]{1,0:T(8,128)(2,1)S(1)}, s16[1040,128]{1,0:T(8,128)(2,1)S(1)}, u32[]{:S(2)}, u32[]{:S(2)}) %collective-permute-start.13) | collective-permute-done | bytes 266272 | tf_op jit(solution)/shard_map/ppermute | solution.py:29
  79.4 1.0 shard_map.88
  81.0 1.8 %collective-permute-start.27 = (s16[528,128]{1,0:T(8,128)(2,1)S(1)}, s16[528,128]{1,0:T(8,128)(2,1)S(1)}, u32[]{:S(2)}, u32[]{:S(2)}) collective-permute-start(s16[528,128]{1,0:T(8,128)(2,1)S(1)} %get-tuple-element.39), channel_id=1, source_target_pairs={{0,4},{1,17},{2,6},{3,19},{4,0},{5,21},{6,2},{7,23},{8,12},{9,25},... | collective-permute-start | bytes 405512 | tf_op jit(solution)/shard_map/ppermute | solution.py:29
  82.8 0.9 collective-permute-start.28
  83.8 1.7 %collective-permute-done.26.refs_0_ = s16[528,128]{1,0:T(8,128)(2,1)S(1)} collective-permute-done((s16[528,128]{1,0:T(8,128)(2,1)S(1)}, s16[528,128]{1,0:T(8,128)(2,1)S(1)}, u32[]{:S(2)}, u32[]{:S(2)}) %collective-permute-start.26) | collective-permute-done | bytes 135200 | tf_op jit(solution)/shard_map/ppermute | solution.py:29
  85.5 2.1 %collective-permute-done.27.refs_1_ = s16[528,128]{1,0:T(8,128)(2,1)S(1)} collective-permute-done((s16[528,128]{1,0:T(8,128)(2,1)S(1)}, s16[528,128]{1,0:T(8,128)(2,1)S(1)}, u32[]{:S(2)}, u32[]{:S(2)}) %collective-permute-start.27) | collective-permute-done | bytes 135200 | tf_op jit(solution)/shard_map/ppermute | solution.py:29
  87.6 1.3 %collective-permute-done.28.refs_2_ = s16[528,128]{1,0:T(8,128)(2,1)S(1)} collective-permute-done((s16[528,128]{1,0:T(8,128)(2,1)S(1)}, s16[528,128]{1,0:T(8,128)(2,1)S(1)}, u32[]{:S(2)}, u32[]{:S(2)}) %collective-permute-start.28) | collective-permute-done | bytes 135200 | tf_op jit(solution)/shard_map/ppermute | solution.py:29
  89.5 11.5 %all_to_all.11.arrived_ref = bf16[8,64,128]{2,1,0:T(8,128)(2,1)S(1)} all-to-all(bf16[8,64,128]{2,1,0:T(8,128)(2,1)S(1)} %bitcast.17), channel_id=1, replica_groups=mesh['expert'=8,'tp_0'=4,'tp_1'=4,'tp_2'=2] {'expert'}, dimensions={0} | all-to-all | bytes 262144 | tf_op jit(solution)/shard_map/all_to_all | solution.py:305
  101.0 1.3 %shard_map.90 = bf16[128,128]{1,0:T(8,128)(2,1)} custom-call(s32[2,128]{1,0:T(2,128)S(1)} %bitcast.23, s32[1,128]{1,0:T(1,128)S(1)} %bitcast.25, f32[2,128]{1,0:T(2,128)S(1)} %bitcast.26, bf16[8,64,128]{2,1,0:T(8,128)(2,1)S(1)} %all_to_all.11.arrived_ref), custom_call_target="tpu_custom_call" | custom-call | tf_op jit(solution)/shard_map/pallas_call | solution.py:306
  (51 shorter events, 6.2 us)
Async XLA Ops:
  19.8 5.0 %collective-permute-start = (bf16[2,256,128]{2,1,0:T(8,128)(2,1)S(1)}, bf16[2,256,128]{2,1,0:T(8,128)(2,1)S(1)}, u32[]{:S(2)}, u32[]{:S(2)}) collective-permute-start(bf16[2,256,128]{2,1,0:T(8,128)(2,1)S(1)} %bitcast.18), channel_id=1, source_target_pairs={{0,8},{1,3},{2,10},{3,5},{4,12},{5,7},{6,14},{7,1},{8,16},{9,11},{... | collective-permute-start | bytes 393224 | tf_op jit(solution)/shard_map/ppermute | solution.py:29
  20.2 6.5 %collective-permute-start.1 = (bf16[2,256,128]{2,1,0:T(8,128)(2,1)S(1)}, bf16[2,256,128]{2,1,0:T(8,128)(2,1)S(1)}, u32[]{:S(2)}, u32[]{:S(2)}) collective-permute-start(bf16[2,256,128]{2,1,0:T(8,128)(2,1)S(1)} %bitcast.19), channel_id=1, source_target_pairs={{0,16},{1,5},{2,18},{3,7},{4,20},{5,1},{6,22},{7,3},{8,24},{9,13},... | collective-permute-start | bytes 393224 | tf_op jit(solution)/shard_map/ppermute | solution.py:29
  22.7 6.2 %collective-permute-start.2 = (bf16[2,256,128]{2,1,0:T(8,128)(2,1)S(1)}, bf16[2,256,128]{2,1,0:T(8,128)(2,1)S(1)}, u32[]{:S(2)}, u32[]{:S(2)}) collective-permute-start(bf16[2,256,128]{2,1,0:T(8,128)(2,1)S(1)} %bitcast.20), channel_id=1, source_target_pairs={{0,24},{1,7},{2,26},{3,1},{4,28},{5,3},{6,30},{7,5},{8,0},{9,15},{... | collective-permute-start | bytes 393224 | tf_op jit(solution)/shard_map/ppermute | solution.py:29
  28.9 6.4 %collective-permute-start.14 = (bf16[4,256,128]{2,1,0:T(8,128)(2,1)S(1)}, bf16[4,256,128]{2,1,0:T(8,128)(2,1)S(1)}, u32[]{:S(2)}, u32[]{:S(2)}) collective-permute-start(bf16[4,256,128]{2,1,0:T(8,128)(2,1)S(1)} %get-tuple-element.30.refs_0_), channel_id=1, source_target_pairs={{0,2},{1,9},{2,4},{3,11},{4,6},{5,13},{6,0},{7,15},{8,10},{9,17},{... | collective-permute-start | bytes 786440 | tf_op jit(solution)/shard_map/ppermute | solution.py:29
  30.5 8.0 %collective-permute-start.15 = (bf16[4,256,128]{2,1,0:T(8,128)(2,1)S(1)}, bf16[4,256,128]{2,1,0:T(8,128)(2,1)S(1)}, u32[]{:S(2)}, u32[]{:S(2)}) collective-permute-start(bf16[4,256,128]{2,1,0:T(8,128)(2,1)S(1)} %get-tuple-element.30.refs_0_), channel_id=1, source_target_pairs={{0,4},{1,17},{2,6},{3,19},{4,0},{5,21},{6,2},{7,23},{8,12},{9,25},... | collective-permute-start | bytes 786440 | tf_op jit(solution)/shard_map/ppermute | solution.py:29
  31.5 9.7 %collective-permute-start.16 = (bf16[4,256,128]{2,1,0:T(8,128)(2,1)S(1)}, bf16[4,256,128]{2,1,0:T(8,128)(2,1)S(1)}, u32[]{:S(2)}, u32[]{:S(2)}) collective-permute-start(bf16[4,256,128]{2,1,0:T(8,128)(2,1)S(1)} %get-tuple-element.30.refs_0_), channel_id=1, source_target_pairs={{0,6},{1,25},{2,0},{3,27},{4,2},{5,29},{6,4},{7,31},{8,14},{9,1},{... | collective-permute-start | bytes 786440 | tf_op jit(solution)/shard_map/ppermute | solution.py:29
  33.9 7.3 %collective-permute-start.17 = (bf16[4,256,128]{2,1,0:T(8,128)(2,1)S(1)}, bf16[4,256,128]{2,1,0:T(8,128)(2,1)S(1)}, u32[]{:S(2)}, u32[]{:S(2)}) collective-permute-start(bf16[4,256,128]{2,1,0:T(8,128)(2,1)S(1)} %get-tuple-element.30.refs_0_), channel_id=1, source_target_pairs={{0,1},{1,0},{2,3},{3,2},{4,5},{5,4},{6,7},{7,6},{8,9},{9,8},{10,11... | collective-permute-start | bytes 786440 | tf_op jit(solution)/shard_map/ppermute | solution.py:29
  33.9 7.8 %collective-permute-start.3 = (bf16[4,256,128]{2,1,0:T(8,128)(2,1)S(1)}, bf16[4,256,128]{2,1,0:T(8,128)(2,1)S(1)}, u32[]{:S(2)}, u32[]{:S(2)}) collective-permute-start(bf16[4,256,128]{2,1,0:T(8,128)(2,1)S(1)} %get-tuple-element.23.refs_0_), channel_id=1, source_target_pairs={{0,2},{1,9},{2,4},{3,11},{4,6},{5,13},{6,0},{7,15},{8,10},{9,17},{... | collective-permute-start | bytes 786440 | tf_op jit(solution)/shard_map/ppermute | solution.py:29
  35.3 8.8 %collective-permute-start.4 = (bf16[4,256,128]{2,1,0:T(8,128)(2,1)S(1)}, bf16[4,256,128]{2,1,0:T(8,128)(2,1)S(1)}, u32[]{:S(2)}, u32[]{:S(2)}) collective-permute-start(bf16[4,256,128]{2,1,0:T(8,128)(2,1)S(1)} %get-tuple-element.23.refs_0_), channel_id=1, source_target_pairs={{0,4},{1,17},{2,6},{3,19},{4,0},{5,21},{6,2},{7,23},{8,12},{9,25},... | collective-permute-start | bytes 786440 | tf_op jit(solution)/shard_map/ppermute | solution.py:29
  38.5 8.4 %collective-permute-start.5 = (bf16[4,256,128]{2,1,0:T(8,128)(2,1)S(1)}, bf16[4,256,128]{2,1,0:T(8,128)(2,1)S(1)}, u32[]{:S(2)}, u32[]{:S(2)}) collective-permute-start(bf16[4,256,128]{2,1,0:T(8,128)(2,1)S(1)} %get-tuple-element.23.refs_0_), channel_id=1, source_target_pairs={{0,6},{1,25},{2,0},{3,27},{4,2},{5,29},{6,4},{7,31},{8,14},{9,1},{... | collective-permute-start | bytes 786440 | tf_op jit(solution)/shard_map/ppermute | solution.py:29
  41.1 5.7 %collective-permute-start.18 = (bf16[4,256,128]{2,1,0:T(8,128)(2,1)S(1)}, bf16[4,256,128]{2,1,0:T(8,128)(2,1)S(1)}, u32[]{:S(2)}, u32[]{:S(2)}) collective-permute-start(bf16[4,256,128]{2,1,0:T(8,128)(2,1)S(1)} %collective-permute-done.14.refs_1_), channel_id=1, source_target_pairs={{0,1},{1,0},{2,3},{3,2},{4,5},{5,4},{6,7},{7,6},{8,9},{9,8},{10,11... | collective-permute-start | bytes 786440 | tf_op jit(solution)/shard_map/ppermute | solution.py:29
  41.2 6.2 %collective-permute-start.19 = (bf16[4,256,128]{2,1,0:T(8,128)(2,1)S(1)}, bf16[4,256,128]{2,1,0:T(8,128)(2,1)S(1)}, u32[]{:S(2)}, u32[]{:S(2)}) collective-permute-start(bf16[4,256,128]{2,1,0:T(8,128)(2,1)S(1)} %collective-permute-done.15.refs_2_), channel_id=1, source_target_pairs={{0,1},{1,0},{2,3},{3,2},{4,5},{5,4},{6,7},{7,6},{8,9},{9,8},{10,11... | collective-permute-start | bytes 786440 | tf_op jit(solution)/shard_map/ppermute | solution.py:29
  41.7 6.0 %collective-permute-start.20 = (bf16[4,256,128]{2,1,0:T(8,128)(2,1)S(1)}, bf16[4,256,128]{2,1,0:T(8,128)(2,1)S(1)}, u32[]{:S(2)}, u32[]{:S(2)}) collective-permute-start(bf16[4,256,128]{2,1,0:T(8,128)(2,1)S(1)} %collective-permute-done.16.refs_3_), channel_id=1, source_target_pairs={{0,1},{1,0},{2,3},{3,2},{4,5},{5,4},{6,7},{7,6},{8,9},{9,8},{10,11... | collective-permute-start | bytes 786440 | tf_op jit(solution)/shard_map/ppermute | solution.py:29
  44.2 10.5 %collective-permute-start.6 = (bf16[4,256,128]{2,1,0:T(8,128)(2,1)S(1)}, bf16[4,256,128]{2,1,0:T(8,128)(2,1)S(1)}, u32[]{:S(2)}, u32[]{:S(2)}) collective-permute-start(bf16[4,256,128]{2,1,0:T(8,128)(2,1)S(1)} %get-tuple-element.23.refs_0_), channel_id=1, source_target_pairs={{0,1},{1,0},{2,3},{3,2},{4,5},{5,4},{6,7},{7,6},{8,9},{9,8},{10,11... | collective-permute-start | bytes 786440 | tf_op jit(solution)/shard_map/ppermute | solution.py:29
  46.9 7.8 %collective-permute-start.7 = (bf16[4,256,128]{2,1,0:T(8,128)(2,1)S(1)}, bf16[4,256,128]{2,1,0:T(8,128)(2,1)S(1)}, u32[]{:S(2)}, u32[]{:S(2)}) collective-permute-start(bf16[4,256,128]{2,1,0:T(8,128)(2,1)S(1)} %collective-permute-done.3.refs_1_), channel_id=1, source_target_pairs={{0,1},{1,0},{2,3},{3,2},{4,5},{5,4},{6,7},{7,6},{8,9},{9,8},{10,11... | collective-permute-start | bytes 786440 | tf_op jit(solution)/shard_map/ppermute | solution.py:29
  46.9 7.8 %collective-permute-start.8 = (bf16[4,256,128]{2,1,0:T(8,128)(2,1)S(1)}, bf16[4,256,128]{2,1,0:T(8,128)(2,1)S(1)}, u32[]{:S(2)}, u32[]{:S(2)}) collective-permute-start(bf16[4,256,128]{2,1,0:T(8,128)(2,1)S(1)} %collective-permute-done.4.refs_2_), channel_id=1, source_target_pairs={{0,1},{1,0},{2,3},{3,2},{4,5},{5,4},{6,7},{7,6},{8,9},{9,8},{10,11... | collective-permute-start | bytes 786440 | tf_op jit(solution)/shard_map/ppermute | solution.py:29
  47.4 7.3 %collective-permute-start.9 = (bf16[4,256,128]{2,1,0:T(8,128)(2,1)S(1)}, bf16[4,256,128]{2,1,0:T(8,128)(2,1)S(1)}, u32[]{:S(2)}, u32[]{:S(2)}) collective-permute-start(bf16[4,256,128]{2,1,0:T(8,128)(2,1)S(1)} %collective-permute-done.5.refs_3_), channel_id=1, source_target_pairs={{0,1},{1,0},{2,3},{3,2},{4,5},{5,4},{6,7},{7,6},{8,9},{9,8},{10,11... | collective-permute-start | bytes 786440 | tf_op jit(solution)/shard_map/ppermute | solution.py:29
  54.3 6.0 %collective-permute-start.21 = (f32[4,4,256,128]{3,2,1,0:T(8,128)S(1)}, f32[4,4,256,128]{3,2,1,0:T(8,128)S(1)}, u32[]{:S(2)}, u32[]{:S(2)}) collective-permute-start(f32[4,4,256,128]{3,2,1,0:T(8,128)S(1)} %get-tuple-element.32), channel_id=1, source_target_pairs={{0,1},{1,0},{2,3},{3,2},{4,5},{5,4},{6,7},{7,6},{8,9},{9,8},{10,11... | collective-permute-start | bytes 6291464 | tf_op jit(solution)/shard_map/ppermute | solution.py:29
  59.9 4.4 %collective-permute-start.10 = (f32[4,4,256,128]{3,2,1,0:T(8,128)S(1)}, f32[4,4,256,128]{3,2,1,0:T(8,128)S(1)}, u32[]{:S(2)}, u32[]{:S(2)}) collective-permute-start(f32[4,4,256,128]{3,2,1,0:T(8,128)S(1)} %get-tuple-element.25), channel_id=1, source_target_pairs={{0,1},{1,0},{2,3},{3,2},{4,5},{5,4},{6,7},{7,6},{8,9},{9,8},{10,11... | collective-permute-start | bytes 6291464 | tf_op jit(solution)/shard_map/ppermute | solution.py:29
  60.8 11.0 %collective-permute-start.23 = (s16[1040,128]{1,0:T(8,128)(2,1)S(1)}, s16[1040,128]{1,0:T(8,128)(2,1)S(1)}, u32[]{:S(2)}, u32[]{:S(2)}) collective-permute-start(s16[1040,128]{1,0:T(8,128)(2,1)S(1)} %get-tuple-element.35), channel_id=1, source_target_pairs={{0,4},{1,17},{2,6},{3,19},{4,0},{5,21},{6,2},{7,23},{8,12},{9,25},... | collective-permute-start | bytes 798728 | tf_op jit(solution)/shard_map/ppermute | solution.py:29
  62.3 9.6 %collective-permute-start.22 = (s16[1040,128]{1,0:T(8,128)(2,1)S(1)}, s16[1040,128]{1,0:T(8,128)(2,1)S(1)}, u32[]{:S(2)}, u32[]{:S(2)}) collective-permute-start(s16[1040,128]{1,0:T(8,128)(2,1)S(1)} %get-tuple-element.34), channel_id=1, source_target_pairs={{0,8},{1,3},{2,10},{3,5},{4,12},{5,7},{6,14},{7,1},{8,16},{9,11},{... | collective-permute-start | bytes 798728 | tf_op jit(solution)/shard_map/ppermute | solution.py:29
  62.9 9.0 %collective-permute-start.25 = (s16[1040,128]{1,0:T(8,128)(2,1)S(1)}, s16[1040,128]{1,0:T(8,128)(2,1)S(1)}, u32[]{:S(2)}, u32[]{:S(2)}) collective-permute-start(s16[1040,128]{1,0:T(8,128)(2,1)S(1)} %get-tuple-element.36), channel_id=1, source_target_pairs={{0,24},{1,7},{2,26},{3,1},{4,28},{5,3},{6,30},{7,5},{8,0},{9,15},{... | collective-permute-start | bytes 798728 | tf_op jit(solution)/shard_map/ppermute | solution.py:29
  64.9 36.1 %copy-start.3 = (s32[128,2]{0,1:T(2,128)S(1)}, s32[128,2]{0,1:T(2,128)}, u32[]{:S(2)}) copy-start(s32[128,2]{0,1:T(2,128)} %param.11) | copy-start | bytes 3076
  64.9 36.1 %copy-start.4 = (s32[128]{0:T(128)S(1)}, s32[128]{0:T(128)}, u32[]{:S(2)}) copy-start(s32[128]{0:T(128)} %param.12) | copy-start | bytes 1540
  64.9 36.1 %copy-start.5 = (f32[128,2]{0,1:T(2,128)S(1)}, f32[128,2]{0,1:T(2,128)}, u32[]{:S(2)}) copy-start(f32[128,2]{0,1:T(2,128)} %param.10) | copy-start | bytes 3076
  64.9 7.0 %collective-permute-start.11 = (s16[1040,128]{1,0:T(8,128)(2,1)S(1)}, s16[1040,128]{1,0:T(8,128)(2,1)S(1)}, u32[]{:S(2)}, u32[]{:S(2)}) collective-permute-start(s16[1040,128]{1,0:T(8,128)(2,1)S(1)} %get-tuple-element.27), channel_id=1, source_target_pairs={{0,8},{1,3},{2,10},{3,5},{4,12},{5,7},{6,14},{7,1},{8,16},{9,11},{... | collective-permute-start | bytes 798728 | tf_op jit(solution)/shard_map/ppermute | solution.py:29
  66.8 7.9 %collective-permute-start.12 = (s16[1040,128]{1,0:T(8,128)(2,1)S(1)}, s16[1040,128]{1,0:T(8,128)(2,1)S(1)}, u32[]{:S(2)}, u32[]{:S(2)}) collective-permute-start(s16[1040,128]{1,0:T(8,128)(2,1)S(1)} %get-tuple-element.28), channel_id=1, source_target_pairs={{0,16},{1,5},{2,18},{3,7},{4,20},{5,1},{6,22},{7,3},{8,24},{9,13},... | collective-permute-start | bytes 798728 | tf_op jit(solution)/shard_map/ppermute | solution.py:29
  71.8 7.6 %collective-permute-start.13 = (s16[1040,128]{1,0:T(8,128)(2,1)S(1)}, s16[1040,128]{1,0:T(8,128)(2,1)S(1)}, u32[]{:S(2)}, u32[]{:S(2)}) collective-permute-start(s16[1040,128]{1,0:T(8,128)(2,1)S(1)} %get-tuple-element.29), channel_id=1, source_target_pairs={{0,24},{1,7},{2,26},{3,1},{4,28},{5,3},{6,30},{7,5},{8,0},{9,15},{... | collective-permute-start | bytes 798728 | tf_op jit(solution)/shard_map/ppermute | solution.py:29
  71.9 7.5 %collective-permute-start.24 = (s16[1040,128]{1,0:T(8,128)(2,1)S(1)}, s16[1040,128]{1,0:T(8,128)(2,1)S(1)}, u32[]{:S(2)}, u32[]{:S(2)}) collective-permute-start(s16[1040,128]{1,0:T(8,128)(2,1)S(1)} %collective-permute-done.23), channel_id=1, source_target_pairs={{0,1},{1,0},{2,3},{3,2},{4,5},{5,4},{6,7},{7,6},{8,9},{9,8},{10,11... | collective-permute-start | bytes 798728 | tf_op jit(solution)/shard_map/ppermute | solution.py:29
  80.4 5.1 %collective-permute-start.26 = (s16[528,128]{1,0:T(8,128)(2,1)S(1)}, s16[528,128]{1,0:T(8,128)(2,1)S(1)}, u32[]{:S(2)}, u32[]{:S(2)}) collective-permute-start(s16[528,128]{1,0:T(8,128)(2,1)S(1)} %get-tuple-element.38), channel_id=1, source_target_pairs={{0,2},{1,9},{2,4},{3,11},{4,6},{5,13},{6,0},{7,15},{8,10},{9,17},{... | collective-permute-start | bytes 405512 | tf_op jit(solution)/shard_map/ppermute | solution.py:29
  81.0 6.6 %collective-permute-start.27 = (s16[528,128]{1,0:T(8,128)(2,1)S(1)}, s16[528,128]{1,0:T(8,128)(2,1)S(1)}, u32[]{:S(2)}, u32[]{:S(2)}) collective-permute-start(s16[528,128]{1,0:T(8,128)(2,1)S(1)} %get-tuple-element.39), channel_id=1, source_target_pairs={{0,4},{1,17},{2,6},{3,19},{4,0},{5,21},{6,2},{7,23},{8,12},{9,25},... | collective-permute-start | bytes 405512 | tf_op jit(solution)/shard_map/ppermute | solution.py:29
  82.8 6.1 %collective-permute-start.28 = (s16[528,128]{1,0:T(8,128)(2,1)S(1)}, s16[528,128]{1,0:T(8,128)(2,1)S(1)}, u32[]{:S(2)}, u32[]{:S(2)}) collective-permute-start(s16[528,128]{1,0:T(8,128)(2,1)S(1)} %get-tuple-element.40), channel_id=1, source_target_pairs={{0,6},{1,25},{2,0},{3,27},{4,2},{5,29},{6,4},{7,31},{8,14},{9,1},{... | collective-permute-start | bytes 405512 | tf_op jit(solution)/shard_map/ppermute | solution.py:29
  (3 other events, 72.7 us)

commit v5 on v3

--- a/solution.py
+++ b/solution.py
@@ -14,6 +14,7 @@
 F32, BF16 = jnp.float32, jnp.bfloat16
 MIB = 1024 * 1024
 CHUNKS = 2
+BLOCK = 64
 STACK_FLOPS = 5000000000
 
 
@@ -90,28 +91,36 @@
     x, y, core = where_ref[0], where_ref[1], where_ref[2]
     rows = normed_ref.shape[0]
     width = own[0].shape[-1]
-    squares = jnp.zeros((rows, width), F32)
-    for pieces in (own, partner):
-        for k2 in range(n):
-            for k1 in range(n):
-                value = pieces[k2][k1].astype(F32)
-                squares = squares + value * value
-    mean_square = jnp.sum(squares, axis=1, keepdims=True) / (2 * n * n * width)
-    scale = lax.rsqrt(mean_square + epsilon)
-    for pieces, parity in ((own, core), (partner, 1 - core)):
-        for k2 in range(n):
-            for k1 in range(n):
-                at_x = lax.rem(x - jnp.where(parity == 0, k1, k2) + n, n)
-                at_y = lax.rem(y - jnp.where(parity == 0, k2, k1) + n, n)
-                t = (at_x * n + at_y) * 2 + parity
-                value = pieces[k2][k1].astype(F32) * scale * gain_ref[:, pl.ds(pl.multiple_of(t * width, width), width)].astype(F32)
-                normed_ref[:, pl.ds(pl.multiple_of(t * width, width), width)] = value.astype(BF16)
+
+    def normalize(i, _):
+        span = pl.ds(pl.multiple_of(i * BLOCK, BLOCK), BLOCK)
+        squares = jnp.zeros((BLOCK, width), F32)
+        for pieces in (own, partner):
+            for k2 in range(n):
+                for k1 in range(n):
+                    value = pieces[k2][k1, span, :].astype(F32)
+                    squares = squares + value * value
+        mean_square = jnp.sum(squares, axis=1, keepdims=True) / (2 * n * n * width)
+        scale = lax.rsqrt(mean_square + epsilon)
+        for pieces, parity in ((own, core), (partner, 1 - core)):
+            for k2 in range(n):
+                for k1 in range(n):
+                    at_x = lax.rem(x - jnp.where(parity == 0, k1, k2) + n, n)
+                    at_y = lax.rem(y - jnp.where(parity == 0, k2, k1) + n, n)
+                    t = (at_x * n + at_y) * 2 + parity
+                    at = pl.ds(pl.multiple_of(t * width, width), width)
+                    value = pieces[k2][k1, span, :].astype(F32) * scale * gain_ref[:, at].astype(F32)
+                    normed_ref[span, at] = value.astype(BF16)
+        return 0
+
+    lax.fori_loop(0, rows // BLOCK, normalize, 0)
     normed = normed_ref[...]
     dims = (((1,), (1,)), ((), ()))
     gate = lax.dot_general(normed, gate_ref[...], dims, preferred_element_type=F32)
     up = lax.dot_general(normed, up_ref[...], dims, preferred_element_type=F32)
     hidden = (gate / (1.0 + jnp.exp(-gate)) * up).astype(BF16)
-    for dx in range(n):
+
+    def project(dx, _):
         for dy in range(n):
             q = lax.rem(x + dx, n) * n + lax.rem(y + dy, n)
             part = down_ref[:, pl.ds(pl.multiple_of(q * 2 * width, 2 * width), 2 * width)]
@@ -120,6 +129,9 @@
             one, two = jnp.where(core == 0, dx, dy), jnp.where(core == 0, dy, dx)
             keep_ref[one, two] = jnp.where(core == 0, low, high)
             send_ref[two, one] = jnp.where(core == 0, high, low)
+        return 0
+
+    lax.fori_loop(0, n, project, 0)
 
 
 def stack_kernel(skipped, *refs):

time: 100 us -> 102 us (1.020)
  Pallas kernels: 16.6 us -> 18.7 us
    pallas_call x2, Pallas kernels: 10.5 us -> 12.6 us  [experts_of(): pl.pallas_call(functools.partial(expert_kernel, n), out_shape=(out, out),...]
  transfers between devices with their start and end apart: 28 -> 28, of which waited for: 15 -> 15; matrix products, arithmetic and copies ran while one was open for 1% -> 1% of each run, Pallas kernels for 12% -> 13%
where the time goes in v5:
time: 102 us
  blocking collectives  29 us (28%)
  starting transfers between devices  28.4 us (28%)
  waiting for transfers between devices  25.1 us (25%)
  Pallas kernels  18.7 us (18%)
    ppermute x28, starting transfers between devices, moved(): return lax.ppermute(array, TP, pairs)  28.4 us
    ppermute x28, waiting for transfers between devices, moved(): return lax.ppermute(array, TP, pairs)  25.1 us
    all_to_all x1, blocking collectives, local(): lax.all_to_all(sent, 'expert', split_axis=0, concat_axis=0, tiled=True)  17.6 us
    pallas_call x2, Pallas kernels, experts_of(): pl.pallas_call(functools.partial(expert_kernel, n), out_shape=(out, out),...  12.6 us
    all_to_all x1, blocking collectives, local(): lax.all_to_all(returning, 'expert', split_axis=0, concat_axis=0, tiled=True)  11.5 us
    pallas_call x1, Pallas kernels, local(): pl.pallas_call(functools.partial(dispatch_kernel, seat_limit, groups), ou...  2.19 us
  transfers between devices with their start and end apart: 28, of which 15 were waited for; matrix products, arithmetic and copies ran while one was open for 1% of the time, Pallas kernels for 13%

profile of v5, /device:TPU:2, one launch (start us, length us, event | category | flops | bytes accessed | tf_op | source)
XLA Modules:
  0.0 102.2 jit_solution(4888040711863297689)
XLA Ops:
  0.0 2.2 %shard_map.82 = bf16[8,64,128]{2,1,0:T(8,128)(2,1)} custom-call(s32[2,128]{1,0:T(2,128)} %bitcast.22, s32[1,128]{1,0:T(1,128)} %bitcast.24, bf16[128,128]{1,0:T(8,128)(2,1)} %tokens_ref.1), custom_call_target="tpu_custom_call" | custom-call | tf_op jit(solution)/shard_map/pallas_call | solution.py:282
  2.2 17.6 %all_to_all.10 = bf16[8,64,128]{2,1,0:T(8,128)(2,1)S(1)} all-to-all(bf16[8,64,128]{2,1,0:T(8,128)(2,1)} %shard_map.82), channel_id=1, replica_groups=mesh['expert'=8,'tp_0'=4,'tp_1'=4,'tp_2'=2] {'expert'}, dimensions={0} | all-to-all | bytes 262144 | tf_op jit(solution)/shard_map/all_to_all | solution.py:287
  19.8 1.5 %collective-permute-start = (bf16[2,256,128]{2,1,0:T(8,128)(2,1)S(1)}, bf16[2,256,128]{2,1,0:T(8,128)(2,1)S(1)}, u32[]{:S(2)}, u32[]{:S(2)}) collective-permute-start(bf16[2,256,128]{2,1,0:T(8,128)(2,1)S(1)} %bitcast.18), channel_id=1, source_target_pairs={{0,8},{1,3},{2,10},{3,5},{4,12},{5,7},{6,14},{7,1},{8,16},{9,11},{... | collective-permute-start | bytes 393224 | tf_op jit(solution)/shard_map/ppermute | solution.py:30
  21.2 1.1 %collective-permute-start.1 = (bf16[2,256,128]{2,1,0:T(8,128)(2,1)S(1)}, bf16[2,256,128]{2,1,0:T(8,128)(2,1)S(1)}, u32[]{:S(2)}, u32[]{:S(2)}) collective-permute-start(bf16[2,256,128]{2,1,0:T(8,128)(2,1)S(1)} %bitcast.19), channel_id=1, source_target_pairs={{0,16},{1,5},{2,18},{3,7},{4,20},{5,1},{6,22},{7,3},{8,24},{9,13},... | collective-permute-start | bytes 393224 | tf_op jit(solution)/shard_map/ppermute | solution.py:30
  22.4 2.2 %collective-permute-start.2 = (bf16[2,256,128]{2,1,0:T(8,128)(2,1)S(1)}, bf16[2,256,128]{2,1,0:T(8,128)(2,1)S(1)}, u32[]{:S(2)}, u32[]{:S(2)}) collective-permute-start(bf16[2,256,128]{2,1,0:T(8,128)(2,1)S(1)} %bitcast.20), channel_id=1, source_target_pairs={{0,24},{1,7},{2,26},{3,1},{4,28},{5,3},{6,30},{7,5},{8,0},{9,15},{... | collective-permute-start | bytes 393224 | tf_op jit(solution)/shard_map/ppermute | solution.py:30
  25.3 2.5 %collective-permute-done.1.refs_4_ = bf16[2,256,128]{2,1,0:T(8,128)(2,1)S(1)} collective-permute-done((bf16[2,256,128]{2,1,0:T(8,128)(2,1)S(1)}, bf16[2,256,128]{2,1,0:T(8,128)(2,1)S(1)}, u32[]{:S(2)}, u32[]{:S(2)}) %collective-permute-start.1) | collective-permute-done | bytes 131104 | tf_op jit(solution)/shard_map/ppermute | solution.py:30
  27.8 0.9 collective-permute-done.2.refs_5_
  28.8 1.7 %collective-permute-start.14 = (bf16[4,256,128]{2,1,0:T(8,128)(2,1)S(1)}, bf16[4,256,128]{2,1,0:T(8,128)(2,1)S(1)}, u32[]{:S(2)}, u32[]{:S(2)}) collective-permute-start(bf16[4,256,128]{2,1,0:T(8,128)(2,1)S(1)} %get-tuple-element.30.refs_0_), channel_id=1, source_target_pairs={{0,2},{1,9},{2,4},{3,11},{4,6},{5,13},{6,0},{7,15},{8,10},{9,17},{... | collective-permute-start | bytes 786440 | tf_op jit(solution)/shard_map/ppermute | solution.py:30
  30.4 2.9 %collective-permute-start.15 = (bf16[4,256,128]{2,1,0:T(8,128)(2,1)S(1)}, bf16[4,256,128]{2,1,0:T(8,128)(2,1)S(1)}, u32[]{:S(2)}, u32[]{:S(2)}) collective-permute-start(bf16[4,256,128]{2,1,0:T(8,128)(2,1)S(1)} %get-tuple-element.30.refs_0_), channel_id=1, source_target_pairs={{0,4},{1,17},{2,6},{3,19},{4,0},{5,21},{6,2},{7,23},{8,12},{9,25},... | collective-permute-start | bytes 786440 | tf_op jit(solution)/shard_map/ppermute | solution.py:30
  33.3 1.3 %collective-permute-start.16 = (bf16[4,256,128]{2,1,0:T(8,128)(2,1)S(1)}, bf16[4,256,128]{2,1,0:T(8,128)(2,1)S(1)}, u32[]{:S(2)}, u32[]{:S(2)}) collective-permute-start(bf16[4,256,128]{2,1,0:T(8,128)(2,1)S(1)} %get-tuple-element.30.refs_0_), channel_id=1, source_target_pairs={{0,6},{1,25},{2,0},{3,27},{4,2},{5,29},{6,4},{7,31},{8,14},{9,1},{... | collective-permute-start | bytes 786440 | tf_op jit(solution)/shard_map/ppermute | solution.py:30
  35.4 1.1 %collective-permute-done.14.refs_1_ = bf16[4,256,128]{2,1,0:T(8,128)(2,1)S(1)} collective-permute-done((bf16[4,256,128]{2,1,0:T(8,128)(2,1)S(1)}, bf16[4,256,128]{2,1,0:T(8,128)(2,1)S(1)}, u32[]{:S(2)}, u32[]{:S(2)}) %collective-permute-start.14) | collective-permute-done | bytes 262176 | tf_op jit(solution)/shard_map/ppermute | solution.py:30
  36.4 2.0 %collective-permute-start.4 = (bf16[4,256,128]{2,1,0:T(8,128)(2,1)S(1)}, bf16[4,256,128]{2,1,0:T(8,128)(2,1)S(1)}, u32[]{:S(2)}, u32[]{:S(2)}) collective-permute-start(bf16[4,256,128]{2,1,0:T(8,128)(2,1)S(1)} %get-tuple-element.23.refs_0_), channel_id=1, source_target_pairs={{0,4},{1,17},{2,6},{3,19},{4,0},{5,21},{6,2},{7,23},{8,12},{9,25},... | collective-permute-start | bytes 786440 | tf_op jit(solution)/shard_map/ppermute | solution.py:30
  38.4 2.2 %collective-permute-done.15.refs_2_ = bf16[4,256,128]{2,1,0:T(8,128)(2,1)S(1)} collective-permute-done((bf16[4,256,128]{2,1,0:T(8,128)(2,1)S(1)}, bf16[4,256,128]{2,1,0:T(8,128)(2,1)S(1)}, u32[]{:S(2)}, u32[]{:S(2)}) %collective-permute-start.15) | collective-permute-done | bytes 262176 | tf_op jit(solution)/shard_map/ppermute | solution.py:30
  41.1 2.2 %collective-permute-done.3.refs_1_ = bf16[4,256,128]{2,1,0:T(8,128)(2,1)S(1)} collective-permute-done((bf16[4,256,128]{2,1,0:T(8,128)(2,1)S(1)}, bf16[4,256,128]{2,1,0:T(8,128)(2,1)S(1)}, u32[]{:S(2)}, u32[]{:S(2)}) %collective-permute-start.3) | collective-permute-done | bytes 262176 | tf_op jit(solution)/shard_map/ppermute | solution.py:30
  43.3 2.8 %collective-permute-done.4.refs_2_ = bf16[4,256,128]{2,1,0:T(8,128)(2,1)S(1)} collective-permute-done((bf16[4,256,128]{2,1,0:T(8,128)(2,1)S(1)}, bf16[4,256,128]{2,1,0:T(8,128)(2,1)S(1)}, u32[]{:S(2)}, u32[]{:S(2)}) %collective-permute-start.4) | collective-permute-done | bytes 262176 | tf_op jit(solution)/shard_map/ppermute | solution.py:30
  47.8 6.3 %shard_map.86 = (f32[4,4,256,128]{3,2,1,0:T(8,128)S(1)}, f32[4,4,256,128]{3,2,1,0:T(8,128)S(1)}) custom-call(s32[3]{0:T(128)S(1)} %pad_add_fusion.refs_1_.where_ref, bf16[4,256,128]{2,1,0:T(8,128)(2,1)S(1)} %get-tuple-element.30.refs_0_, bf16[4,256,128]{2,1,0:T(8,128)(2,1)S(1)} %collective-permute-done.14.refs_1_, ...), custom_call_target="tpu_custom_call" | custom-call | flops 3000000000 | tf_op jit(solution)/shard_map/pallas_call | solution.py:164
  54.4 6.3 %shard_map.84 = (f32[4,4,256,128]{3,2,1,0:T(8,128)S(1)}, f32[4,4,256,128]{3,2,1,0:T(8,128)S(1)}) custom-call(s32[3]{0:T(128)S(1)} %pad_add_fusion.refs_1_.where_ref, bf16[4,256,128]{2,1,0:T(8,128)(2,1)S(1)} %get-tuple-element.23.refs_0_, bf16[4,256,128]{2,1,0:T(8,128)(2,1)S(1)} %collective-permute-done.3.refs_1_, ...), custom_call_target="tpu_custom_call" | custom-call | flops 3000000000 | tf_op jit(solution)/shard_map/pallas_call | solution.py:164
  61.6 1.1 %collective-permute-start.22 = (s16[1040,128]{1,0:T(8,128)(2,1)S(1)}, s16[1040,128]{1,0:T(8,128)(2,1)S(1)}, u32[]{:S(2)}, u32[]{:S(2)}) collective-permute-start(s16[1040,128]{1,0:T(8,128)(2,1)S(1)} %get-tuple-element.34), channel_id=1, source_target_pairs={{0,8},{1,3},{2,10},{3,5},{4,12},{5,7},{6,14},{7,1},{8,16},{9,11},{... | collective-permute-start | bytes 798728 | tf_op jit(solution)/shard_map/ppermute | solution.py:30
  62.7 1.8 %collective-permute-start.23 = (s16[1040,128]{1,0:T(8,128)(2,1)S(1)}, s16[1040,128]{1,0:T(8,128)(2,1)S(1)}, u32[]{:S(2)}, u32[]{:S(2)}) collective-permute-start(s16[1040,128]{1,0:T(8,128)(2,1)S(1)} %get-tuple-element.35), channel_id=1, source_target_pairs={{0,16},{1,5},{2,18},{3,7},{4,20},{5,1},{6,22},{7,3},{8,24},{9,13},... | collective-permute-start | bytes 798728 | tf_op jit(solution)/shard_map/ppermute | solution.py:30
  64.5 2.1 %collective-permute-start.24 = (s16[1040,128]{1,0:T(8,128)(2,1)S(1)}, s16[1040,128]{1,0:T(8,128)(2,1)S(1)}, u32[]{:S(2)}, u32[]{:S(2)}) collective-permute-start(s16[1040,128]{1,0:T(8,128)(2,1)S(1)} %get-tuple-element.36), channel_id=1, source_target_pairs={{0,24},{1,7},{2,26},{3,1},{4,28},{5,3},{6,30},{7,5},{8,0},{9,15},{... | collective-permute-start | bytes 798728 | tf_op jit(solution)/shard_map/ppermute | solution.py:30
  67.2 2.9 %collective-permute-start.12 = (s16[1040,128]{1,0:T(8,128)(2,1)S(1)}, s16[1040,128]{1,0:T(8,128)(2,1)S(1)}, u32[]{:S(2)}, u32[]{:S(2)}) collective-permute-start(s16[1040,128]{1,0:T(8,128)(2,1)S(1)} %get-tuple-element.28), channel_id=1, source_target_pairs={{0,16},{1,5},{2,18},{3,7},{4,20},{5,1},{6,22},{7,3},{8,24},{9,13},... | collective-permute-start | bytes 798728 | tf_op jit(solution)/shard_map/ppermute | solution.py:30
  70.7 2.8 %collective-permute-done.24.refs_7_ = s16[1040,128]{1,0:T(8,128)(2,1)S(1)} collective-permute-done((s16[1040,128]{1,0:T(8,128)(2,1)S(1)}, s16[1040,128]{1,0:T(8,128)(2,1)S(1)}, u32[]{:S(2)}, u32[]{:S(2)}) %collective-permute-start.24) | collective-permute-done | bytes 266272 | tf_op jit(solution)/shard_map/ppermute | solution.py:30
  73.8 2.6 %collective-permute-done.12.refs_2_ = s16[1040,128]{1,0:T(8,128)(2,1)S(1)} collective-permute-done((s16[1040,128]{1,0:T(8,128)(2,1)S(1)}, s16[1040,128]{1,0:T(8,128)(2,1)S(1)}, u32[]{:S(2)}, u32[]{:S(2)}) %collective-permute-start.12) | collective-permute-done | bytes 266272 | tf_op jit(solution)/shard_map/ppermute | solution.py:30
  76.4 2.8 %collective-permute-done.13.refs_3_ = s16[1040,128]{1,0:T(8,128)(2,1)S(1)} collective-permute-done((s16[1040,128]{1,0:T(8,128)(2,1)S(1)}, s16[1040,128]{1,0:T(8,128)(2,1)S(1)}, u32[]{:S(2)}, u32[]{:S(2)}) %collective-permute-start.13) | collective-permute-done | bytes 266272 | tf_op jit(solution)/shard_map/ppermute | solution.py:30
  79.2 1.0 shard_map.88
  80.2 1.6 %collective-permute-start.25 = (s16[528,128]{1,0:T(8,128)(2,1)S(1)}, s16[528,128]{1,0:T(8,128)(2,1)S(1)}, u32[]{:S(2)}, u32[]{:S(2)}) collective-permute-start(s16[528,128]{1,0:T(8,128)(2,1)S(1)} %get-tuple-element.38), channel_id=1, source_target_pairs={{0,2},{1,9},{2,4},{3,11},{4,6},{5,13},{6,0},{7,15},{8,10},{9,17},{... | collective-permute-start | bytes 405512 | tf_op jit(solution)/shard_map/ppermute | solution.py:30
  81.8 2.1 %collective-permute-start.26 = (s16[528,128]{1,0:T(8,128)(2,1)S(1)}, s16[528,128]{1,0:T(8,128)(2,1)S(1)}, u32[]{:S(2)}, u32[]{:S(2)}) collective-permute-start(s16[528,128]{1,0:T(8,128)(2,1)S(1)} %get-tuple-element.39), channel_id=1, source_target_pairs={{0,4},{1,17},{2,6},{3,19},{4,0},{5,21},{6,2},{7,23},{8,12},{9,25},... | collective-permute-start | bytes 405512 | tf_op jit(solution)/shard_map/ppermute | solution.py:30
  83.9 1.1 %collective-permute-start.27 = (s16[528,128]{1,0:T(8,128)(2,1)S(1)}, s16[528,128]{1,0:T(8,128)(2,1)S(1)}, u32[]{:S(2)}, u32[]{:S(2)}) collective-permute-start(s16[528,128]{1,0:T(8,128)(2,1)S(1)} %get-tuple-element.40), channel_id=1, source_target_pairs={{0,6},{1,25},{2,0},{3,27},{4,2},{5,29},{6,4},{7,31},{8,14},{9,1},{... | collective-permute-start | bytes 405512 | tf_op jit(solution)/shard_map/ppermute | solution.py:30
  85.0 1.5 %collective-permute-done.25.refs_0_ = s16[528,128]{1,0:T(8,128)(2,1)S(1)} collective-permute-done((s16[528,128]{1,0:T(8,128)(2,1)S(1)}, s16[528,128]{1,0:T(8,128)(2,1)S(1)}, u32[]{:S(2)}, u32[]{:S(2)}) %collective-permute-start.25) | collective-permute-done | bytes 135200 | tf_op jit(solution)/shard_map/ppermute | solution.py:30
  86.5 1.8 %collective-permute-done.26.refs_1_ = s16[528,128]{1,0:T(8,128)(2,1)S(1)} collective-permute-done((s16[528,128]{1,0:T(8,128)(2,1)S(1)}, s16[528,128]{1,0:T(8,128)(2,1)S(1)}, u32[]{:S(2)}, u32[]{:S(2)}) %collective-permute-start.26) | collective-permute-done | bytes 135200 | tf_op jit(solution)/shard_map/ppermute | solution.py:30
  89.4 11.5 %all_to_all.11.arrived_ref = bf16[8,64,128]{2,1,0:T(8,128)(2,1)S(1)} all-to-all(bf16[8,64,128]{2,1,0:T(8,128)(2,1)S(1)} %bitcast.17), channel_id=1, replica_groups=mesh['expert'=8,'tp_0'=4,'tp_1'=4,'tp_2'=2] {'expert'}, dimensions={0} | all-to-all | bytes 262144 | tf_op jit(solution)/shard_map/all_to_all | solution.py:301
  100.9 1.3 %shard_map.90 = bf16[128,128]{1,0:T(8,128)(2,1)} custom-call(s32[2,128]{1,0:T(2,128)S(1)} %bitcast.23, s32[1,128]{1,0:T(1,128)S(1)} %bitcast.25, f32[2,128]{1,0:T(2,128)S(1)} %bitcast.26, bf16[8,64,128]{2,1,0:T(8,128)(2,1)S(1)} %all_to_all.11.arrived_ref), custom_call_target="tpu_custom_call" | custom-call | tf_op jit(solution)/shard_map/pallas_call | solution.py:302
  (49 shorter events, 7.6 us)
Async XLA Ops:
  19.8 5.6 %collective-permute-start = (bf16[2,256,128]{2,1,0:T(8,128)(2,1)S(1)}, bf16[2,256,128]{2,1,0:T(8,128)(2,1)S(1)}, u32[]{:S(2)}, u32[]{:S(2)}) collective-permute-start(bf16[2,256,128]{2,1,0:T(8,128)(2,1)S(1)} %bitcast.18), channel_id=1, source_target_pairs={{0,8},{1,3},{2,10},{3,5},{4,12},{5,7},{6,14},{7,1},{8,16},{9,11},{... | collective-permute-start | bytes 393224 | tf_op jit(solution)/shard_map/ppermute | solution.py:30
  21.2 6.6 %collective-permute-start.1 = (bf16[2,256,128]{2,1,0:T(8,128)(2,1)S(1)}, bf16[2,256,128]{2,1,0:T(8,128)(2,1)S(1)}, u32[]{:S(2)}, u32[]{:S(2)}) collective-permute-start(bf16[2,256,128]{2,1,0:T(8,128)(2,1)S(1)} %bitcast.19), channel_id=1, source_target_pairs={{0,16},{1,5},{2,18},{3,7},{4,20},{5,1},{6,22},{7,3},{8,24},{9,13},... | collective-permute-start | bytes 393224 | tf_op jit(solution)/shard_map/ppermute | solution.py:30
  22.4 6.4 %collective-permute-start.2 = (bf16[2,256,128]{2,1,0:T(8,128)(2,1)S(1)}, bf16[2,256,128]{2,1,0:T(8,128)(2,1)S(1)}, u32[]{:S(2)}, u32[]{:S(2)}) collective-permute-start(bf16[2,256,128]{2,1,0:T(8,128)(2,1)S(1)} %bitcast.20), channel_id=1, source_target_pairs={{0,24},{1,7},{2,26},{3,1},{4,28},{5,3},{6,30},{7,5},{8,0},{9,15},{... | collective-permute-start | bytes 393224 | tf_op jit(solution)/shard_map/ppermute | solution.py:30
  25.3 22.4 %copy-start.2 = (bf16[1,448,4096]{2,1,0:T(8,128)(2,1)S(1)}, bf16[1,448,4096]{2,1,0:T(8,128)(2,1)}, u32[]{:S(2)}) copy-start(bf16[1,448,4096]{2,1,0:T(8,128)(2,1)} %param.15) | copy-start | bytes 11010052
  28.8 7.7 %collective-permute-start.14 = (bf16[4,256,128]{2,1,0:T(8,128)(2,1)S(1)}, bf16[4,256,128]{2,1,0:T(8,128)(2,1)S(1)}, u32[]{:S(2)}, u32[]{:S(2)}) collective-permute-start(bf16[4,256,128]{2,1,0:T(8,128)(2,1)S(1)} %get-tuple-element.30.refs_0_), channel_id=1, source_target_pairs={{0,2},{1,9},{2,4},{3,11},{4,6},{5,13},{6,0},{7,15},{8,10},{9,17},{... | collective-permute-start | bytes 786440 | tf_op jit(solution)/shard_map/ppermute | solution.py:30
  30.4 10.2 %collective-permute-start.15 = (bf16[4,256,128]{2,1,0:T(8,128)(2,1)S(1)}, bf16[4,256,128]{2,1,0:T(8,128)(2,1)S(1)}, u32[]{:S(2)}, u32[]{:S(2)}) collective-permute-start(bf16[4,256,128]{2,1,0:T(8,128)(2,1)S(1)} %get-tuple-element.30.refs_0_), channel_id=1, source_target_pairs={{0,4},{1,17},{2,6},{3,19},{4,0},{5,21},{6,2},{7,23},{8,12},{9,25},... | collective-permute-start | bytes 786440 | tf_op jit(solution)/shard_map/ppermute | solution.py:30
  33.3 7.3 %collective-permute-start.16 = (bf16[4,256,128]{2,1,0:T(8,128)(2,1)S(1)}, bf16[4,256,128]{2,1,0:T(8,128)(2,1)S(1)}, u32[]{:S(2)}, u32[]{:S(2)}) collective-permute-start(bf16[4,256,128]{2,1,0:T(8,128)(2,1)S(1)} %get-tuple-element.30.refs_0_), channel_id=1, source_target_pairs={{0,6},{1,25},{2,0},{3,27},{4,2},{5,29},{6,4},{7,31},{8,14},{9,1},{... | collective-permute-start | bytes 786440 | tf_op jit(solution)/shard_map/ppermute | solution.py:30
  34.7 5.9 %collective-permute-start.17 = (bf16[4,256,128]{2,1,0:T(8,128)(2,1)S(1)}, bf16[4,256,128]{2,1,0:T(8,128)(2,1)S(1)}, u32[]{:S(2)}, u32[]{:S(2)}) collective-permute-start(bf16[4,256,128]{2,1,0:T(8,128)(2,1)S(1)} %get-tuple-element.30.refs_0_), channel_id=1, source_target_pairs={{0,1},{1,0},{2,3},{3,2},{4,5},{5,4},{6,7},{7,6},{8,9},{9,8},{10,11... | collective-permute-start | bytes 786440 | tf_op jit(solution)/shard_map/ppermute | solution.py:30
  34.7 8.6 %collective-permute-start.3 = (bf16[4,256,128]{2,1,0:T(8,128)(2,1)S(1)}, bf16[4,256,128]{2,1,0:T(8,128)(2,1)S(1)}, u32[]{:S(2)}, u32[]{:S(2)}) collective-permute-start(bf16[4,256,128]{2,1,0:T(8,128)(2,1)S(1)} %get-tuple-element.23.refs_0_), channel_id=1, source_target_pairs={{0,2},{1,9},{2,4},{3,11},{4,6},{5,13},{6,0},{7,15},{8,10},{9,17},{... | collective-permute-start | bytes 786440 | tf_op jit(solution)/shard_map/ppermute | solution.py:30
  36.4 9.7 %collective-permute-start.4 = (bf16[4,256,128]{2,1,0:T(8,128)(2,1)S(1)}, bf16[4,256,128]{2,1,0:T(8,128)(2,1)S(1)}, u32[]{:S(2)}, u32[]{:S(2)}) collective-permute-start(bf16[4,256,128]{2,1,0:T(8,128)(2,1)S(1)} %get-tuple-element.23.refs_0_), channel_id=1, source_target_pairs={{0,4},{1,17},{2,6},{3,19},{4,0},{5,21},{6,2},{7,23},{8,12},{9,25},... | collective-permute-start | bytes 786440 | tf_op jit(solution)/shard_map/ppermute | solution.py:30
  40.6 6.4 %collective-permute-start.5 = (bf16[4,256,128]{2,1,0:T(8,128)(2,1)S(1)}, bf16[4,256,128]{2,1,0:T(8,128)(2,1)S(1)}, u32[]{:S(2)}, u32[]{:S(2)}) collective-permute-start(bf16[4,256,128]{2,1,0:T(8,128)(2,1)S(1)} %get-tuple-element.23.refs_0_), channel_id=1, source_target_pairs={{0,6},{1,25},{2,0},{3,27},{4,2},{5,29},{6,4},{7,31},{8,14},{9,1},{... | collective-permute-start | bytes 786440 | tf_op jit(solution)/shard_map/ppermute | solution.py:30
  40.6 6.4 %collective-permute-start.18 = (bf16[4,256,128]{2,1,0:T(8,128)(2,1)S(1)}, bf16[4,256,128]{2,1,0:T(8,128)(2,1)S(1)}, u32[]{:S(2)}, u32[]{:S(2)}) collective-permute-start(bf16[4,256,128]{2,1,0:T(8,128)(2,1)S(1)} %collective-permute-done.14.refs_1_), channel_id=1, source_target_pairs={{0,1},{1,0},{2,3},{3,2},{4,5},{5,4},{6,7},{7,6},{8,9},{9,8},{10,11... | collective-permute-start | bytes 786440 | tf_op jit(solution)/shard_map/ppermute | solution.py:30
  40.6 6.9 %collective-permute-start.19 = (bf16[4,256,128]{2,1,0:T(8,128)(2,1)S(1)}, bf16[4,256,128]{2,1,0:T(8,128)(2,1)S(1)}, u32[]{:S(2)}, u32[]{:S(2)}) collective-permute-start(bf16[4,256,128]{2,1,0:T(8,128)(2,1)S(1)} %collective-permute-done.15.refs_2_), channel_id=1, source_target_pairs={{0,1},{1,0},{2,3},{3,2},{4,5},{5,4},{6,7},{7,6},{8,9},{9,8},{10,11... | collective-permute-start | bytes 786440 | tf_op jit(solution)/shard_map/ppermute | solution.py:30
  43.3 4.5 %collective-permute-start.20 = (bf16[4,256,128]{2,1,0:T(8,128)(2,1)S(1)}, bf16[4,256,128]{2,1,0:T(8,128)(2,1)S(1)}, u32[]{:S(2)}, u32[]{:S(2)}) collective-permute-start(bf16[4,256,128]{2,1,0:T(8,128)(2,1)S(1)} %collective-permute-done.16.refs_3_), channel_id=1, source_target_pairs={{0,1},{1,0},{2,3},{3,2},{4,5},{5,4},{6,7},{7,6},{8,9},{9,8},{10,11... | collective-permute-start | bytes 786440 | tf_op jit(solution)/shard_map/ppermute | solution.py:30
  46.1 8.3 %collective-permute-start.6 = (bf16[4,256,128]{2,1,0:T(8,128)(2,1)S(1)}, bf16[4,256,128]{2,1,0:T(8,128)(2,1)S(1)}, u32[]{:S(2)}, u32[]{:S(2)}) collective-permute-start(bf16[4,256,128]{2,1,0:T(8,128)(2,1)S(1)} %get-tuple-element.23.refs_0_), channel_id=1, source_target_pairs={{0,1},{1,0},{2,3},{3,2},{4,5},{5,4},{6,7},{7,6},{8,9},{9,8},{10,11... | collective-permute-start | bytes 786440 | tf_op jit(solution)/shard_map/ppermute | solution.py:30
  46.9 7.4 %collective-permute-start.7 = (bf16[4,256,128]{2,1,0:T(8,128)(2,1)S(1)}, bf16[4,256,128]{2,1,0:T(8,128)(2,1)S(1)}, u32[]{:S(2)}, u32[]{:S(2)}) collective-permute-start(bf16[4,256,128]{2,1,0:T(8,128)(2,1)S(1)} %collective-permute-done.3.refs_1_), channel_id=1, source_target_pairs={{0,1},{1,0},{2,3},{3,2},{4,5},{5,4},{6,7},{7,6},{8,9},{9,8},{10,11... | collective-permute-start | bytes 786440 | tf_op jit(solution)/shard_map/ppermute | solution.py:30
  47.0 7.4 %collective-permute-start.8 = (bf16[4,256,128]{2,1,0:T(8,128)(2,1)S(1)}, bf16[4,256,128]{2,1,0:T(8,128)(2,1)S(1)}, u32[]{:S(2)}, u32[]{:S(2)}) collective-permute-start(bf16[4,256,128]{2,1,0:T(8,128)(2,1)S(1)} %collective-permute-done.4.refs_2_), channel_id=1, source_target_pairs={{0,1},{1,0},{2,3},{3,2},{4,5},{5,4},{6,7},{7,6},{8,9},{9,8},{10,11... | collective-permute-start | bytes 786440 | tf_op jit(solution)/shard_map/ppermute | solution.py:30
  47.5 6.9 %collective-permute-start.9 = (bf16[4,256,128]{2,1,0:T(8,128)(2,1)S(1)}, bf16[4,256,128]{2,1,0:T(8,128)(2,1)S(1)}, u32[]{:S(2)}, u32[]{:S(2)}) collective-permute-start(bf16[4,256,128]{2,1,0:T(8,128)(2,1)S(1)} %collective-permute-done.5.refs_3_), channel_id=1, source_target_pairs={{0,1},{1,0},{2,3},{3,2},{4,5},{5,4},{6,7},{7,6},{8,9},{9,8},{10,11... | collective-permute-start | bytes 786440 | tf_op jit(solution)/shard_map/ppermute | solution.py:30
  54.1 7.0 %collective-permute-start.21 = (f32[4,4,256,128]{3,2,1,0:T(8,128)S(1)}, f32[4,4,256,128]{3,2,1,0:T(8,128)S(1)}, u32[]{:S(2)}, u32[]{:S(2)}) collective-permute-start(f32[4,4,256,128]{3,2,1,0:T(8,128)S(1)} %get-tuple-element.32), channel_id=1, source_target_pairs={{0,1},{1,0},{2,3},{3,2},{4,5},{5,4},{6,7},{7,6},{8,9},{9,8},{10,11... | collective-permute-start | bytes 6291464 | tf_op jit(solution)/shard_map/ppermute | solution.py:30
  60.7 5.8 %collective-permute-start.10 = (f32[4,4,256,128]{3,2,1,0:T(8,128)S(1)}, f32[4,4,256,128]{3,2,1,0:T(8,128)S(1)}, u32[]{:S(2)}, u32[]{:S(2)}) collective-permute-start(f32[4,4,256,128]{3,2,1,0:T(8,128)S(1)} %get-tuple-element.25), channel_id=1, source_target_pairs={{0,1},{1,0},{2,3},{3,2},{4,5},{5,4},{6,7},{7,6},{8,9},{9,8},{10,11... | collective-permute-start | bytes 6291464 | tf_op jit(solution)/shard_map/ppermute | solution.py:30
  61.6 8.5 %collective-permute-start.22 = (s16[1040,128]{1,0:T(8,128)(2,1)S(1)}, s16[1040,128]{1,0:T(8,128)(2,1)S(1)}, u32[]{:S(2)}, u32[]{:S(2)}) collective-permute-start(s16[1040,128]{1,0:T(8,128)(2,1)S(1)} %get-tuple-element.34), channel_id=1, source_target_pairs={{0,8},{1,3},{2,10},{3,5},{4,12},{5,7},{6,14},{7,1},{8,16},{9,11},{... | collective-permute-start | bytes 798728 | tf_op jit(solution)/shard_map/ppermute | solution.py:30
  62.7 8.0 %collective-permute-start.23 = (s16[1040,128]{1,0:T(8,128)(2,1)S(1)}, s16[1040,128]{1,0:T(8,128)(2,1)S(1)}, u32[]{:S(2)}, u32[]{:S(2)}) collective-permute-start(s16[1040,128]{1,0:T(8,128)(2,1)S(1)} %get-tuple-element.35), channel_id=1, source_target_pairs={{0,16},{1,5},{2,18},{3,7},{4,20},{5,1},{6,22},{7,3},{8,24},{9,13},... | collective-permute-start | bytes 798728 | tf_op jit(solution)/shard_map/ppermute | solution.py:30
  64.5 9.0 %collective-permute-start.24 = (s16[1040,128]{1,0:T(8,128)(2,1)S(1)}, s16[1040,128]{1,0:T(8,128)(2,1)S(1)}, u32[]{:S(2)}, u32[]{:S(2)}) collective-permute-start(s16[1040,128]{1,0:T(8,128)(2,1)S(1)} %get-tuple-element.36), channel_id=1, source_target_pairs={{0,24},{1,7},{2,26},{3,1},{4,28},{5,3},{6,30},{7,5},{8,0},{9,15},{... | collective-permute-start | bytes 798728 | tf_op jit(solution)/shard_map/ppermute | solution.py:30
  67.1 33.8 %copy-start.3 = (s32[128,2]{0,1:T(2,128)S(1)}, s32[128,2]{0,1:T(2,128)}, u32[]{:S(2)}) copy-start(s32[128,2]{0,1:T(2,128)} %param.11) | copy-start | bytes 3076
  67.1 33.8 %copy-start.4 = (s32[128]{0:T(128)S(1)}, s32[128]{0:T(128)}, u32[]{:S(2)}) copy-start(s32[128]{0:T(128)} %param.12) | copy-start | bytes 1540
  67.1 33.8 %copy-start.5 = (f32[128,2]{0,1:T(2,128)S(1)}, f32[128,2]{0,1:T(2,128)}, u32[]{:S(2)}) copy-start(f32[128,2]{0,1:T(2,128)} %param.10) | copy-start | bytes 3076
  67.1 6.7 %collective-permute-start.11 = (s16[1040,128]{1,0:T(8,128)(2,1)S(1)}, s16[1040,128]{1,0:T(8,128)(2,1)S(1)}, u32[]{:S(2)}, u32[]{:S(2)}) collective-permute-start(s16[1040,128]{1,0:T(8,128)(2,1)S(1)} %get-tuple-element.27), channel_id=1, source_target_pairs={{0,8},{1,3},{2,10},{3,5},{4,12},{5,7},{6,14},{7,1},{8,16},{9,11},{... | collective-permute-start | bytes 798728 | tf_op jit(solution)/shard_map/ppermute | solution.py:30
  67.2 9.2 %collective-permute-start.12 = (s16[1040,128]{1,0:T(8,128)(2,1)S(1)}, s16[1040,128]{1,0:T(8,128)(2,1)S(1)}, u32[]{:S(2)}, u32[]{:S(2)}) collective-permute-start(s16[1040,128]{1,0:T(8,128)(2,1)S(1)} %get-tuple-element.28), channel_id=1, source_target_pairs={{0,16},{1,5},{2,18},{3,7},{4,20},{5,1},{6,22},{7,3},{8,24},{9,13},... | collective-permute-start | bytes 798728 | tf_op jit(solution)/shard_map/ppermute | solution.py:30
  70.1 9.1 %collective-permute-start.13 = (s16[1040,128]{1,0:T(8,128)(2,1)S(1)}, s16[1040,128]{1,0:T(8,128)(2,1)S(1)}, u32[]{:S(2)}, u32[]{:S(2)}) collective-permute-start(s16[1040,128]{1,0:T(8,128)(2,1)S(1)} %get-tuple-element.29), channel_id=1, source_target_pairs={{0,24},{1,7},{2,26},{3,1},{4,28},{5,3},{6,30},{7,5},{8,0},{9,15},{... | collective-permute-start | bytes 798728 | tf_op jit(solution)/shard_map/ppermute | solution.py:30
  80.2 6.3 %collective-permute-start.25 = (s16[528,128]{1,0:T(8,128)(2,1)S(1)}, s16[528,128]{1,0:T(8,128)(2,1)S(1)}, u32[]{:S(2)}, u32[]{:S(2)}) collective-permute-start(s16[528,128]{1,0:T(8,128)(2,1)S(1)} %get-tuple-element.38), channel_id=1, source_target_pairs={{0,2},{1,9},{2,4},{3,11},{4,6},{5,13},{6,0},{7,15},{8,10},{9,17},{... | collective-permute-start | bytes 405512 | tf_op jit(solution)/shard_map/ppermute | solution.py:30
  81.8 6.5 %collective-permute-start.26 = (s16[528,128]{1,0:T(8,128)(2,1)S(1)}, s16[528,128]{1,0:T(8,128)(2,1)S(1)}, u32[]{:S(2)}, u32[]{:S(2)}) collective-permute-start(s16[528,128]{1,0:T(8,128)(2,1)S(1)} %get-tuple-element.39), channel_id=1, source_target_pairs={{0,4},{1,17},{2,6},{3,19},{4,0},{5,21},{6,2},{7,23},{8,12},{9,25},... | collective-permute-start | bytes 405512 | tf_op jit(solution)/shard_map/ppermute | solution.py:30
  83.9 5.0 %collective-permute-start.27 = (s16[528,128]{1,0:T(8,128)(2,1)S(1)}, s16[528,128]{1,0:T(8,128)(2,1)S(1)}, u32[]{:S(2)}, u32[]{:S(2)}) collective-permute-start(s16[528,128]{1,0:T(8,128)(2,1)S(1)} %get-tuple-element.40), channel_id=1, source_target_pairs={{0,6},{1,25},{2,0},{3,27},{4,2},{5,29},{6,4},{7,31},{8,14},{9,1},{... | collective-permute-start | bytes 405512 | tf_op jit(solution)/shard_map/ppermute | solution.py:30
  (2 other events, 44.9 us)

commit v6 on v3

--- a/solution.py
+++ b/solution.py
@@ -86,10 +86,9 @@
 
 def expert_kernel(n, where_ref, *refs):
     own, partner = refs[:n], refs[n : 2 * n]
-    gain_ref, gate_ref, up_ref, down_ref, keep_ref, send_ref, normed_ref = refs[2 * n :]
+    gain_ref, gate_ref, up_ref, down_ref, keep_ref, send_ref = refs[2 * n :]
     x, y, core = where_ref[0], where_ref[1], where_ref[2]
-    rows = normed_ref.shape[0]
-    width = own[0].shape[-1]
+    rows, width = own[0].shape[1:]
     squares = jnp.zeros((rows, width), F32)
     for pieces in (own, partner):
         for k2 in range(n):
@@ -98,18 +97,21 @@
                 squares = squares + value * value
     mean_square = jnp.sum(squares, axis=1, keepdims=True) / (2 * n * n * width)
     scale = lax.rsqrt(mean_square + epsilon)
-    for pieces, parity in ((own, core), (partner, 1 - core)):
+    dims = (((1,), (1,)), ((), ()))
+    gate = up = None
+    for k1 in range(n):
         for k2 in range(n):
-            for k1 in range(n):
-                at_x = lax.rem(x - jnp.where(parity == 0, k1, k2) + n, n)
-                at_y = lax.rem(y - jnp.where(parity == 0, k2, k1) + n, n)
-                t = (at_x * n + at_y) * 2 + parity
-                value = pieces[k2][k1].astype(F32) * scale * gain_ref[:, pl.ds(pl.multiple_of(t * width, width), width)].astype(F32)
-                normed_ref[:, pl.ds(pl.multiple_of(t * width, width), width)] = value.astype(BF16)
-    normed = normed_ref[...]
-    dims = (((1,), (1,)), ((), ()))
-    gate = lax.dot_general(normed, gate_ref[...], dims, preferred_element_type=F32)
-    up = lax.dot_general(normed, up_ref[...], dims, preferred_element_type=F32)
+            at_x = lax.rem(x - jnp.where(core == 0, k1, k2) + n, n)
+            at_y = lax.rem(y - jnp.where(core == 0, k2, k1) + n, n)
+            at = pl.ds(pl.multiple_of((at_x * n + at_y) * 2 * width, 2 * width), 2 * width)
+            mine, other = own[k2][k1], partner[k1][k2]
+            pair = [jnp.where(core == 0, mine, other), jnp.where(core == 0, other, mine)]
+            value = jnp.concatenate(pair, axis=1).astype(F32) * scale * gain_ref[:, at].astype(F32)
+            value = value.astype(BF16)
+            gate_part = lax.dot_general(value, gate_ref[:, at], dims, preferred_element_type=F32)
+            up_part = lax.dot_general(value, up_ref[:, at], dims, preferred_element_type=F32)
+            gate = gate_part if gate is None else gate + gate_part
+            up = up_part if up is None else up + up_part
     hidden = (gate / (1.0 + jnp.exp(-gate)) * up).astype(BF16)
     for dx in range(n):
         for dy in range(n):
@@ -146,7 +148,6 @@
 def experts_of(where, own, partner, gains, gate, up, down):
     n = len(own)
     _, rows, width = own[0].shape
-    model = gate.shape[1]
     vmem = pl.BlockSpec(memory_space=pltpu.VMEM)
     out = jax.ShapeDtypeStruct((n, n, rows, width), F32)
     return pl.pallas_call(
@@ -154,7 +155,6 @@
         out_shape=(out, out),
         in_specs=[pl.BlockSpec(memory_space=pltpu.SMEM)] + [vmem] * (2 * n + 4),
         out_specs=(vmem, vmem),
-        scratch_shapes=[pltpu.VMEM((rows, model), BF16)],
         compiler_params=pltpu.CompilerParams(vmem_limit_bytes=10 * MIB),
         cost_estimate=pl.CostEstimate(flops=3000000000, transcendentals=0, bytes_accessed=0),
     )(where, *own, *partner, gains, gate, up, down)

time: 100 us -> 99.2 us (level)
  Pallas kernels: 16.6 us -> 15.5 us
    pallas_call x2, Pallas kernels: 10.5 us -> 9.34 us  [experts_of(): pl.pallas_call(functools.partial(expert_kernel, n), out_shape=(out, out),...]
  transfers between devices with their start and end apart: 28 -> 28, of which waited for: 15 -> 14; matrix products, arithmetic and copies ran while one was open for 1% -> 1% of each run, Pallas kernels for 12% -> 11%
where the time goes in v6:
time: 99.2 us; the launch traced here: 98.8 us
  blocking collectives  29 us (29%)
  starting transfers between devices  28.5 us (29%)
  waiting for transfers between devices  24.9 us (25%)
  Pallas kernels  15.5 us (16%)
    ppermute x28, starting transfers between devices, moved(): return lax.ppermute(array, TP, pairs)  28.5 us
    ppermute x28, waiting for transfers between devices, moved(): return lax.ppermute(array, TP, pairs)  24.9 us
    all_to_all x1, blocking collectives, local(): lax.all_to_all(sent, 'expert', split_axis=0, concat_axis=0, tiled=True)  17.6 us
    all_to_all x1, blocking collectives, local(): lax.all_to_all(returning, 'expert', split_axis=0, concat_axis=0, tiled=True)  11.5 us
    pallas_call x2, Pallas kernels, experts_of(): pl.pallas_call(functools.partial(expert_kernel, n), out_shape=(out, out),...  9.34 us
    pallas_call x1, Pallas kernels, local(): pl.pallas_call(functools.partial(dispatch_kernel, seat_limit, groups), ou...  2.19 us
  transfers between devices with their start and end apart: 28, of which 14 were waited for; matrix products, arithmetic and copies ran while one was open for 1% of the time, Pallas kernels for 11%

profile of v6, /device:TPU:2, one launch (start us, length us, event | category | flops | bytes accessed | tf_op | source)
XLA Modules:
  0.0 98.8 jit_solution(430634591059924907)
XLA Ops:
  0.0 2.2 %shard_map.82 = bf16[8,64,128]{2,1,0:T(8,128)(2,1)} custom-call(s32[2,128]{1,0:T(2,128)} %bitcast.22, s32[1,128]{1,0:T(1,128)} %bitcast.24, bf16[128,128]{1,0:T(8,128)(2,1)} %tokens_ref.1), custom_call_target="tpu_custom_call" | custom-call | tf_op jit(solution)/shard_map/pallas_call | solution.py:270
  2.2 17.6 %all_to_all.10 = bf16[8,64,128]{2,1,0:T(8,128)(2,1)S(1)} all-to-all(bf16[8,64,128]{2,1,0:T(8,128)(2,1)} %shard_map.82), channel_id=1, replica_groups=mesh['expert'=8,'tp_0'=4,'tp_1'=4,'tp_2'=2] {'expert'}, dimensions={0} | all-to-all | bytes 262144 | tf_op jit(solution)/shard_map/all_to_all | solution.py:275
  19.8 1.5 %collective-permute-start = (bf16[2,256,128]{2,1,0:T(8,128)(2,1)S(1)}, bf16[2,256,128]{2,1,0:T(8,128)(2,1)S(1)}, u32[]{:S(2)}, u32[]{:S(2)}) collective-permute-start(bf16[2,256,128]{2,1,0:T(8,128)(2,1)S(1)} %bitcast.18), channel_id=1, source_target_pairs={{0,8},{1,3},{2,10},{3,5},{4,12},{5,7},{6,14},{7,1},{8,16},{9,11},{... | collective-permute-start | bytes 393224 | tf_op jit(solution)/shard_map/ppermute | solution.py:29
  21.2 1.1 %collective-permute-start.1 = (bf16[2,256,128]{2,1,0:T(8,128)(2,1)S(1)}, bf16[2,256,128]{2,1,0:T(8,128)(2,1)S(1)}, u32[]{:S(2)}, u32[]{:S(2)}) collective-permute-start(bf16[2,256,128]{2,1,0:T(8,128)(2,1)S(1)} %bitcast.19), channel_id=1, source_target_pairs={{0,16},{1,5},{2,18},{3,7},{4,20},{5,1},{6,22},{7,3},{8,24},{9,13},... | collective-permute-start | bytes 393224 | tf_op jit(solution)/shard_map/ppermute | solution.py:29
  22.4 2.2 %collective-permute-start.2 = (bf16[2,256,128]{2,1,0:T(8,128)(2,1)S(1)}, bf16[2,256,128]{2,1,0:T(8,128)(2,1)S(1)}, u32[]{:S(2)}, u32[]{:S(2)}) collective-permute-start(bf16[2,256,128]{2,1,0:T(8,128)(2,1)S(1)} %bitcast.20), channel_id=1, source_target_pairs={{0,24},{1,7},{2,26},{3,1},{4,28},{5,3},{6,30},{7,5},{8,0},{9,15},{... | collective-permute-start | bytes 393224 | tf_op jit(solution)/shard_map/ppermute | solution.py:29
  25.3 2.5 %collective-permute-done.1.refs_4_ = bf16[2,256,128]{2,1,0:T(8,128)(2,1)S(1)} collective-permute-done((bf16[2,256,128]{2,1,0:T(8,128)(2,1)S(1)}, bf16[2,256,128]{2,1,0:T(8,128)(2,1)S(1)}, u32[]{:S(2)}, u32[]{:S(2)}) %collective-permute-start.1) | collective-permute-done | bytes 131104 | tf_op jit(solution)/shard_map/ppermute | solution.py:29
  27.8 0.9 collective-permute-done.2.refs_5_
  28.8 1.7 %collective-permute-start.14 = (bf16[4,256,128]{2,1,0:T(8,128)(2,1)S(1)}, bf16[4,256,128]{2,1,0:T(8,128)(2,1)S(1)}, u32[]{:S(2)}, u32[]{:S(2)}) collective-permute-start(bf16[4,256,128]{2,1,0:T(8,128)(2,1)S(1)} %get-tuple-element.30.refs_0_), channel_id=1, source_target_pairs={{0,2},{1,9},{2,4},{3,11},{4,6},{5,13},{6,0},{7,15},{8,10},{9,17},{... | collective-permute-start | bytes 786440 | tf_op jit(solution)/shard_map/ppermute | solution.py:29
  30.4 2.9 %collective-permute-start.15 = (bf16[4,256,128]{2,1,0:T(8,128)(2,1)S(1)}, bf16[4,256,128]{2,1,0:T(8,128)(2,1)S(1)}, u32[]{:S(2)}, u32[]{:S(2)}) collective-permute-start(bf16[4,256,128]{2,1,0:T(8,128)(2,1)S(1)} %get-tuple-element.30.refs_0_), channel_id=1, source_target_pairs={{0,4},{1,17},{2,6},{3,19},{4,0},{5,21},{6,2},{7,23},{8,12},{9,25},... | collective-permute-start | bytes 786440 | tf_op jit(solution)/shard_map/ppermute | solution.py:29
  33.3 1.3 %collective-permute-start.16 = (bf16[4,256,128]{2,1,0:T(8,128)(2,1)S(1)}, bf16[4,256,128]{2,1,0:T(8,128)(2,1)S(1)}, u32[]{:S(2)}, u32[]{:S(2)}) collective-permute-start(bf16[4,256,128]{2,1,0:T(8,128)(2,1)S(1)} %get-tuple-element.30.refs_0_), channel_id=1, source_target_pairs={{0,6},{1,25},{2,0},{3,27},{4,2},{5,29},{6,4},{7,31},{8,14},{9,1},{... | collective-permute-start | bytes 786440 | tf_op jit(solution)/shard_map/ppermute | solution.py:29
  35.4 1.1 %collective-permute-done.14.refs_1_ = bf16[4,256,128]{2,1,0:T(8,128)(2,1)S(1)} collective-permute-done((bf16[4,256,128]{2,1,0:T(8,128)(2,1)S(1)}, bf16[4,256,128]{2,1,0:T(8,128)(2,1)S(1)}, u32[]{:S(2)}, u32[]{:S(2)}) %collective-permute-start.14) | collective-permute-done | bytes 262176 | tf_op jit(solution)/shard_map/ppermute | solution.py:29
  36.4 2.0 %collective-permute-start.4 = (bf16[4,256,128]{2,1,0:T(8,128)(2,1)S(1)}, bf16[4,256,128]{2,1,0:T(8,128)(2,1)S(1)}, u32[]{:S(2)}, u32[]{:S(2)}) collective-permute-start(bf16[4,256,128]{2,1,0:T(8,128)(2,1)S(1)} %get-tuple-element.23.refs_0_), channel_id=1, source_target_pairs={{0,4},{1,17},{2,6},{3,19},{4,0},{5,21},{6,2},{7,23},{8,12},{9,25},... | collective-permute-start | bytes 786440 | tf_op jit(solution)/shard_map/ppermute | solution.py:29
  38.4 2.2 %collective-permute-done.15.refs_2_ = bf16[4,256,128]{2,1,0:T(8,128)(2,1)S(1)} collective-permute-done((bf16[4,256,128]{2,1,0:T(8,128)(2,1)S(1)}, bf16[4,256,128]{2,1,0:T(8,128)(2,1)S(1)}, u32[]{:S(2)}, u32[]{:S(2)}) %collective-permute-start.15) | collective-permute-done | bytes 262176 | tf_op jit(solution)/shard_map/ppermute | solution.py:29
  41.1 2.2 %collective-permute-done.3.refs_1_ = bf16[4,256,128]{2,1,0:T(8,128)(2,1)S(1)} collective-permute-done((bf16[4,256,128]{2,1,0:T(8,128)(2,1)S(1)}, bf16[4,256,128]{2,1,0:T(8,128)(2,1)S(1)}, u32[]{:S(2)}, u32[]{:S(2)}) %collective-permute-start.3) | collective-permute-done | bytes 262176 | tf_op jit(solution)/shard_map/ppermute | solution.py:29
  43.3 2.8 %collective-permute-done.4.refs_2_ = bf16[4,256,128]{2,1,0:T(8,128)(2,1)S(1)} collective-permute-done((bf16[4,256,128]{2,1,0:T(8,128)(2,1)S(1)}, bf16[4,256,128]{2,1,0:T(8,128)(2,1)S(1)}, u32[]{:S(2)}, u32[]{:S(2)}) %collective-permute-start.4) | collective-permute-done | bytes 262176 | tf_op jit(solution)/shard_map/ppermute | solution.py:29
  47.8 4.7 %shard_map.86 = (f32[4,4,256,128]{3,2,1,0:T(8,128)S(1)}, f32[4,4,256,128]{3,2,1,0:T(8,128)S(1)}) custom-call(s32[3]{0:T(128)S(1)} %pad_add_fusion.refs_1_.where_ref, bf16[4,256,128]{2,1,0:T(8,128)(2,1)S(1)} %get-tuple-element.30.refs_0_, bf16[4,256,128]{2,1,0:T(8,128)(2,1)S(1)} %collective-permute-done.14.refs_1_, ...), custom_call_target="tpu_custom_call" | custom-call | flops 3000000000 | tf_op jit(solution)/shard_map/pallas_call | solution.py:153
  52.8 4.7 %shard_map.84 = (f32[4,4,256,128]{3,2,1,0:T(8,128)S(1)}, f32[4,4,256,128]{3,2,1,0:T(8,128)S(1)}) custom-call(s32[3]{0:T(128)S(1)} %pad_add_fusion.refs_1_.where_ref, bf16[4,256,128]{2,1,0:T(8,128)(2,1)S(1)} %get-tuple-element.23.refs_0_, bf16[4,256,128]{2,1,0:T(8,128)(2,1)S(1)} %collective-permute-done.3.refs_1_, ...), custom_call_target="tpu_custom_call" | custom-call | flops 3000000000 | tf_op jit(solution)/shard_map/pallas_call | solution.py:153
  58.3 1.1 %collective-permute-start.22 = (s16[1040,128]{1,0:T(8,128)(2,1)S(1)}, s16[1040,128]{1,0:T(8,128)(2,1)S(1)}, u32[]{:S(2)}, u32[]{:S(2)}) collective-permute-start(s16[1040,128]{1,0:T(8,128)(2,1)S(1)} %get-tuple-element.34), channel_id=1, source_target_pairs={{0,8},{1,3},{2,10},{3,5},{4,12},{5,7},{6,14},{7,1},{8,16},{9,11},{... | collective-permute-start | bytes 798728 | tf_op jit(solution)/shard_map/ppermute | solution.py:29
  59.4 1.8 %collective-permute-start.23 = (s16[1040,128]{1,0:T(8,128)(2,1)S(1)}, s16[1040,128]{1,0:T(8,128)(2,1)S(1)}, u32[]{:S(2)}, u32[]{:S(2)}) collective-permute-start(s16[1040,128]{1,0:T(8,128)(2,1)S(1)} %get-tuple-element.35), channel_id=1, source_target_pairs={{0,16},{1,5},{2,18},{3,7},{4,20},{5,1},{6,22},{7,3},{8,24},{9,13},... | collective-permute-start | bytes 798728 | tf_op jit(solution)/shard_map/ppermute | solution.py:29
  61.2 2.0 %collective-permute-start.24 = (s16[1040,128]{1,0:T(8,128)(2,1)S(1)}, s16[1040,128]{1,0:T(8,128)(2,1)S(1)}, u32[]{:S(2)}, u32[]{:S(2)}) collective-permute-start(s16[1040,128]{1,0:T(8,128)(2,1)S(1)} %get-tuple-element.36), channel_id=1, source_target_pairs={{0,24},{1,7},{2,26},{3,1},{4,28},{5,3},{6,30},{7,5},{8,0},{9,15},{... | collective-permute-start | bytes 798728 | tf_op jit(solution)/shard_map/ppermute | solution.py:29
  64.2 2.9 %collective-permute-start.12 = (s16[1040,128]{1,0:T(8,128)(2,1)S(1)}, s16[1040,128]{1,0:T(8,128)(2,1)S(1)}, u32[]{:S(2)}, u32[]{:S(2)}) collective-permute-start(s16[1040,128]{1,0:T(8,128)(2,1)S(1)} %get-tuple-element.28), channel_id=1, source_target_pairs={{0,16},{1,5},{2,18},{3,7},{4,20},{5,1},{6,22},{7,3},{8,24},{9,13},... | collective-permute-start | bytes 798728 | tf_op jit(solution)/shard_map/ppermute | solution.py:29
  67.4 2.7 %collective-permute-done.24.refs_7_ = s16[1040,128]{1,0:T(8,128)(2,1)S(1)} collective-permute-done((s16[1040,128]{1,0:T(8,128)(2,1)S(1)}, s16[1040,128]{1,0:T(8,128)(2,1)S(1)}, u32[]{:S(2)}, u32[]{:S(2)}) %collective-permute-start.24) | collective-permute-done | bytes 266272 | tf_op jit(solution)/shard_map/ppermute | solution.py:29
  70.6 2.6 %collective-permute-done.12.refs_2_ = s16[1040,128]{1,0:T(8,128)(2,1)S(1)} collective-permute-done((s16[1040,128]{1,0:T(8,128)(2,1)S(1)}, s16[1040,128]{1,0:T(8,128)(2,1)S(1)}, u32[]{:S(2)}, u32[]{:S(2)}) %collective-permute-start.12) | collective-permute-done | bytes 266272 | tf_op jit(solution)/shard_map/ppermute | solution.py:29
  73.2 2.8 %collective-permute-done.13.refs_3_ = s16[1040,128]{1,0:T(8,128)(2,1)S(1)} collective-permute-done((s16[1040,128]{1,0:T(8,128)(2,1)S(1)}, s16[1040,128]{1,0:T(8,128)(2,1)S(1)}, u32[]{:S(2)}, u32[]{:S(2)}) %collective-permute-start.13) | collective-permute-done | bytes 266272 | tf_op jit(solution)/shard_map/ppermute | solution.py:29
  75.9 1.0 %shard_map.88 = (f32[512,128]{1,0:T(8,128)S(1)}, s16[528,128]{1,0:T(8,128)(2,1)S(1)}, s16[528,128]{1,0:T(8,128)(2,1)S(1)}, s16[528,128]{1,0:T(8,128)(2,1)S(1)}) custom-call(f32[4,256,128]{2,1,0:T(8,128)S(1)} %get-tuple-element.26.refs_0_, s16[1040,128]{1,0:T(8,128)(2,1)S(1)} %collective-permute-done.11.refs_1_, ...), custom_call_target="tpu_custom_call" | custom-call | tf_op jit(solution)/shard_map/pallas_call | solution.py:249
  76.9 1.5 %collective-permute-start.25 = (s16[528,128]{1,0:T(8,128)(2,1)S(1)}, s16[528,128]{1,0:T(8,128)(2,1)S(1)}, u32[]{:S(2)}, u32[]{:S(2)}) collective-permute-start(s16[528,128]{1,0:T(8,128)(2,1)S(1)} %get-tuple-element.38), channel_id=1, source_target_pairs={{0,2},{1,9},{2,4},{3,11},{4,6},{5,13},{6,0},{7,15},{8,10},{9,17},{... | collective-permute-start | bytes 405512 | tf_op jit(solution)/shard_map/ppermute | solution.py:29
  78.4 2.1 %collective-permute-start.26 = (s16[528,128]{1,0:T(8,128)(2,1)S(1)}, s16[528,128]{1,0:T(8,128)(2,1)S(1)}, u32[]{:S(2)}, u32[]{:S(2)}) collective-permute-start(s16[528,128]{1,0:T(8,128)(2,1)S(1)} %get-tuple-element.39), channel_id=1, source_target_pairs={{0,4},{1,17},{2,6},{3,19},{4,0},{5,21},{6,2},{7,23},{8,12},{9,25},... | collective-permute-start | bytes 405512 | tf_op jit(solution)/shard_map/ppermute | solution.py:29
  80.5 1.2 %collective-permute-start.27 = (s16[528,128]{1,0:T(8,128)(2,1)S(1)}, s16[528,128]{1,0:T(8,128)(2,1)S(1)}, u32[]{:S(2)}, u32[]{:S(2)}) collective-permute-start(s16[528,128]{1,0:T(8,128)(2,1)S(1)} %get-tuple-element.40), channel_id=1, source_target_pairs={{0,6},{1,25},{2,0},{3,27},{4,2},{5,29},{6,4},{7,31},{8,14},{9,1},{... | collective-permute-start | bytes 405512 | tf_op jit(solution)/shard_map/ppermute | solution.py:29
  81.7 1.5 %collective-permute-done.25.refs_0_ = s16[528,128]{1,0:T(8,128)(2,1)S(1)} collective-permute-done((s16[528,128]{1,0:T(8,128)(2,1)S(1)}, s16[528,128]{1,0:T(8,128)(2,1)S(1)}, u32[]{:S(2)}, u32[]{:S(2)}) %collective-permute-start.25) | collective-permute-done | bytes 135200 | tf_op jit(solution)/shard_map/ppermute | solution.py:29
  83.2 1.7 %collective-permute-done.26.refs_1_ = s16[528,128]{1,0:T(8,128)(2,1)S(1)} collective-permute-done((s16[528,128]{1,0:T(8,128)(2,1)S(1)}, s16[528,128]{1,0:T(8,128)(2,1)S(1)}, u32[]{:S(2)}, u32[]{:S(2)}) %collective-permute-start.26) | collective-permute-done | bytes 135200 | tf_op jit(solution)/shard_map/ppermute | solution.py:29
  86.1 11.5 %all_to_all.11.arrived_ref = bf16[8,64,128]{2,1,0:T(8,128)(2,1)S(1)} all-to-all(bf16[8,64,128]{2,1,0:T(8,128)(2,1)S(1)} %bitcast.17), channel_id=1, replica_groups=mesh['expert'=8,'tp_0'=4,'tp_1'=4,'tp_2'=2] {'expert'}, dimensions={0} | all-to-all | bytes 262144 | tf_op jit(solution)/shard_map/all_to_all | solution.py:289
  97.6 1.3 %shard_map.90 = bf16[128,128]{1,0:T(8,128)(2,1)} custom-call(s32[2,128]{1,0:T(2,128)S(1)} %bitcast.23, s32[1,128]{1,0:T(1,128)S(1)} %bitcast.25, f32[2,128]{1,0:T(2,128)S(1)} %bitcast.26, bf16[8,64,128]{2,1,0:T(8,128)(2,1)S(1)} %all_to_all.11.arrived_ref), custom_call_target="tpu_custom_call" | custom-call | tf_op jit(solution)/shard_map/pallas_call | solution.py:290
  (49 shorter events, 7.7 us)
Async XLA Ops:
  19.8 5.6 %collective-permute-start = (bf16[2,256,128]{2,1,0:T(8,128)(2,1)S(1)}, bf16[2,256,128]{2,1,0:T(8,128)(2,1)S(1)}, u32[]{:S(2)}, u32[]{:S(2)}) collective-permute-start(bf16[2,256,128]{2,1,0:T(8,128)(2,1)S(1)} %bitcast.18), channel_id=1, source_target_pairs={{0,8},{1,3},{2,10},{3,5},{4,12},{5,7},{6,14},{7,1},{8,16},{9,11},{... | collective-permute-start | bytes 393224 | tf_op jit(solution)/shard_map/ppermute | solution.py:29
  21.2 6.6 %collective-permute-start.1 = (bf16[2,256,128]{2,1,0:T(8,128)(2,1)S(1)}, bf16[2,256,128]{2,1,0:T(8,128)(2,1)S(1)}, u32[]{:S(2)}, u32[]{:S(2)}) collective-permute-start(bf16[2,256,128]{2,1,0:T(8,128)(2,1)S(1)} %bitcast.19), channel_id=1, source_target_pairs={{0,16},{1,5},{2,18},{3,7},{4,20},{5,1},{6,22},{7,3},{8,24},{9,13},... | collective-permute-start | bytes 393224 | tf_op jit(solution)/shard_map/ppermute | solution.py:29
  22.4 6.4 %collective-permute-start.2 = (bf16[2,256,128]{2,1,0:T(8,128)(2,1)S(1)}, bf16[2,256,128]{2,1,0:T(8,128)(2,1)S(1)}, u32[]{:S(2)}, u32[]{:S(2)}) collective-permute-start(bf16[2,256,128]{2,1,0:T(8,128)(2,1)S(1)} %bitcast.20), channel_id=1, source_target_pairs={{0,24},{1,7},{2,26},{3,1},{4,28},{5,3},{6,30},{7,5},{8,0},{9,15},{... | collective-permute-start | bytes 393224 | tf_op jit(solution)/shard_map/ppermute | solution.py:29
  25.3 22.4 %copy-start.2 = (bf16[1,448,4096]{2,1,0:T(8,128)(2,1)S(1)}, bf16[1,448,4096]{2,1,0:T(8,128)(2,1)}, u32[]{:S(2)}) copy-start(bf16[1,448,4096]{2,1,0:T(8,128)(2,1)} %param.15) | copy-start | bytes 11010052
  28.8 7.7 %collective-permute-start.14 = (bf16[4,256,128]{2,1,0:T(8,128)(2,1)S(1)}, bf16[4,256,128]{2,1,0:T(8,128)(2,1)S(1)}, u32[]{:S(2)}, u32[]{:S(2)}) collective-permute-start(bf16[4,256,128]{2,1,0:T(8,128)(2,1)S(1)} %get-tuple-element.30.refs_0_), channel_id=1, source_target_pairs={{0,2},{1,9},{2,4},{3,11},{4,6},{5,13},{6,0},{7,15},{8,10},{9,17},{... | collective-permute-start | bytes 786440 | tf_op jit(solution)/shard_map/ppermute | solution.py:29
  30.4 10.2 %collective-permute-start.15 = (bf16[4,256,128]{2,1,0:T(8,128)(2,1)S(1)}, bf16[4,256,128]{2,1,0:T(8,128)(2,1)S(1)}, u32[]{:S(2)}, u32[]{:S(2)}) collective-permute-start(bf16[4,256,128]{2,1,0:T(8,128)(2,1)S(1)} %get-tuple-element.30.refs_0_), channel_id=1, source_target_pairs={{0,4},{1,17},{2,6},{3,19},{4,0},{5,21},{6,2},{7,23},{8,12},{9,25},... | collective-permute-start | bytes 786440 | tf_op jit(solution)/shard_map/ppermute | solution.py:29
  33.3 7.3 %collective-permute-start.16 = (bf16[4,256,128]{2,1,0:T(8,128)(2,1)S(1)}, bf16[4,256,128]{2,1,0:T(8,128)(2,1)S(1)}, u32[]{:S(2)}, u32[]{:S(2)}) collective-permute-start(bf16[4,256,128]{2,1,0:T(8,128)(2,1)S(1)} %get-tuple-element.30.refs_0_), channel_id=1, source_target_pairs={{0,6},{1,25},{2,0},{3,27},{4,2},{5,29},{6,4},{7,31},{8,14},{9,1},{... | collective-permute-start | bytes 786440 | tf_op jit(solution)/shard_map/ppermute | solution.py:29
  34.7 5.9 %collective-permute-start.17 = (bf16[4,256,128]{2,1,0:T(8,128)(2,1)S(1)}, bf16[4,256,128]{2,1,0:T(8,128)(2,1)S(1)}, u32[]{:S(2)}, u32[]{:S(2)}) collective-permute-start(bf16[4,256,128]{2,1,0:T(8,128)(2,1)S(1)} %get-tuple-element.30.refs_0_), channel_id=1, source_target_pairs={{0,1},{1,0},{2,3},{3,2},{4,5},{5,4},{6,7},{7,6},{8,9},{9,8},{10,11... | collective-permute-start | bytes 786440 | tf_op jit(solution)/shard_map/ppermute | solution.py:29
  34.7 8.6 %collective-permute-start.3 = (bf16[4,256,128]{2,1,0:T(8,128)(2,1)S(1)}, bf16[4,256,128]{2,1,0:T(8,128)(2,1)S(1)}, u32[]{:S(2)}, u32[]{:S(2)}) collective-permute-start(bf16[4,256,128]{2,1,0:T(8,128)(2,1)S(1)} %get-tuple-element.23.refs_0_), channel_id=1, source_target_pairs={{0,2},{1,9},{2,4},{3,11},{4,6},{5,13},{6,0},{7,15},{8,10},{9,17},{... | collective-permute-start | bytes 786440 | tf_op jit(solution)/shard_map/ppermute | solution.py:29
  36.4 9.7 %collective-permute-start.4 = (bf16[4,256,128]{2,1,0:T(8,128)(2,1)S(1)}, bf16[4,256,128]{2,1,0:T(8,128)(2,1)S(1)}, u32[]{:S(2)}, u32[]{:S(2)}) collective-permute-start(bf16[4,256,128]{2,1,0:T(8,128)(2,1)S(1)} %get-tuple-element.23.refs_0_), channel_id=1, source_target_pairs={{0,4},{1,17},{2,6},{3,19},{4,0},{5,21},{6,2},{7,23},{8,12},{9,25},... | collective-permute-start | bytes 786440 | tf_op jit(solution)/shard_map/ppermute | solution.py:29
  40.6 6.4 %collective-permute-start.5 = (bf16[4,256,128]{2,1,0:T(8,128)(2,1)S(1)}, bf16[4,256,128]{2,1,0:T(8,128)(2,1)S(1)}, u32[]{:S(2)}, u32[]{:S(2)}) collective-permute-start(bf16[4,256,128]{2,1,0:T(8,128)(2,1)S(1)} %get-tuple-element.23.refs_0_), channel_id=1, source_target_pairs={{0,6},{1,25},{2,0},{3,27},{4,2},{5,29},{6,4},{7,31},{8,14},{9,1},{... | collective-permute-start | bytes 786440 | tf_op jit(solution)/shard_map/ppermute | solution.py:29
  40.6 6.4 %collective-permute-start.18 = (bf16[4,256,128]{2,1,0:T(8,128)(2,1)S(1)}, bf16[4,256,128]{2,1,0:T(8,128)(2,1)S(1)}, u32[]{:S(2)}, u32[]{:S(2)}) collective-permute-start(bf16[4,256,128]{2,1,0:T(8,128)(2,1)S(1)} %collective-permute-done.14.refs_1_), channel_id=1, source_target_pairs={{0,1},{1,0},{2,3},{3,2},{4,5},{5,4},{6,7},{7,6},{8,9},{9,8},{10,11... | collective-permute-start | bytes 786440 | tf_op jit(solution)/shard_map/ppermute | solution.py:29
  40.6 6.9 %collective-permute-start.19 = (bf16[4,256,128]{2,1,0:T(8,128)(2,1)S(1)}, bf16[4,256,128]{2,1,0:T(8,128)(2,1)S(1)}, u32[]{:S(2)}, u32[]{:S(2)}) collective-permute-start(bf16[4,256,128]{2,1,0:T(8,128)(2,1)S(1)} %collective-permute-done.15.refs_2_), channel_id=1, source_target_pairs={{0,1},{1,0},{2,3},{3,2},{4,5},{5,4},{6,7},{7,6},{8,9},{9,8},{10,11... | collective-permute-start | bytes 786440 | tf_op jit(solution)/shard_map/ppermute | solution.py:29
  43.3 4.5 %collective-permute-start.20 = (bf16[4,256,128]{2,1,0:T(8,128)(2,1)S(1)}, bf16[4,256,128]{2,1,0:T(8,128)(2,1)S(1)}, u32[]{:S(2)}, u32[]{:S(2)}) collective-permute-start(bf16[4,256,128]{2,1,0:T(8,128)(2,1)S(1)} %collective-permute-done.16.refs_3_), channel_id=1, source_target_pairs={{0,1},{1,0},{2,3},{3,2},{4,5},{5,4},{6,7},{7,6},{8,9},{9,8},{10,11... | collective-permute-start | bytes 786440 | tf_op jit(solution)/shard_map/ppermute | solution.py:29
  46.1 6.7 %collective-permute-start.6 = (bf16[4,256,128]{2,1,0:T(8,128)(2,1)S(1)}, bf16[4,256,128]{2,1,0:T(8,128)(2,1)S(1)}, u32[]{:S(2)}, u32[]{:S(2)}) collective-permute-start(bf16[4,256,128]{2,1,0:T(8,128)(2,1)S(1)} %get-tuple-element.23.refs_0_), channel_id=1, source_target_pairs={{0,1},{1,0},{2,3},{3,2},{4,5},{5,4},{6,7},{7,6},{8,9},{9,8},{10,11... | collective-permute-start | bytes 786440 | tf_op jit(solution)/shard_map/ppermute | solution.py:29
  46.9 5.8 %collective-permute-start.7 = (bf16[4,256,128]{2,1,0:T(8,128)(2,1)S(1)}, bf16[4,256,128]{2,1,0:T(8,128)(2,1)S(1)}, u32[]{:S(2)}, u32[]{:S(2)}) collective-permute-start(bf16[4,256,128]{2,1,0:T(8,128)(2,1)S(1)} %collective-permute-done.3.refs_1_), channel_id=1, source_target_pairs={{0,1},{1,0},{2,3},{3,2},{4,5},{5,4},{6,7},{7,6},{8,9},{9,8},{10,11... | collective-permute-start | bytes 786440 | tf_op jit(solution)/shard_map/ppermute | solution.py:29
  47.0 5.8 %collective-permute-start.8 = (bf16[4,256,128]{2,1,0:T(8,128)(2,1)S(1)}, bf16[4,256,128]{2,1,0:T(8,128)(2,1)S(1)}, u32[]{:S(2)}, u32[]{:S(2)}) collective-permute-start(bf16[4,256,128]{2,1,0:T(8,128)(2,1)S(1)} %collective-permute-done.4.refs_2_), channel_id=1, source_target_pairs={{0,1},{1,0},{2,3},{3,2},{4,5},{5,4},{6,7},{7,6},{8,9},{9,8},{10,11... | collective-permute-start | bytes 786440 | tf_op jit(solution)/shard_map/ppermute | solution.py:29
  47.5 5.3 %collective-permute-start.9 = (bf16[4,256,128]{2,1,0:T(8,128)(2,1)S(1)}, bf16[4,256,128]{2,1,0:T(8,128)(2,1)S(1)}, u32[]{:S(2)}, u32[]{:S(2)}) collective-permute-start(bf16[4,256,128]{2,1,0:T(8,128)(2,1)S(1)} %collective-permute-done.5.refs_3_), channel_id=1, source_target_pairs={{0,1},{1,0},{2,3},{3,2},{4,5},{5,4},{6,7},{7,6},{8,9},{9,8},{10,11... | collective-permute-start | bytes 786440 | tf_op jit(solution)/shard_map/ppermute | solution.py:29
  52.4 5.4 %collective-permute-start.21 = (f32[4,4,256,128]{3,2,1,0:T(8,128)S(1)}, f32[4,4,256,128]{3,2,1,0:T(8,128)S(1)}, u32[]{:S(2)}, u32[]{:S(2)}) collective-permute-start(f32[4,4,256,128]{3,2,1,0:T(8,128)S(1)} %get-tuple-element.32), channel_id=1, source_target_pairs={{0,1},{1,0},{2,3},{3,2},{4,5},{5,4},{6,7},{7,6},{8,9},{9,8},{10,11... | collective-permute-start | bytes 6291464 | tf_op jit(solution)/shard_map/ppermute | solution.py:29
  57.4 5.8 %collective-permute-start.10 = (f32[4,4,256,128]{3,2,1,0:T(8,128)S(1)}, f32[4,4,256,128]{3,2,1,0:T(8,128)S(1)}, u32[]{:S(2)}, u32[]{:S(2)}) collective-permute-start(f32[4,4,256,128]{3,2,1,0:T(8,128)S(1)} %get-tuple-element.25), channel_id=1, source_target_pairs={{0,1},{1,0},{2,3},{3,2},{4,5},{5,4},{6,7},{7,6},{8,9},{9,8},{10,11... | collective-permute-start | bytes 6291464 | tf_op jit(solution)/shard_map/ppermute | solution.py:29
  58.3 8.7 %collective-permute-start.22 = (s16[1040,128]{1,0:T(8,128)(2,1)S(1)}, s16[1040,128]{1,0:T(8,128)(2,1)S(1)}, u32[]{:S(2)}, u32[]{:S(2)}) collective-permute-start(s16[1040,128]{1,0:T(8,128)(2,1)S(1)} %get-tuple-element.34), channel_id=1, source_target_pairs={{0,8},{1,3},{2,10},{3,5},{4,12},{5,7},{6,14},{7,1},{8,16},{9,11},{... | collective-permute-start | bytes 798728 | tf_op jit(solution)/shard_map/ppermute | solution.py:29
  59.4 8.0 %collective-permute-start.23 = (s16[1040,128]{1,0:T(8,128)(2,1)S(1)}, s16[1040,128]{1,0:T(8,128)(2,1)S(1)}, u32[]{:S(2)}, u32[]{:S(2)}) collective-permute-start(s16[1040,128]{1,0:T(8,128)(2,1)S(1)} %get-tuple-element.35), channel_id=1, source_target_pairs={{0,16},{1,5},{2,18},{3,7},{4,20},{5,1},{6,22},{7,3},{8,24},{9,13},... | collective-permute-start | bytes 798728 | tf_op jit(solution)/shard_map/ppermute | solution.py:29
  61.2 9.0 %collective-permute-start.24 = (s16[1040,128]{1,0:T(8,128)(2,1)S(1)}, s16[1040,128]{1,0:T(8,128)(2,1)S(1)}, u32[]{:S(2)}, u32[]{:S(2)}) collective-permute-start(s16[1040,128]{1,0:T(8,128)(2,1)S(1)} %get-tuple-element.36), channel_id=1, source_target_pairs={{0,24},{1,7},{2,26},{3,1},{4,28},{5,3},{6,30},{7,5},{8,0},{9,15},{... | collective-permute-start | bytes 798728 | tf_op jit(solution)/shard_map/ppermute | solution.py:29
  63.8 33.7 %copy-start.3 = (s32[128,2]{0,1:T(2,128)S(1)}, s32[128,2]{0,1:T(2,128)}, u32[]{:S(2)}) copy-start(s32[128,2]{0,1:T(2,128)} %param.11) | copy-start | bytes 3076
  63.8 33.7 %copy-start.4 = (s32[128]{0:T(128)S(1)}, s32[128]{0:T(128)}, u32[]{:S(2)}) copy-start(s32[128]{0:T(128)} %param.12) | copy-start | bytes 1540
  63.8 33.7 %copy-start.5 = (f32[128,2]{0,1:T(2,128)S(1)}, f32[128,2]{0,1:T(2,128)}, u32[]{:S(2)}) copy-start(f32[128,2]{0,1:T(2,128)} %param.10) | copy-start | bytes 3076
  63.8 6.7 %collective-permute-start.11 = (s16[1040,128]{1,0:T(8,128)(2,1)S(1)}, s16[1040,128]{1,0:T(8,128)(2,1)S(1)}, u32[]{:S(2)}, u32[]{:S(2)}) collective-permute-start(s16[1040,128]{1,0:T(8,128)(2,1)S(1)} %get-tuple-element.27), channel_id=1, source_target_pairs={{0,8},{1,3},{2,10},{3,5},{4,12},{5,7},{6,14},{7,1},{8,16},{9,11},{... | collective-permute-start | bytes 798728 | tf_op jit(solution)/shard_map/ppermute | solution.py:29
  64.2 9.0 %collective-permute-start.12 = (s16[1040,128]{1,0:T(8,128)(2,1)S(1)}, s16[1040,128]{1,0:T(8,128)(2,1)S(1)}, u32[]{:S(2)}, u32[]{:S(2)}) collective-permute-start(s16[1040,128]{1,0:T(8,128)(2,1)S(1)} %get-tuple-element.28), channel_id=1, source_target_pairs={{0,16},{1,5},{2,18},{3,7},{4,20},{5,1},{6,22},{7,3},{8,24},{9,13},... | collective-permute-start | bytes 798728 | tf_op jit(solution)/shard_map/ppermute | solution.py:29
  67.1 8.9 %collective-permute-start.13 = (s16[1040,128]{1,0:T(8,128)(2,1)S(1)}, s16[1040,128]{1,0:T(8,128)(2,1)S(1)}, u32[]{:S(2)}, u32[]{:S(2)}) collective-permute-start(s16[1040,128]{1,0:T(8,128)(2,1)S(1)} %get-tuple-element.29), channel_id=1, source_target_pairs={{0,24},{1,7},{2,26},{3,1},{4,28},{5,3},{6,30},{7,5},{8,0},{9,15},{... | collective-permute-start | bytes 798728 | tf_op jit(solution)/shard_map/ppermute | solution.py:29
  76.9 6.3 %collective-permute-start.25 = (s16[528,128]{1,0:T(8,128)(2,1)S(1)}, s16[528,128]{1,0:T(8,128)(2,1)S(1)}, u32[]{:S(2)}, u32[]{:S(2)}) collective-permute-start(s16[528,128]{1,0:T(8,128)(2,1)S(1)} %get-tuple-element.38), channel_id=1, source_target_pairs={{0,2},{1,9},{2,4},{3,11},{4,6},{5,13},{6,0},{7,15},{8,10},{9,17},{... | collective-permute-start | bytes 405512 | tf_op jit(solution)/shard_map/ppermute | solution.py:29
  78.4 6.5 %collective-permute-start.26 = (s16[528,128]{1,0:T(8,128)(2,1)S(1)}, s16[528,128]{1,0:T(8,128)(2,1)S(1)}, u32[]{:S(2)}, u32[]{:S(2)}) collective-permute-start(s16[528,128]{1,0:T(8,128)(2,1)S(1)} %get-tuple-element.39), channel_id=1, source_target_pairs={{0,4},{1,17},{2,6},{3,19},{4,0},{5,21},{6,2},{7,23},{8,12},{9,25},... | collective-permute-start | bytes 405512 | tf_op jit(solution)/shard_map/ppermute | solution.py:29
  80.5 5.1 %collective-permute-start.27 = (s16[528,128]{1,0:T(8,128)(2,1)S(1)}, s16[528,128]{1,0:T(8,128)(2,1)S(1)}, u32[]{:S(2)}, u32[]{:S(2)}) collective-permute-start(s16[528,128]{1,0:T(8,128)(2,1)S(1)} %get-tuple-element.40), channel_id=1, source_target_pairs={{0,6},{1,25},{2,0},{3,27},{4,2},{5,29},{6,4},{7,31},{8,14},{9,1},{... | collective-permute-start | bytes 405512 | tf_op jit(solution)/shard_map/ppermute | solution.py:29
  (2 other events, 44.9 us)

commit v7 on v6

--- a/solution.py
+++ b/solution.py
@@ -99,6 +99,7 @@
     scale = lax.rsqrt(mean_square + epsilon)
     dims = (((1,), (1,)), ((), ()))
     gate = up = None
+    held = []
     for k1 in range(n):
         for k2 in range(n):
             at_x = lax.rem(x - jnp.where(core == 0, k1, k2) + n, n)
@@ -108,8 +109,13 @@
             pair = [jnp.where(core == 0, mine, other), jnp.where(core == 0, other, mine)]
             value = jnp.concatenate(pair, axis=1).astype(F32) * scale * gain_ref[:, at].astype(F32)
             value = value.astype(BF16)
-            gate_part = lax.dot_general(value, gate_ref[:, at], dims, preferred_element_type=F32)
-            up_part = lax.dot_general(value, up_ref[:, at], dims, preferred_element_type=F32)
+            held.append((value, gate_ref[:, at], up_ref[:, at]))
+            if len(held) < 2:
+                continue
+            value, gate_part, up_part = (jnp.concatenate(parts, axis=1) for parts in zip(*held))
+            held = []
+            gate_part = lax.dot_general(value, gate_part, dims, preferred_element_type=F32)
+            up_part = lax.dot_general(value, up_part, dims, preferred_element_type=F32)
             gate = gate_part if gate is None else gate + gate_part
             up = up_part if up is None else up + up_part
     hidden = (gate / (1.0 + jnp.exp(-gate)) * up).astype(BF16)

time: 99.2 us -> 99.1 us (level)
  transfers between devices with their start and end apart: 28 -> 28, of which waited for: 14 -> 14; matrix products, arithmetic and copies ran while one was open for 1% -> 1% of each run, Pallas kernels for 11% -> 10%
where the time goes in v7:
time: 99.1 us; the launch traced here: 98.8 us
  blocking collectives  29 us (29%)
  starting transfers between devices  28.6 us (29%)
  waiting for transfers between devices  24.8 us (25%)
  Pallas kernels  15.4 us (16%)
    ppermute x28, starting transfers between devices, moved(): return lax.ppermute(array, TP, pairs)  28.6 us
    ppermute x28, waiting for transfers between devices, moved(): return lax.ppermute(array, TP, pairs)  24.8 us
    all_to_all x1, blocking collectives, local(): lax.all_to_all(sent, 'expert', split_axis=0, concat_axis=0, tiled=True)  17.6 us
    all_to_all x1, blocking collectives, local(): lax.all_to_all(returning, 'expert', split_axis=0, concat_axis=0, tiled=True)  11.5 us
    pallas_call x2, Pallas kernels, experts_of(): pl.pallas_call(functools.partial(expert_kernel, n), out_shape=(out, out),...  9.28 us
    pallas_call x1, Pallas kernels, local(): pl.pallas_call(functools.partial(dispatch_kernel, seat_limit, groups), ou...  2.19 us
  transfers between devices with their start and end apart: 28, of which 14 were waited for; matrix products, arithmetic and copies ran while one was open for 1% of the time, Pallas kernels for 10%

profile of v7, /device:TPU:2, one launch (start us, length us, event | category | flops | bytes accessed | tf_op | source)
XLA Modules:
  0.0 98.8 jit_solution(17843106136681969092)
XLA Ops:
  0.0 2.2 %shard_map.82 = bf16[8,64,128]{2,1,0:T(8,128)(2,1)} custom-call(s32[2,128]{1,0:T(2,128)} %bitcast.22, s32[1,128]{1,0:T(1,128)} %bitcast.24, bf16[128,128]{1,0:T(8,128)(2,1)} %tokens_ref.1), custom_call_target="tpu_custom_call" | custom-call | tf_op jit(solution)/shard_map/pallas_call | solution.py:276
  2.2 17.6 %all_to_all.10 = bf16[8,64,128]{2,1,0:T(8,128)(2,1)S(1)} all-to-all(bf16[8,64,128]{2,1,0:T(8,128)(2,1)} %shard_map.82), channel_id=1, replica_groups=mesh['expert'=8,'tp_0'=4,'tp_1'=4,'tp_2'=2] {'expert'}, dimensions={0} | all-to-all | bytes 262144 | tf_op jit(solution)/shard_map/all_to_all | solution.py:281
  19.8 1.5 %collective-permute-start = (bf16[2,256,128]{2,1,0:T(8,128)(2,1)S(1)}, bf16[2,256,128]{2,1,0:T(8,128)(2,1)S(1)}, u32[]{:S(2)}, u32[]{:S(2)}) collective-permute-start(bf16[2,256,128]{2,1,0:T(8,128)(2,1)S(1)} %bitcast.18), channel_id=1, source_target_pairs={{0,8},{1,3},{2,10},{3,5},{4,12},{5,7},{6,14},{7,1},{8,16},{9,11},{... | collective-permute-start | bytes 393224 | tf_op jit(solution)/shard_map/ppermute | solution.py:29
  21.2 1.1 %collective-permute-start.1 = (bf16[2,256,128]{2,1,0:T(8,128)(2,1)S(1)}, bf16[2,256,128]{2,1,0:T(8,128)(2,1)S(1)}, u32[]{:S(2)}, u32[]{:S(2)}) collective-permute-start(bf16[2,256,128]{2,1,0:T(8,128)(2,1)S(1)} %bitcast.19), channel_id=1, source_target_pairs={{0,16},{1,5},{2,18},{3,7},{4,20},{5,1},{6,22},{7,3},{8,24},{9,13},... | collective-permute-start | bytes 393224 | tf_op jit(solution)/shard_map/ppermute | solution.py:29
  22.4 2.2 %collective-permute-start.2 = (bf16[2,256,128]{2,1,0:T(8,128)(2,1)S(1)}, bf16[2,256,128]{2,1,0:T(8,128)(2,1)S(1)}, u32[]{:S(2)}, u32[]{:S(2)}) collective-permute-start(bf16[2,256,128]{2,1,0:T(8,128)(2,1)S(1)} %bitcast.20), channel_id=1, source_target_pairs={{0,24},{1,7},{2,26},{3,1},{4,28},{5,3},{6,30},{7,5},{8,0},{9,15},{... | collective-permute-start | bytes 393224 | tf_op jit(solution)/shard_map/ppermute | solution.py:29
  25.3 2.5 %collective-permute-done.1.refs_4_ = bf16[2,256,128]{2,1,0:T(8,128)(2,1)S(1)} collective-permute-done((bf16[2,256,128]{2,1,0:T(8,128)(2,1)S(1)}, bf16[2,256,128]{2,1,0:T(8,128)(2,1)S(1)}, u32[]{:S(2)}, u32[]{:S(2)}) %collective-permute-start.1) | collective-permute-done | bytes 131104 | tf_op jit(solution)/shard_map/ppermute | solution.py:29
  27.8 0.9 collective-permute-done.2.refs_5_
  28.8 1.7 %collective-permute-start.14 = (bf16[4,256,128]{2,1,0:T(8,128)(2,1)S(1)}, bf16[4,256,128]{2,1,0:T(8,128)(2,1)S(1)}, u32[]{:S(2)}, u32[]{:S(2)}) collective-permute-start(bf16[4,256,128]{2,1,0:T(8,128)(2,1)S(1)} %get-tuple-element.30.refs_0_), channel_id=1, source_target_pairs={{0,2},{1,9},{2,4},{3,11},{4,6},{5,13},{6,0},{7,15},{8,10},{9,17},{... | collective-permute-start | bytes 786440 | tf_op jit(solution)/shard_map/ppermute | solution.py:29
  30.4 2.9 %collective-permute-start.15 = (bf16[4,256,128]{2,1,0:T(8,128)(2,1)S(1)}, bf16[4,256,128]{2,1,0:T(8,128)(2,1)S(1)}, u32[]{:S(2)}, u32[]{:S(2)}) collective-permute-start(bf16[4,256,128]{2,1,0:T(8,128)(2,1)S(1)} %get-tuple-element.30.refs_0_), channel_id=1, source_target_pairs={{0,4},{1,17},{2,6},{3,19},{4,0},{5,21},{6,2},{7,23},{8,12},{9,25},... | collective-permute-start | bytes 786440 | tf_op jit(solution)/shard_map/ppermute | solution.py:29
  33.3 1.3 %collective-permute-start.16 = (bf16[4,256,128]{2,1,0:T(8,128)(2,1)S(1)}, bf16[4,256,128]{2,1,0:T(8,128)(2,1)S(1)}, u32[]{:S(2)}, u32[]{:S(2)}) collective-permute-start(bf16[4,256,128]{2,1,0:T(8,128)(2,1)S(1)} %get-tuple-element.30.refs_0_), channel_id=1, source_target_pairs={{0,6},{1,25},{2,0},{3,27},{4,2},{5,29},{6,4},{7,31},{8,14},{9,1},{... | collective-permute-start | bytes 786440 | tf_op jit(solution)/shard_map/ppermute | solution.py:29
  35.4 1.1 %collective-permute-done.14.refs_1_ = bf16[4,256,128]{2,1,0:T(8,128)(2,1)S(1)} collective-permute-done((bf16[4,256,128]{2,1,0:T(8,128)(2,1)S(1)}, bf16[4,256,128]{2,1,0:T(8,128)(2,1)S(1)}, u32[]{:S(2)}, u32[]{:S(2)}) %collective-permute-start.14) | collective-permute-done | bytes 262176 | tf_op jit(solution)/shard_map/ppermute | solution.py:29
  36.4 2.0 %collective-permute-start.4 = (bf16[4,256,128]{2,1,0:T(8,128)(2,1)S(1)}, bf16[4,256,128]{2,1,0:T(8,128)(2,1)S(1)}, u32[]{:S(2)}, u32[]{:S(2)}) collective-permute-start(bf16[4,256,128]{2,1,0:T(8,128)(2,1)S(1)} %get-tuple-element.23.refs_0_), channel_id=1, source_target_pairs={{0,4},{1,17},{2,6},{3,19},{4,0},{5,21},{6,2},{7,23},{8,12},{9,25},... | collective-permute-start | bytes 786440 | tf_op jit(solution)/shard_map/ppermute | solution.py:29
  38.4 2.2 %collective-permute-done.15.refs_2_ = bf16[4,256,128]{2,1,0:T(8,128)(2,1)S(1)} collective-permute-done((bf16[4,256,128]{2,1,0:T(8,128)(2,1)S(1)}, bf16[4,256,128]{2,1,0:T(8,128)(2,1)S(1)}, u32[]{:S(2)}, u32[]{:S(2)}) %collective-permute-start.15) | collective-permute-done | bytes 262176 | tf_op jit(solution)/shard_map/ppermute | solution.py:29
  41.1 2.2 %collective-permute-done.3.refs_1_ = bf16[4,256,128]{2,1,0:T(8,128)(2,1)S(1)} collective-permute-done((bf16[4,256,128]{2,1,0:T(8,128)(2,1)S(1)}, bf16[4,256,128]{2,1,0:T(8,128)(2,1)S(1)}, u32[]{:S(2)}, u32[]{:S(2)}) %collective-permute-start.3) | collective-permute-done | bytes 262176 | tf_op jit(solution)/shard_map/ppermute | solution.py:29
  43.3 2.8 %collective-permute-done.4.refs_2_ = bf16[4,256,128]{2,1,0:T(8,128)(2,1)S(1)} collective-permute-done((bf16[4,256,128]{2,1,0:T(8,128)(2,1)S(1)}, bf16[4,256,128]{2,1,0:T(8,128)(2,1)S(1)}, u32[]{:S(2)}, u32[]{:S(2)}) %collective-permute-start.4) | collective-permute-done | bytes 262176 | tf_op jit(solution)/shard_map/ppermute | solution.py:29
  47.8 4.6 %shard_map.86 = (f32[4,4,256,128]{3,2,1,0:T(8,128)S(1)}, f32[4,4,256,128]{3,2,1,0:T(8,128)S(1)}) custom-call(s32[3]{0:T(128)S(1)} %pad_add_fusion.refs_1_.where_ref, bf16[4,256,128]{2,1,0:T(8,128)(2,1)S(1)} %get-tuple-element.30.refs_0_, bf16[4,256,128]{2,1,0:T(8,128)(2,1)S(1)} %collective-permute-done.14.refs_1_, ...), custom_call_target="tpu_custom_call" | custom-call | flops 3000000000 | tf_op jit(solution)/shard_map/pallas_call | solution.py:159
  52.8 4.6 %shard_map.84 = (f32[4,4,256,128]{3,2,1,0:T(8,128)S(1)}, f32[4,4,256,128]{3,2,1,0:T(8,128)S(1)}) custom-call(s32[3]{0:T(128)S(1)} %pad_add_fusion.refs_1_.where_ref, bf16[4,256,128]{2,1,0:T(8,128)(2,1)S(1)} %get-tuple-element.23.refs_0_, bf16[4,256,128]{2,1,0:T(8,128)(2,1)S(1)} %collective-permute-done.3.refs_1_, ...), custom_call_target="tpu_custom_call" | custom-call | flops 3000000000 | tf_op jit(solution)/shard_map/pallas_call | solution.py:159
  58.3 1.1 %collective-permute-start.22 = (s16[1040,128]{1,0:T(8,128)(2,1)S(1)}, s16[1040,128]{1,0:T(8,128)(2,1)S(1)}, u32[]{:S(2)}, u32[]{:S(2)}) collective-permute-start(s16[1040,128]{1,0:T(8,128)(2,1)S(1)} %get-tuple-element.34), channel_id=1, source_target_pairs={{0,8},{1,3},{2,10},{3,5},{4,12},{5,7},{6,14},{7,1},{8,16},{9,11},{... | collective-permute-start | bytes 798728 | tf_op jit(solution)/shard_map/ppermute | solution.py:29
  59.4 1.8 %collective-permute-start.23 = (s16[1040,128]{1,0:T(8,128)(2,1)S(1)}, s16[1040,128]{1,0:T(8,128)(2,1)S(1)}, u32[]{:S(2)}, u32[]{:S(2)}) collective-permute-start(s16[1040,128]{1,0:T(8,128)(2,1)S(1)} %get-tuple-element.35), channel_id=1, source_target_pairs={{0,16},{1,5},{2,18},{3,7},{4,20},{5,1},{6,22},{7,3},{8,24},{9,13},... | collective-permute-start | bytes 798728 | tf_op jit(solution)/shard_map/ppermute | solution.py:29
  61.2 2.0 %collective-permute-start.24 = (s16[1040,128]{1,0:T(8,128)(2,1)S(1)}, s16[1040,128]{1,0:T(8,128)(2,1)S(1)}, u32[]{:S(2)}, u32[]{:S(2)}) collective-permute-start(s16[1040,128]{1,0:T(8,128)(2,1)S(1)} %get-tuple-element.36), channel_id=1, source_target_pairs={{0,24},{1,7},{2,26},{3,1},{4,28},{5,3},{6,30},{7,5},{8,0},{9,15},{... | collective-permute-start | bytes 798728 | tf_op jit(solution)/shard_map/ppermute | solution.py:29
  64.1 2.9 %collective-permute-start.12 = (s16[1040,128]{1,0:T(8,128)(2,1)S(1)}, s16[1040,128]{1,0:T(8,128)(2,1)S(1)}, u32[]{:S(2)}, u32[]{:S(2)}) collective-permute-start(s16[1040,128]{1,0:T(8,128)(2,1)S(1)} %get-tuple-element.28), channel_id=1, source_target_pairs={{0,16},{1,5},{2,18},{3,7},{4,20},{5,1},{6,22},{7,3},{8,24},{9,13},... | collective-permute-start | bytes 798728 | tf_op jit(solution)/shard_map/ppermute | solution.py:29
  67.4 2.8 %collective-permute-done.24.refs_7_ = s16[1040,128]{1,0:T(8,128)(2,1)S(1)} collective-permute-done((s16[1040,128]{1,0:T(8,128)(2,1)S(1)}, s16[1040,128]{1,0:T(8,128)(2,1)S(1)}, u32[]{:S(2)}, u32[]{:S(2)}) %collective-permute-start.24) | collective-permute-done | bytes 266272 | tf_op jit(solution)/shard_map/ppermute | solution.py:29
  70.5 2.6 %collective-permute-done.12.refs_2_ = s16[1040,128]{1,0:T(8,128)(2,1)S(1)} collective-permute-done((s16[1040,128]{1,0:T(8,128)(2,1)S(1)}, s16[1040,128]{1,0:T(8,128)(2,1)S(1)}, u32[]{:S(2)}, u32[]{:S(2)}) %collective-permute-start.12) | collective-permute-done | bytes 266272 | tf_op jit(solution)/shard_map/ppermute | solution.py:29
  73.1 2.8 %collective-permute-done.13.refs_3_ = s16[1040,128]{1,0:T(8,128)(2,1)S(1)} collective-permute-done((s16[1040,128]{1,0:T(8,128)(2,1)S(1)}, s16[1040,128]{1,0:T(8,128)(2,1)S(1)}, u32[]{:S(2)}, u32[]{:S(2)}) %collective-permute-start.13) | collective-permute-done | bytes 266272 | tf_op jit(solution)/shard_map/ppermute | solution.py:29
  75.9 1.0 %shard_map.88 = (f32[512,128]{1,0:T(8,128)S(1)}, s16[528,128]{1,0:T(8,128)(2,1)S(1)}, s16[528,128]{1,0:T(8,128)(2,1)S(1)}, s16[528,128]{1,0:T(8,128)(2,1)S(1)}) custom-call(f32[4,256,128]{2,1,0:T(8,128)S(1)} %get-tuple-element.26.refs_0_, s16[1040,128]{1,0:T(8,128)(2,1)S(1)} %collective-permute-done.11.refs_1_, ...), custom_call_target="tpu_custom_call" | custom-call | tf_op jit(solution)/shard_map/pallas_call | solution.py:255
  76.9 1.5 %collective-permute-start.25 = (s16[528,128]{1,0:T(8,128)(2,1)S(1)}, s16[528,128]{1,0:T(8,128)(2,1)S(1)}, u32[]{:S(2)}, u32[]{:S(2)}) collective-permute-start(s16[528,128]{1,0:T(8,128)(2,1)S(1)} %get-tuple-element.38), channel_id=1, source_target_pairs={{0,2},{1,9},{2,4},{3,11},{4,6},{5,13},{6,0},{7,15},{8,10},{9,17},{... | collective-permute-start | bytes 405512 | tf_op jit(solution)/shard_map/ppermute | solution.py:29
  78.4 2.0 %collective-permute-start.26 = (s16[528,128]{1,0:T(8,128)(2,1)S(1)}, s16[528,128]{1,0:T(8,128)(2,1)S(1)}, u32[]{:S(2)}, u32[]{:S(2)}) collective-permute-start(s16[528,128]{1,0:T(8,128)(2,1)S(1)} %get-tuple-element.39), channel_id=1, source_target_pairs={{0,4},{1,17},{2,6},{3,19},{4,0},{5,21},{6,2},{7,23},{8,12},{9,25},... | collective-permute-start | bytes 405512 | tf_op jit(solution)/shard_map/ppermute | solution.py:29
  80.4 1.3 %collective-permute-start.27 = (s16[528,128]{1,0:T(8,128)(2,1)S(1)}, s16[528,128]{1,0:T(8,128)(2,1)S(1)}, u32[]{:S(2)}, u32[]{:S(2)}) collective-permute-start(s16[528,128]{1,0:T(8,128)(2,1)S(1)} %get-tuple-element.40), channel_id=1, source_target_pairs={{0,6},{1,25},{2,0},{3,27},{4,2},{5,29},{6,4},{7,31},{8,14},{9,1},{... | collective-permute-start | bytes 405512 | tf_op jit(solution)/shard_map/ppermute | solution.py:29
  81.7 1.5 %collective-permute-done.25.refs_0_ = s16[528,128]{1,0:T(8,128)(2,1)S(1)} collective-permute-done((s16[528,128]{1,0:T(8,128)(2,1)S(1)}, s16[528,128]{1,0:T(8,128)(2,1)S(1)}, u32[]{:S(2)}, u32[]{:S(2)}) %collective-permute-start.25) | collective-permute-done | bytes 135200 | tf_op jit(solution)/shard_map/ppermute | solution.py:29
  83.2 1.7 %collective-permute-done.26.refs_1_ = s16[528,128]{1,0:T(8,128)(2,1)S(1)} collective-permute-done((s16[528,128]{1,0:T(8,128)(2,1)S(1)}, s16[528,128]{1,0:T(8,128)(2,1)S(1)}, u32[]{:S(2)}, u32[]{:S(2)}) %collective-permute-start.26) | collective-permute-done | bytes 135200 | tf_op jit(solution)/shard_map/ppermute | solution.py:29
  86.1 11.5 %all_to_all.11.arrived_ref = bf16[8,64,128]{2,1,0:T(8,128)(2,1)S(1)} all-to-all(bf16[8,64,128]{2,1,0:T(8,128)(2,1)S(1)} %bitcast.17), channel_id=1, replica_groups=mesh['expert'=8,'tp_0'=4,'tp_1'=4,'tp_2'=2] {'expert'}, dimensions={0} | all-to-all | bytes 262144 | tf_op jit(solution)/shard_map/all_to_all | solution.py:295
  97.5 1.3 %shard_map.90 = bf16[128,128]{1,0:T(8,128)(2,1)} custom-call(s32[2,128]{1,0:T(2,128)S(1)} %bitcast.23, s32[1,128]{1,0:T(1,128)S(1)} %bitcast.25, f32[2,128]{1,0:T(2,128)S(1)} %bitcast.26, bf16[8,64,128]{2,1,0:T(8,128)(2,1)S(1)} %all_to_all.11.arrived_ref), custom_call_target="tpu_custom_call" | custom-call | tf_op jit(solution)/shard_map/pallas_call | solution.py:296
  (49 shorter events, 7.6 us)
Async XLA Ops:
  19.8 5.6 %collective-permute-start = (bf16[2,256,128]{2,1,0:T(8,128)(2,1)S(1)}, bf16[2,256,128]{2,1,0:T(8,128)(2,1)S(1)}, u32[]{:S(2)}, u32[]{:S(2)}) collective-permute-start(bf16[2,256,128]{2,1,0:T(8,128)(2,1)S(1)} %bitcast.18), channel_id=1, source_target_pairs={{0,8},{1,3},{2,10},{3,5},{4,12},{5,7},{6,14},{7,1},{8,16},{9,11},{... | collective-permute-start | bytes 393224 | tf_op jit(solution)/shard_map/ppermute | solution.py:29
  21.2 6.6 %collective-permute-start.1 = (bf16[2,256,128]{2,1,0:T(8,128)(2,1)S(1)}, bf16[2,256,128]{2,1,0:T(8,128)(2,1)S(1)}, u32[]{:S(2)}, u32[]{:S(2)}) collective-permute-start(bf16[2,256,128]{2,1,0:T(8,128)(2,1)S(1)} %bitcast.19), channel_id=1, source_target_pairs={{0,16},{1,5},{2,18},{3,7},{4,20},{5,1},{6,22},{7,3},{8,24},{9,13},... | collective-permute-start | bytes 393224 | tf_op jit(solution)/shard_map/ppermute | solution.py:29
  22.4 6.4 %collective-permute-start.2 = (bf16[2,256,128]{2,1,0:T(8,128)(2,1)S(1)}, bf16[2,256,128]{2,1,0:T(8,128)(2,1)S(1)}, u32[]{:S(2)}, u32[]{:S(2)}) collective-permute-start(bf16[2,256,128]{2,1,0:T(8,128)(2,1)S(1)} %bitcast.20), channel_id=1, source_target_pairs={{0,24},{1,7},{2,26},{3,1},{4,28},{5,3},{6,30},{7,5},{8,0},{9,15},{... | collective-permute-start | bytes 393224 | tf_op jit(solution)/shard_map/ppermute | solution.py:29
  25.3 22.4 %copy-start.2 = (bf16[1,448,4096]{2,1,0:T(8,128)(2,1)S(1)}, bf16[1,448,4096]{2,1,0:T(8,128)(2,1)}, u32[]{:S(2)}) copy-start(bf16[1,448,4096]{2,1,0:T(8,128)(2,1)} %param.15) | copy-start | bytes 11010052
  28.8 7.7 %collective-permute-start.14 = (bf16[4,256,128]{2,1,0:T(8,128)(2,1)S(1)}, bf16[4,256,128]{2,1,0:T(8,128)(2,1)S(1)}, u32[]{:S(2)}, u32[]{:S(2)}) collective-permute-start(bf16[4,256,128]{2,1,0:T(8,128)(2,1)S(1)} %get-tuple-element.30.refs_0_), channel_id=1, source_target_pairs={{0,2},{1,9},{2,4},{3,11},{4,6},{5,13},{6,0},{7,15},{8,10},{9,17},{... | collective-permute-start | bytes 786440 | tf_op jit(solution)/shard_map/ppermute | solution.py:29
  30.4 10.2 %collective-permute-start.15 = (bf16[4,256,128]{2,1,0:T(8,128)(2,1)S(1)}, bf16[4,256,128]{2,1,0:T(8,128)(2,1)S(1)}, u32[]{:S(2)}, u32[]{:S(2)}) collective-permute-start(bf16[4,256,128]{2,1,0:T(8,128)(2,1)S(1)} %get-tuple-element.30.refs_0_), channel_id=1, source_target_pairs={{0,4},{1,17},{2,6},{3,19},{4,0},{5,21},{6,2},{7,23},{8,12},{9,25},... | collective-permute-start | bytes 786440 | tf_op jit(solution)/shard_map/ppermute | solution.py:29
  33.3 7.3 %collective-permute-start.16 = (bf16[4,256,128]{2,1,0:T(8,128)(2,1)S(1)}, bf16[4,256,128]{2,1,0:T(8,128)(2,1)S(1)}, u32[]{:S(2)}, u32[]{:S(2)}) collective-permute-start(bf16[4,256,128]{2,1,0:T(8,128)(2,1)S(1)} %get-tuple-element.30.refs_0_), channel_id=1, source_target_pairs={{0,6},{1,25},{2,0},{3,27},{4,2},{5,29},{6,4},{7,31},{8,14},{9,1},{... | collective-permute-start | bytes 786440 | tf_op jit(solution)/shard_map/ppermute | solution.py:29
  34.7 5.9 %collective-permute-start.17 = (bf16[4,256,128]{2,1,0:T(8,128)(2,1)S(1)}, bf16[4,256,128]{2,1,0:T(8,128)(2,1)S(1)}, u32[]{:S(2)}, u32[]{:S(2)}) collective-permute-start(bf16[4,256,128]{2,1,0:T(8,128)(2,1)S(1)} %get-tuple-element.30.refs_0_), channel_id=1, source_target_pairs={{0,1},{1,0},{2,3},{3,2},{4,5},{5,4},{6,7},{7,6},{8,9},{9,8},{10,11... | collective-permute-start | bytes 786440 | tf_op jit(solution)/shard_map/ppermute | solution.py:29
  34.7 8.6 %collective-permute-start.3 = (bf16[4,256,128]{2,1,0:T(8,128)(2,1)S(1)}, bf16[4,256,128]{2,1,0:T(8,128)(2,1)S(1)}, u32[]{:S(2)}, u32[]{:S(2)}) collective-permute-start(bf16[4,256,128]{2,1,0:T(8,128)(2,1)S(1)} %get-tuple-element.23.refs_0_), channel_id=1, source_target_pairs={{0,2},{1,9},{2,4},{3,11},{4,6},{5,13},{6,0},{7,15},{8,10},{9,17},{... | collective-permute-start | bytes 786440 | tf_op jit(solution)/shard_map/ppermute | solution.py:29
  36.4 9.7 %collective-permute-start.4 = (bf16[4,256,128]{2,1,0:T(8,128)(2,1)S(1)}, bf16[4,256,128]{2,1,0:T(8,128)(2,1)S(1)}, u32[]{:S(2)}, u32[]{:S(2)}) collective-permute-start(bf16[4,256,128]{2,1,0:T(8,128)(2,1)S(1)} %get-tuple-element.23.refs_0_), channel_id=1, source_target_pairs={{0,4},{1,17},{2,6},{3,19},{4,0},{5,21},{6,2},{7,23},{8,12},{9,25},... | collective-permute-start | bytes 786440 | tf_op jit(solution)/shard_map/ppermute | solution.py:29
  40.6 6.4 %collective-permute-start.5 = (bf16[4,256,128]{2,1,0:T(8,128)(2,1)S(1)}, bf16[4,256,128]{2,1,0:T(8,128)(2,1)S(1)}, u32[]{:S(2)}, u32[]{:S(2)}) collective-permute-start(bf16[4,256,128]{2,1,0:T(8,128)(2,1)S(1)} %get-tuple-element.23.refs_0_), channel_id=1, source_target_pairs={{0,6},{1,25},{2,0},{3,27},{4,2},{5,29},{6,4},{7,31},{8,14},{9,1},{... | collective-permute-start | bytes 786440 | tf_op jit(solution)/shard_map/ppermute | solution.py:29
  40.6 6.4 %collective-permute-start.18 = (bf16[4,256,128]{2,1,0:T(8,128)(2,1)S(1)}, bf16[4,256,128]{2,1,0:T(8,128)(2,1)S(1)}, u32[]{:S(2)}, u32[]{:S(2)}) collective-permute-start(bf16[4,256,128]{2,1,0:T(8,128)(2,1)S(1)} %collective-permute-done.14.refs_1_), channel_id=1, source_target_pairs={{0,1},{1,0},{2,3},{3,2},{4,5},{5,4},{6,7},{7,6},{8,9},{9,8},{10,11... | collective-permute-start | bytes 786440 | tf_op jit(solution)/shard_map/ppermute | solution.py:29
  40.6 6.9 %collective-permute-start.19 = (bf16[4,256,128]{2,1,0:T(8,128)(2,1)S(1)}, bf16[4,256,128]{2,1,0:T(8,128)(2,1)S(1)}, u32[]{:S(2)}, u32[]{:S(2)}) collective-permute-start(bf16[4,256,128]{2,1,0:T(8,128)(2,1)S(1)} %collective-permute-done.15.refs_2_), channel_id=1, source_target_pairs={{0,1},{1,0},{2,3},{3,2},{4,5},{5,4},{6,7},{7,6},{8,9},{9,8},{10,11... | collective-permute-start | bytes 786440 | tf_op jit(solution)/shard_map/ppermute | solution.py:29
  43.3 4.5 %collective-permute-start.20 = (bf16[4,256,128]{2,1,0:T(8,128)(2,1)S(1)}, bf16[4,256,128]{2,1,0:T(8,128)(2,1)S(1)}, u32[]{:S(2)}, u32[]{:S(2)}) collective-permute-start(bf16[4,256,128]{2,1,0:T(8,128)(2,1)S(1)} %collective-permute-done.16.refs_3_), channel_id=1, source_target_pairs={{0,1},{1,0},{2,3},{3,2},{4,5},{5,4},{6,7},{7,6},{8,9},{9,8},{10,11... | collective-permute-start | bytes 786440 | tf_op jit(solution)/shard_map/ppermute | solution.py:29
  46.1 6.6 %collective-permute-start.6 = (bf16[4,256,128]{2,1,0:T(8,128)(2,1)S(1)}, bf16[4,256,128]{2,1,0:T(8,128)(2,1)S(1)}, u32[]{:S(2)}, u32[]{:S(2)}) collective-permute-start(bf16[4,256,128]{2,1,0:T(8,128)(2,1)S(1)} %get-tuple-element.23.refs_0_), channel_id=1, source_target_pairs={{0,1},{1,0},{2,3},{3,2},{4,5},{5,4},{6,7},{7,6},{8,9},{9,8},{10,11... | collective-permute-start | bytes 786440 | tf_op jit(solution)/shard_map/ppermute | solution.py:29
  46.9 5.8 %collective-permute-start.7 = (bf16[4,256,128]{2,1,0:T(8,128)(2,1)S(1)}, bf16[4,256,128]{2,1,0:T(8,128)(2,1)S(1)}, u32[]{:S(2)}, u32[]{:S(2)}) collective-permute-start(bf16[4,256,128]{2,1,0:T(8,128)(2,1)S(1)} %collective-permute-done.3.refs_1_), channel_id=1, source_target_pairs={{0,1},{1,0},{2,3},{3,2},{4,5},{5,4},{6,7},{7,6},{8,9},{9,8},{10,11... | collective-permute-start | bytes 786440 | tf_op jit(solution)/shard_map/ppermute | solution.py:29
  47.0 5.8 %collective-permute-start.8 = (bf16[4,256,128]{2,1,0:T(8,128)(2,1)S(1)}, bf16[4,256,128]{2,1,0:T(8,128)(2,1)S(1)}, u32[]{:S(2)}, u32[]{:S(2)}) collective-permute-start(bf16[4,256,128]{2,1,0:T(8,128)(2,1)S(1)} %collective-permute-done.4.refs_2_), channel_id=1, source_target_pairs={{0,1},{1,0},{2,3},{3,2},{4,5},{5,4},{6,7},{7,6},{8,9},{9,8},{10,11... | collective-permute-start | bytes 786440 | tf_op jit(solution)/shard_map/ppermute | solution.py:29
  47.5 5.3 %collective-permute-start.9 = (bf16[4,256,128]{2,1,0:T(8,128)(2,1)S(1)}, bf16[4,256,128]{2,1,0:T(8,128)(2,1)S(1)}, u32[]{:S(2)}, u32[]{:S(2)}) collective-permute-start(bf16[4,256,128]{2,1,0:T(8,128)(2,1)S(1)} %collective-permute-done.5.refs_3_), channel_id=1, source_target_pairs={{0,1},{1,0},{2,3},{3,2},{4,5},{5,4},{6,7},{7,6},{8,9},{9,8},{10,11... | collective-permute-start | bytes 786440 | tf_op jit(solution)/shard_map/ppermute | solution.py:29
  52.4 5.4 %collective-permute-start.21 = (f32[4,4,256,128]{3,2,1,0:T(8,128)S(1)}, f32[4,4,256,128]{3,2,1,0:T(8,128)S(1)}, u32[]{:S(2)}, u32[]{:S(2)}) collective-permute-start(f32[4,4,256,128]{3,2,1,0:T(8,128)S(1)} %get-tuple-element.32), channel_id=1, source_target_pairs={{0,1},{1,0},{2,3},{3,2},{4,5},{5,4},{6,7},{7,6},{8,9},{9,8},{10,11... | collective-permute-start | bytes 6291464 | tf_op jit(solution)/shard_map/ppermute | solution.py:29
  57.4 5.8 %collective-permute-start.10 = (f32[4,4,256,128]{3,2,1,0:T(8,128)S(1)}, f32[4,4,256,128]{3,2,1,0:T(8,128)S(1)}, u32[]{:S(2)}, u32[]{:S(2)}) collective-permute-start(f32[4,4,256,128]{3,2,1,0:T(8,128)S(1)} %get-tuple-element.25), channel_id=1, source_target_pairs={{0,1},{1,0},{2,3},{3,2},{4,5},{5,4},{6,7},{7,6},{8,9},{9,8},{10,11... | collective-permute-start | bytes 6291464 | tf_op jit(solution)/shard_map/ppermute | solution.py:29
  58.3 8.7 %collective-permute-start.22 = (s16[1040,128]{1,0:T(8,128)(2,1)S(1)}, s16[1040,128]{1,0:T(8,128)(2,1)S(1)}, u32[]{:S(2)}, u32[]{:S(2)}) collective-permute-start(s16[1040,128]{1,0:T(8,128)(2,1)S(1)} %get-tuple-element.34), channel_id=1, source_target_pairs={{0,8},{1,3},{2,10},{3,5},{4,12},{5,7},{6,14},{7,1},{8,16},{9,11},{... | collective-permute-start | bytes 798728 | tf_op jit(solution)/shard_map/ppermute | solution.py:29
  59.4 8.0 %collective-permute-start.23 = (s16[1040,128]{1,0:T(8,128)(2,1)S(1)}, s16[1040,128]{1,0:T(8,128)(2,1)S(1)}, u32[]{:S(2)}, u32[]{:S(2)}) collective-permute-start(s16[1040,128]{1,0:T(8,128)(2,1)S(1)} %get-tuple-element.35), channel_id=1, source_target_pairs={{0,16},{1,5},{2,18},{3,7},{4,20},{5,1},{6,22},{7,3},{8,24},{9,13},... | collective-permute-start | bytes 798728 | tf_op jit(solution)/shard_map/ppermute | solution.py:29
  61.2 9.0 %collective-permute-start.24 = (s16[1040,128]{1,0:T(8,128)(2,1)S(1)}, s16[1040,128]{1,0:T(8,128)(2,1)S(1)}, u32[]{:S(2)}, u32[]{:S(2)}) collective-permute-start(s16[1040,128]{1,0:T(8,128)(2,1)S(1)} %get-tuple-element.36), channel_id=1, source_target_pairs={{0,24},{1,7},{2,26},{3,1},{4,28},{5,3},{6,30},{7,5},{8,0},{9,15},{... | collective-permute-start | bytes 798728 | tf_op jit(solution)/shard_map/ppermute | solution.py:29
  63.8 33.7 %copy-start.3 = (s32[128,2]{0,1:T(2,128)S(1)}, s32[128,2]{0,1:T(2,128)}, u32[]{:S(2)}) copy-start(s32[128,2]{0,1:T(2,128)} %param.11) | copy-start | bytes 3076
  63.8 33.7 %copy-start.4 = (s32[128]{0:T(128)S(1)}, s32[128]{0:T(128)}, u32[]{:S(2)}) copy-start(s32[128]{0:T(128)} %param.12) | copy-start | bytes 1540
  63.8 33.7 %copy-start.5 = (f32[128,2]{0,1:T(2,128)S(1)}, f32[128,2]{0,1:T(2,128)}, u32[]{:S(2)}) copy-start(f32[128,2]{0,1:T(2,128)} %param.10) | copy-start | bytes 3076
  63.8 6.7 %collective-permute-start.11 = (s16[1040,128]{1,0:T(8,128)(2,1)S(1)}, s16[1040,128]{1,0:T(8,128)(2,1)S(1)}, u32[]{:S(2)}, u32[]{:S(2)}) collective-permute-start(s16[1040,128]{1,0:T(8,128)(2,1)S(1)} %get-tuple-element.27), channel_id=1, source_target_pairs={{0,8},{1,3},{2,10},{3,5},{4,12},{5,7},{6,14},{7,1},{8,16},{9,11},{... | collective-permute-start | bytes 798728 | tf_op jit(solution)/shard_map/ppermute | solution.py:29
  64.1 9.0 %collective-permute-start.12 = (s16[1040,128]{1,0:T(8,128)(2,1)S(1)}, s16[1040,128]{1,0:T(8,128)(2,1)S(1)}, u32[]{:S(2)}, u32[]{:S(2)}) collective-permute-start(s16[1040,128]{1,0:T(8,128)(2,1)S(1)} %get-tuple-element.28), channel_id=1, source_target_pairs={{0,16},{1,5},{2,18},{3,7},{4,20},{5,1},{6,22},{7,3},{8,24},{9,13},... | collective-permute-start | bytes 798728 | tf_op jit(solution)/shard_map/ppermute | solution.py:29
  67.0 8.9 %collective-permute-start.13 = (s16[1040,128]{1,0:T(8,128)(2,1)S(1)}, s16[1040,128]{1,0:T(8,128)(2,1)S(1)}, u32[]{:S(2)}, u32[]{:S(2)}) collective-permute-start(s16[1040,128]{1,0:T(8,128)(2,1)S(1)} %get-tuple-element.29), channel_id=1, source_target_pairs={{0,24},{1,7},{2,26},{3,1},{4,28},{5,3},{6,30},{7,5},{8,0},{9,15},{... | collective-permute-start | bytes 798728 | tf_op jit(solution)/shard_map/ppermute | solution.py:29
  76.9 6.3 %collective-permute-start.25 = (s16[528,128]{1,0:T(8,128)(2,1)S(1)}, s16[528,128]{1,0:T(8,128)(2,1)S(1)}, u32[]{:S(2)}, u32[]{:S(2)}) collective-permute-start(s16[528,128]{1,0:T(8,128)(2,1)S(1)} %get-tuple-element.38), channel_id=1, source_target_pairs={{0,2},{1,9},{2,4},{3,11},{4,6},{5,13},{6,0},{7,15},{8,10},{9,17},{... | collective-permute-start | bytes 405512 | tf_op jit(solution)/shard_map/ppermute | solution.py:29
  78.4 6.5 %collective-permute-start.26 = (s16[528,128]{1,0:T(8,128)(2,1)S(1)}, s16[528,128]{1,0:T(8,128)(2,1)S(1)}, u32[]{:S(2)}, u32[]{:S(2)}) collective-permute-start(s16[528,128]{1,0:T(8,128)(2,1)S(1)} %get-tuple-element.39), channel_id=1, source_target_pairs={{0,4},{1,17},{2,6},{3,19},{4,0},{5,21},{6,2},{7,23},{8,12},{9,25},... | collective-permute-start | bytes 405512 | tf_op jit(solution)/shard_map/ppermute | solution.py:29
  80.4 5.1 %collective-permute-start.27 = (s16[528,128]{1,0:T(8,128)(2,1)S(1)}, s16[528,128]{1,0:T(8,128)(2,1)S(1)}, u32[]{:S(2)}, u32[]{:S(2)}) collective-permute-start(s16[528,128]{1,0:T(8,128)(2,1)S(1)} %get-tuple-element.40), channel_id=1, source_target_pairs={{0,6},{1,25},{2,0},{3,27},{4,2},{5,29},{6,4},{7,31},{8,14},{9,1},{... | collective-permute-start | bytes 405512 | tf_op jit(solution)/shard_map/ppermute | solution.py:29
  (2 other events, 44.9 us)
